TPU v7x, 512 devices: a whole 4x8x8 slice. The times are simulated.
512 devices in a mesh: gx: 8 (over z), gy: 4 (over y_hi), gz: 16 (over y_lo, x, core).
Axes of the slice: x: 4, y: 8 (y_hi: 4, y_lo: 2; y = y_hi * 2 + y_lo), z: 8, core: 2. Of those that a mesh axis runs over, the one named last changes fastest.
Arguments:
- schur: bfloat16 [8, 4, 16, 1024, 1024], P('gx', 'gy', 'gz'), may hold values from -0.2 to 2.7
- block_map: int32 [8, 4, 16, 26], P('gx', 'gy', 'gz'), may hold values from 0 to 7
- vectors: bfloat16 [8, 4, 16, 1024, 512], P('gx', 'gy', 'gz'), may hold values from -3 to 3
Outputs:
- assembled: bfloat16 [8, 4, 16, 1024, 512], P('gx', 'gy', 'gz')
- update: bfloat16 [8, 4, 16, 1024, 512], P('gx', 'gy', 'gz')
All inputs are finite; a program needn't handle non-finite values.
Results may differ from a plain program's by a relative error of at most 0.0056.
Values may be sent and summed in bfloat16 or wider, within the bound.
No kernel may reach another device: no remote copies, remote signals or barrier semaphores. Data moves between devices by JAX's collectives and lax.ppermute only.
A program may use at most 64 MiB of HBM per device.

v0:
```python
import jax
import jax.numpy as jnp
from jax import lax
from jax.sharding import PartitionSpec as P

BLOCK = 128


def from_behind(value, axis, steps):
    count = lax.axis_size(axis)
    pairs = [(source, (source + steps) % count) for source in range(count)]
    return lax.ppermute(value, axis, pairs)


def directions():
    return [
        (a, b, c)
        for a in (-1, 0, 1)
        for b in (-1, 0, 1)
        for c in (-1, 0, 1)
        if (a, b, c) != (0, 0, 0)
    ]


def slot_number(along_x, along_y, along_z):
    return 9 * (along_x + 1) + 3 * (along_y + 1) + (along_z + 1)


def local(schur, block_map, vectors):
    offsets = directions()
    matrix = schur[0, 0, 0]
    right_side = vectors[0, 0, 0]
    block_links = block_map[0, 0, 0]
    order_size = matrix.shape[0]
    blocks = order_size // BLOCK
    product = jnp.dot(matrix, right_side, preferred_element_type=jnp.float32).astype(jnp.bfloat16)
    tile_grid = matrix.reshape(blocks, BLOCK, blocks, BLOCK)
    diagonal = jnp.stack([tile_grid[k, :, k, :] for k in range(blocks)])
    payload = jnp.concatenate([diagonal, product.reshape(blocks, BLOCK, -1)], axis=2)
    labels = jnp.arange(blocks, dtype=jnp.int32)
    centre = jnp.full((1,), -1, jnp.int32)
    links_grid = jnp.concatenate([block_links[:13], centre, block_links[13:]])
    send_chooser = (links_grid[:, None] == labels[None, :]).astype(jnp.bfloat16)
    outgoing = jnp.einsum(
        "sb,bij->sij", send_chooser, payload, preferred_element_type=jnp.float32
    ).astype(jnp.bfloat16)
    columns = lax.axis_size("gy")
    layers = lax.axis_size("gz")
    row_here = lax.axis_index("gy")
    layer_here = lax.axis_index("gz")
    plane_size = columns * layers
    received = jnp.zeros_like(outgoing)
    for along_x, along_y, along_z in offsets:
        target = slot_number(-along_x, -along_y, -along_z)
        stride = along_x * plane_size + along_y * layers + along_z
        moved = from_behind(outgoing[target], ("gx", "gy", "gz"), -stride)
        received = received.at[target].set(moved)
    alive_list = []
    for along_x in (-1, 0, 1):
        for along_y in (-1, 0, 1):
            for along_z in (-1, 0, 1):
                alive_list.append(
                    (row_here - along_y >= 0)
                    & (row_here - along_y < columns)
                    & (layer_here - along_z >= 0)
                    & (layer_here - along_z < layers)
                )
    alive = jnp.stack(alive_list).astype(jnp.bfloat16)
    receive_links = links_grid[::-1]
    weights = (receive_links[:, None] == labels[None, :]).astype(jnp.bfloat16) * alive[:, None]
    totals = payload.astype(jnp.float32) + jnp.einsum(
        "sb,sij->bij", weights, received, preferred_element_type=jnp.float32
    )
    counts = 1.0 + jnp.sum(weights.astype(jnp.float32), axis=0)
    coupling = totals[:, :, :BLOCK]
    summed = totals[:, :, BLOCK:]
    scaled = (
        jnp.einsum("bij,bjk->bik", coupling, summed, precision=lax.Precision.HIGHEST)
        / counts[:, None, None]
    ).astype(jnp.bfloat16)
    update = jnp.dot(
        matrix, scaled.reshape(order_size, -1), preferred_element_type=jnp.float32
    ).astype(jnp.bfloat16)
    assembled = summed.reshape(order_size, -1).astype(jnp.bfloat16)
    return (assembled[None, None, None], update[None, None, None])


def solution(mesh):
    placed = (
        P("gx", "gy", "gz", None, None),
        P("gx", "gy", "gz", None),
        P("gx", "gy", "gz", None, None),
    )
    return jax.shard_map(
        local,
        mesh=mesh,
        in_specs=placed,
        out_specs=(P("gx", "gy", "gz", None, None), P("gx", "gy", "gz", None, None)),
        check_vma=False,
    )
```

profile of v0, /device:TPU:47, one launch (start us, length us, event | category | flops | bytes accessed | tf_op | source)
XLA Modules:
  0.0 195.9 jit_solution(15784522462275635630)
XLA Ops:
  1.9 3.0 %fusion.12 = bf16[1024,512]{1,0:T(8,128)(2,1)S(1)} fusion(bf16[1,1,1,1024,1024]{4,3,2,1,0:T(8,128)(2,1)} %param.55, bf16[1,1,1,1024,512]{4,3,2,1,0:T(8,128)(2,1)S(1)} %copy-done), kind=kOutput, calls=%fused_computation.11 | convolution fusion | flops 1074266112 | bytes 4194304 | tf_op jit(solution)/shard_map/dot_general | solution.py:36
  7.6 1.8 convolution_convert_fusion
  9.4 2.3 %copy-done.1 = bf16[27,128,640]{2,0,1:T(8,128)(2,1)} copy-done((bf16[27,128,640]{2,0,1:T(8,128)(2,1)}, bf16[27,128,640]{2,0,1:T(8,128)(2,1)S(1)}, u32[]{:S(2)}) %copy-start.1) | copy-done | bytes 4423704
  11.7 1.8 fusion.35
  14.2 5.7 %collective-permute-start = (bf16[128,640]{1,0:T(8,128)(2,1)}, bf16[128,640]{1,0:T(8,128)(2,1)S(1)}, u32[]{:S(2)}, u32[]{:S(2)}) collective-permute-start(bf16[128,640]{1,0:T(8,128)(2,1)} %bitcast.190), channel_id=1, source_target_pairs={{0,81},{1,82},{2,83},{3,84},{4,85},{5,86},{6,87},{7,88},{8,89},{9,... | collective-permute-start | bytes 491528 | tf_op jit(solution)/shard_map/ppermute | solution.py:12
  20.6 6.0 %collective-permute-start.1 = (bf16[128,640]{1,0:T(8,128)(2,1)}, bf16[128,640]{1,0:T(8,128)(2,1)}, u32[]{:S(2)}, u32[]{:S(2)}) collective-permute-start(bf16[128,640]{1,0:T(8,128)(2,1)} %bitcast.189), channel_id=1, source_target_pairs={{0,80},{1,81},{2,82},{3,83},{4,84},{5,85},{6,86},{7,87},{8,88},{9,... | collective-permute-start | bytes 491528 | tf_op jit(solution)/shard_map/ppermute | solution.py:12
  27.3 6.3 %collective-permute-start.2 = (bf16[128,640]{1,0:T(8,128)(2,1)}, bf16[128,640]{1,0:T(8,128)(2,1)}, u32[]{:S(2)}, u32[]{:S(2)}) collective-permute-start(bf16[128,640]{1,0:T(8,128)(2,1)} %bitcast.188), channel_id=1, source_target_pairs={{0,79},{1,80},{2,81},{3,82},{4,83},{5,84},{6,85},{7,86},{8,87},{9,... | collective-permute-start | bytes 491528 | tf_op jit(solution)/shard_map/ppermute | solution.py:12
  34.3 7.6 %collective-permute-start.3 = (bf16[128,640]{1,0:T(8,128)(2,1)}, bf16[128,640]{1,0:T(8,128)(2,1)}, u32[]{:S(2)}, u32[]{:S(2)}) collective-permute-start(bf16[128,640]{1,0:T(8,128)(2,1)} %bitcast.187), channel_id=1, source_target_pairs={{0,65},{1,66},{2,67},{3,68},{4,69},{5,70},{6,71},{7,72},{8,73},{9,... | collective-permute-start | bytes 491528 | tf_op jit(solution)/shard_map/ppermute | solution.py:12
  42.6 3.1 %collective-permute-start.4 = (bf16[128,640]{1,0:T(8,128)(2,1)}, bf16[128,640]{1,0:T(8,128)(2,1)}, u32[]{:S(2)}, u32[]{:S(2)}) collective-permute-start(bf16[128,640]{1,0:T(8,128)(2,1)} %bitcast.186), channel_id=1, source_target_pairs={{0,64},{1,65},{2,66},{3,67},{4,68},{5,69},{6,70},{7,71},{8,72},{9,... | collective-permute-start | bytes 491528 | tf_op jit(solution)/shard_map/ppermute | solution.py:12
  45.9 14.4 %fusion.34 = (bf16[1,128,640]{2,0,1:T(2,128)(2,1)}, bf16[1,128,640]{2,0,1:T(2,128)(2,1)}, bf16[1,128,640]{2,0,1:T(2,128)(2,1)}, bf16[1,128,640]{2,0,1:T(2,128)(2...) fusion(bf16[27,128,640]{2,0,1:T(8,128)(2,1)} %copy-done.1), kind=kLoop, calls=%fused_computation.93 | loop fusion | bytes 6225920 | tf_op jit(solution)/shard_map/slice | solution.py:56
  60.6 1.1 copy.108
  61.8 1.0 copy.109
  62.8 1.0 copy.110
  63.8 1.0 copy.111
  64.8 1.0 copy.112
  65.8 1.0 copy.113
  66.8 1.0 copy.114
  68.4 1.9 collective-permute-start.5
  70.9 5.3 %collective-permute-start.6 = (bf16[128,640]{1,0:T(8,128)(2,1)S(1)}, bf16[128,640]{1,0:T(8,128)(2,1)S(1)}, u32[]{:S(2)}, u32[]{:S(2)}) collective-permute-start(bf16[128,640]{1,0:T(8,128)(2,1)S(1)} %bitcast.212), channel_id=1, source_target_pairs={{0,49},{1,50},{2,51},{3,52},{4,53},{5,54},{6,55},{7,56},{8,57},{9,... | collective-permute-start | bytes 491528 | tf_op jit(solution)/shard_map/ppermute | solution.py:12
  76.2 0.9 bitcast_dynamic-update-slice_fusion.24
  77.1 2.6 %collective-permute-start.7 = (bf16[128,640]{1,0:T(8,128)(2,1)S(1)}, bf16[128,640]{1,0:T(8,128)(2,1)S(1)}, u32[]{:S(2)}, u32[]{:S(2)}) collective-permute-start(bf16[128,640]{1,0:T(8,128)(2,1)S(1)} %bitcast.216), channel_id=1, source_target_pairs={{0,48},{1,49},{2,50},{3,51},{4,52},{5,53},{6,54},{7,55},{8,56},{9,... | collective-permute-start | bytes 491528 | tf_op jit(solution)/shard_map/ppermute | solution.py:12
  80.7 3.1 %collective-permute-start.8 = (bf16[128,640]{1,0:T(8,128)(2,1)S(1)}, bf16[128,640]{1,0:T(8,128)(2,1)S(1)}, u32[]{:S(2)}, u32[]{:S(2)}) collective-permute-start(bf16[128,640]{1,0:T(8,128)(2,1)S(1)} %bitcast.215), channel_id=1, source_target_pairs={{0,47},{1,48},{2,49},{3,50},{4,51},{5,52},{6,53},{7,54},{8,55},{9,... | collective-permute-start | bytes 491528 | tf_op jit(solution)/shard_map/ppermute | solution.py:12
  84.8 7.3 %collective-permute-start.9 = (bf16[128,640]{1,0:T(8,128)(2,1)S(1)}, bf16[128,640]{1,0:T(8,128)(2,1)S(1)}, u32[]{:S(2)}, u32[]{:S(2)}) collective-permute-start(bf16[128,640]{1,0:T(8,128)(2,1)S(1)} %bitcast.213), channel_id=1, source_target_pairs={{0,17},{1,18},{2,19},{3,20},{4,21},{5,22},{6,23},{7,24},{8,25},{9,... | collective-permute-start | bytes 491528 | tf_op jit(solution)/shard_map/ppermute | solution.py:12
  93.0 1.9 collective-permute-start.10
  95.0 1.9 collective-permute-start.11
  97.0 7.6 %collective-permute-start.12 = (bf16[128,640]{1,0:T(8,128)(2,1)S(1)}, bf16[128,640]{1,0:T(8,128)(2,1)S(1)}, u32[]{:S(2)}, u32[]{:S(2)}) collective-permute-start(bf16[128,640]{1,0:T(8,128)(2,1)S(1)} %bitcast.209), channel_id=1, source_target_pairs={{0,1},{1,2},{2,3},{3,4},{4,5},{5,6},{6,7},{7,8},{8,9},{9,10},{10,1... | collective-permute-start | bytes 491528 | tf_op jit(solution)/shard_map/ppermute | solution.py:12
  104.7 1.9 collective-permute-start.13
  106.6 5.1 %collective-permute-start.14 = (bf16[128,640]{1,0:T(8,128)(2,1)S(1)}, bf16[128,640]{1,0:T(8,128)(2,1)S(1)}, u32[]{:S(2)}, u32[]{:S(2)}) collective-permute-start(bf16[128,640]{1,0:T(8,128)(2,1)S(1)} %bitcast.207), channel_id=1, source_target_pairs={{0,497},{1,498},{2,499},{3,500},{4,501},{5,502},{6,503},{7,504},{8... | collective-permute-start | bytes 491528 | tf_op jit(solution)/shard_map/ppermute | solution.py:12
  111.7 1.7 collective-permute-done.10
  113.4 3.4 %collective-permute-start.15 = (bf16[128,640]{1,0:T(8,128)(2,1)S(1)}, bf16[128,640]{1,0:T(8,128)(2,1)S(1)}, u32[]{:S(2)}, u32[]{:S(2)}) collective-permute-start(bf16[128,640]{1,0:T(8,128)(2,1)S(1)} %bitcast.206), channel_id=1, source_target_pairs={{0,496},{1,497},{2,498},{3,499},{4,500},{5,501},{6,502},{7,503},{8... | collective-permute-start | bytes 491528 | tf_op jit(solution)/shard_map/ppermute | solution.py:12
  116.9 4.1 %collective-permute-start.16 = (bf16[128,640]{1,0:T(8,128)(2,1)S(1)}, bf16[128,640]{1,0:T(8,128)(2,1)S(1)}, u32[]{:S(2)}, u32[]{:S(2)}) collective-permute-start(bf16[128,640]{1,0:T(8,128)(2,1)S(1)} %bitcast.205), channel_id=1, source_target_pairs={{0,495},{1,496},{2,497},{3,498},{4,499},{5,500},{6,501},{7,502},{8... | collective-permute-start | bytes 491528 | tf_op jit(solution)/shard_map/ppermute | solution.py:12
  121.1 8.6 %collective-permute-start.17 = (bf16[128,640]{1,0:T(8,128)(2,1)S(1)}, bf16[128,640]{1,0:T(8,128)(2,1)S(1)}, u32[]{:S(2)}, u32[]{:S(2)}) collective-permute-start(bf16[128,640]{1,0:T(8,128)(2,1)S(1)} %bitcast.204), channel_id=1, source_target_pairs={{0,465},{1,466},{2,467},{3,468},{4,469},{5,470},{6,471},{7,472},{8... | collective-permute-start | bytes 491528 | tf_op jit(solution)/shard_map/ppermute | solution.py:12
  129.7 4.1 %collective-permute-start.18 = (bf16[128,640]{1,0:T(8,128)(2,1)S(1)}, bf16[128,640]{1,0:T(8,128)(2,1)S(1)}, u32[]{:S(2)}, u32[]{:S(2)}) collective-permute-start(bf16[128,640]{1,0:T(8,128)(2,1)S(1)} %bitcast.203), channel_id=1, source_target_pairs={{0,464},{1,465},{2,466},{3,467},{4,468},{5,469},{6,470},{7,471},{8... | collective-permute-start | bytes 491528 | tf_op jit(solution)/shard_map/ppermute | solution.py:12
  133.9 1.9 collective-permute-start.19
  135.9 9.0 %collective-permute-start.20 = (bf16[128,640]{1,0:T(8,128)(2,1)S(1)}, bf16[128,640]{1,0:T(8,128)(2,1)S(1)}, u32[]{:S(2)}, u32[]{:S(2)}) collective-permute-start(bf16[128,640]{1,0:T(8,128)(2,1)S(1)} %bitcast.201), channel_id=1, source_target_pairs={{0,449},{1,450},{2,451},{3,452},{4,453},{5,454},{6,455},{7,456},{8... | collective-permute-start | bytes 491528 | tf_op jit(solution)/shard_map/ppermute | solution.py:12
  145.0 3.4 %collective-permute-start.21 = (bf16[128,640]{1,0:T(8,128)(2,1)S(1)}, bf16[128,640]{1,0:T(8,128)(2,1)S(1)}, u32[]{:S(2)}, u32[]{:S(2)}) collective-permute-start(bf16[128,640]{1,0:T(8,128)(2,1)S(1)} %bitcast.200), channel_id=1, source_target_pairs={{0,448},{1,449},{2,450},{3,451},{4,452},{5,453},{6,454},{7,455},{8... | collective-permute-start | bytes 491528 | tf_op jit(solution)/shard_map/ppermute | solution.py:12
  148.4 1.9 collective-permute-start.22
  150.4 8.2 %collective-permute-start.23 = (bf16[128,640]{1,0:T(8,128)(2,1)S(1)}, bf16[128,640]{1,0:T(8,128)(2,1)S(1)}, u32[]{:S(2)}, u32[]{:S(2)}) collective-permute-start(bf16[128,640]{1,0:T(8,128)(2,1)S(1)} %bitcast.198), channel_id=1, source_target_pairs={{0,433},{1,434},{2,435},{3,436},{4,437},{5,438},{6,439},{7,440},{8... | collective-permute-start | bytes 491528 | tf_op jit(solution)/shard_map/ppermute | solution.py:12
  158.6 1.9 collective-permute-start.24
  160.6 2.1 %collective-permute-start.25 = (bf16[128,640]{1,0:T(8,128)(2,1)S(1)}, bf16[128,640]{1,0:T(8,128)(2,1)S(1)}, u32[]{:S(2)}, u32[]{:S(2)}) collective-permute-start(bf16[128,640]{1,0:T(8,128)(2,1)S(1)} %bitcast.196), channel_id=1, source_target_pairs={{0,431},{1,432},{2,433},{3,434},{4,435},{5,436},{6,437},{7,438},{8... | collective-permute-start | bytes 491528 | tf_op jit(solution)/shard_map/ppermute | solution.py:12
  162.8 5.6 %collective-permute-done.23 = bf16[128,640]{1,0:T(8,128)(2,1)S(1)} collective-permute-done((bf16[128,640]{1,0:T(8,128)(2,1)S(1)}, bf16[128,640]{1,0:T(8,128)(2,1)S(1)}, u32[]{:S(2)}, u32[]{:S(2)}) %collective-permute-start.23) | collective-permute-done | bytes 163872 | tf_op jit(solution)/shard_map/ppermute | solution.py:12
  168.5 4.4 %collective-permute-done.24 = bf16[128,640]{1,0:T(8,128)(2,1)S(1)} collective-permute-done((bf16[128,640]{1,0:T(8,128)(2,1)S(1)}, bf16[128,640]{1,0:T(8,128)(2,1)S(1)}, u32[]{:S(2)}, u32[]{:S(2)}) %collective-permute-start.24) | collective-permute-done | bytes 163872 | tf_op jit(solution)/shard_map/ppermute | solution.py:12
  172.8 12.7 %collective-permute-done.25 = bf16[128,640]{1,0:T(8,128)(2,1)S(1)} collective-permute-done((bf16[128,640]{1,0:T(8,128)(2,1)S(1)}, bf16[128,640]{1,0:T(8,128)(2,1)S(1)}, u32[]{:S(2)}, u32[]{:S(2)}) %collective-permute-start.25) | collective-permute-done | bytes 163872 | tf_op jit(solution)/shard_map/ppermute | solution.py:12
  185.5 3.0 %convert_add_fusion = f32[8,128,640]{2,0,1:T(8,128)S(1)} fusion(bf16[27,128,640]{2,1,0:T(8,128)(2,1)S(1)} %bitcast_dynamic-update-slice_fusion, bf16[8,128,512]{2,0,1:T(8,128)(2,1)S(1)} %copy.39, bf16[8,128,128]{2,0,1:T(8,128)(2,1)S(1)} %stack.22, s32[27]{0:T(128)S(1)} %rev.3, bf16[27]{0:T(256)(128)(2,1)S(1)} %convert_element_type.45), kind=kOutput, calls=%fused_computation.3 | convolution fusion | flops 38666672 | bytes 8356002 | tf_op jit(solution)/shard_map/sb,sij->bij/dot_general | solution.py:71
  189.0 3.0 %divide_convert_fusion = bf16[8,128,512]{2,1,0:T(8,128)(2,1)S(1)} fusion(f32[8,128,512]{2,0,1:T(8,128)S(1)} %slice.713, f32[8]{0:T(128)S(1)} %broadcast_add_fusion, f32[8,128,128]{2,0,1:T(8,128)S(1)} %slice.714), kind=kOutput, calls=%fused_computation.10 | convolution fusion | flops 806354944 | bytes 3670048 | tf_op jit(solution)/shard_map/bij,bjk->bik/dot_general | solution.py:78
  192.0 1.3 fusion.18
  193.3 1.3 copy.44
  194.7 1.3 copy.41
  (109 shorter events, 12.4 us)
Async XLA Ops:
  0.6 1.3 copy-start
  1.9 3.6 %copy-start.2 = (bf16[1,1,1,1024,1024]{4,3,2,1,0:T(8,128)(2,1)S(1)}, bf16[1,1,1,1024,1024]{4,3,2,1,0:T(8,128)(2,1)}, u32[]{:S(2)}) copy-start(bf16[1,1,1,1024,1024]{4,3,2,1,0:T(8,128)(2,1)} %param.55) | copy-start | bytes 6291460
  9.4 2.3 %copy-start.1 = (bf16[27,128,640]{2,0,1:T(8,128)(2,1)}, bf16[27,128,640]{2,0,1:T(8,128)(2,1)S(1)}, u32[]{:S(2)}) copy-start(bf16[27,128,640]{2,0,1:T(8,128)(2,1)S(1)} %convolution_convert_fusion) | copy-start | bytes 13271044
  14.2 54.2 %collective-permute-start = (bf16[128,640]{1,0:T(8,128)(2,1)}, bf16[128,640]{1,0:T(8,128)(2,1)S(1)}, u32[]{:S(2)}, u32[]{:S(2)}) collective-permute-start(bf16[128,640]{1,0:T(8,128)(2,1)} %bitcast.190), channel_id=1, source_target_pairs={{0,81},{1,82},{2,83},{3,84},{4,85},{5,86},{6,87},{7,88},{8,89},{9,... | collective-permute-start | bytes 491528 | tf_op jit(solution)/shard_map/ppermute | solution.py:12
  20.6 50.3 %collective-permute-start.1 = (bf16[128,640]{1,0:T(8,128)(2,1)}, bf16[128,640]{1,0:T(8,128)(2,1)}, u32[]{:S(2)}, u32[]{:S(2)}) collective-permute-start(bf16[128,640]{1,0:T(8,128)(2,1)} %bitcast.189), channel_id=1, source_target_pairs={{0,80},{1,81},{2,82},{3,83},{4,84},{5,85},{6,86},{7,87},{8,88},{9,... | collective-permute-start | bytes 491528 | tf_op jit(solution)/shard_map/ppermute | solution.py:12
  27.3 49.8 %collective-permute-start.2 = (bf16[128,640]{1,0:T(8,128)(2,1)}, bf16[128,640]{1,0:T(8,128)(2,1)}, u32[]{:S(2)}, u32[]{:S(2)}) collective-permute-start(bf16[128,640]{1,0:T(8,128)(2,1)} %bitcast.188), channel_id=1, source_target_pairs={{0,79},{1,80},{2,81},{3,82},{4,83},{5,84},{6,85},{7,86},{8,87},{9,... | collective-permute-start | bytes 491528 | tf_op jit(solution)/shard_map/ppermute | solution.py:12
  34.3 46.4 %collective-permute-start.3 = (bf16[128,640]{1,0:T(8,128)(2,1)}, bf16[128,640]{1,0:T(8,128)(2,1)}, u32[]{:S(2)}, u32[]{:S(2)}) collective-permute-start(bf16[128,640]{1,0:T(8,128)(2,1)} %bitcast.187), channel_id=1, source_target_pairs={{0,65},{1,66},{2,67},{3,68},{4,69},{5,70},{6,71},{7,72},{8,73},{9,... | collective-permute-start | bytes 491528 | tf_op jit(solution)/shard_map/ppermute | solution.py:12
  42.6 42.1 %collective-permute-start.4 = (bf16[128,640]{1,0:T(8,128)(2,1)}, bf16[128,640]{1,0:T(8,128)(2,1)}, u32[]{:S(2)}, u32[]{:S(2)}) collective-permute-start(bf16[128,640]{1,0:T(8,128)(2,1)} %bitcast.186), channel_id=1, source_target_pairs={{0,64},{1,65},{2,66},{3,67},{4,68},{5,69},{6,70},{7,71},{8,72},{9,... | collective-permute-start | bytes 491528 | tf_op jit(solution)/shard_map/ppermute | solution.py:12
  60.4 7.3 %copy-start.14 = (bf16[1,128,640]{2,0,1:T(2,128)(2,1)S(1)}, bf16[1,128,640]{2,0,1:T(2,128)(2,1)}, u32[]{:S(2)}) copy-start(bf16[1,128,640]{2,0,1:T(2,128)(2,1)} %get-tuple-element.327) | copy-start | bytes 491524
  60.4 7.4 %copy-start.13 = (bf16[1,128,640]{2,0,1:T(2,128)(2,1)S(1)}, bf16[1,128,640]{2,0,1:T(2,128)(2,1)}, u32[]{:S(2)}) copy-start(bf16[1,128,640]{2,0,1:T(2,128)(2,1)} %get-tuple-element.328) | copy-start | bytes 491524
  60.4 7.4 %copy-start.12 = (bf16[1,128,640]{2,0,1:T(2,128)(2,1)S(1)}, bf16[1,128,640]{2,0,1:T(2,128)(2,1)}, u32[]{:S(2)}) copy-start(bf16[1,128,640]{2,0,1:T(2,128)(2,1)} %get-tuple-element.329) | copy-start | bytes 491524
  60.5 7.4 %copy-start.11 = (bf16[1,128,640]{2,0,1:T(2,128)(2,1)S(1)}, bf16[1,128,640]{2,0,1:T(2,128)(2,1)}, u32[]{:S(2)}) copy-start(bf16[1,128,640]{2,0,1:T(2,128)(2,1)} %get-tuple-element.330) | copy-start | bytes 491524
  60.5 7.5 %copy-start.10 = (bf16[1,128,640]{2,0,1:T(2,128)(2,1)S(1)}, bf16[1,128,640]{2,0,1:T(2,128)(2,1)}, u32[]{:S(2)}) copy-start(bf16[1,128,640]{2,0,1:T(2,128)(2,1)} %get-tuple-element.331) | copy-start | bytes 491524
  60.5 7.5 %copy-start.9 = (bf16[1,128,640]{2,0,1:T(2,128)(2,1)S(1)}, bf16[1,128,640]{2,0,1:T(2,128)(2,1)}, u32[]{:S(2)}) copy-start(bf16[1,128,640]{2,0,1:T(2,128)(2,1)} %get-tuple-element.332) | copy-start | bytes 491524
  60.5 7.5 %copy-start.8 = (bf16[1,128,640]{2,0,1:T(2,128)(2,1)S(1)}, bf16[1,128,640]{2,0,1:T(2,128)(2,1)}, u32[]{:S(2)}) copy-start(bf16[1,128,640]{2,0,1:T(2,128)(2,1)} %get-tuple-element.333) | copy-start | bytes 491524
  60.5 7.6 %copy-start.7 = (bf16[1,128,640]{2,0,1:T(2,128)(2,1)S(1)}, bf16[1,128,640]{2,0,1:T(2,128)(2,1)}, u32[]{:S(2)}) copy-start(bf16[1,128,640]{2,0,1:T(2,128)(2,1)} %get-tuple-element.334) | copy-start | bytes 491524
  60.5 7.6 %copy-start.6 = (bf16[1,128,640]{2,0,1:T(2,128)(2,1)S(1)}, bf16[1,128,640]{2,0,1:T(2,128)(2,1)}, u32[]{:S(2)}) copy-start(bf16[1,128,640]{2,0,1:T(2,128)(2,1)} %get-tuple-element.335) | copy-start | bytes 491524
  60.5 7.6 %copy-start.5 = (bf16[1,128,640]{2,0,1:T(2,128)(2,1)S(1)}, bf16[1,128,640]{2,0,1:T(2,128)(2,1)}, u32[]{:S(2)}) copy-start(bf16[1,128,640]{2,0,1:T(2,128)(2,1)} %get-tuple-element.336) | copy-start | bytes 491524
  60.6 7.6 %copy-start.4 = (bf16[1,128,640]{2,0,1:T(2,128)(2,1)S(1)}, bf16[1,128,640]{2,0,1:T(2,128)(2,1)}, u32[]{:S(2)}) copy-start(bf16[1,128,640]{2,0,1:T(2,128)(2,1)} %get-tuple-element.337) | copy-start | bytes 491524
  68.4 24.7 %collective-permute-start.5 = (bf16[128,640]{1,0:T(8,128)(2,1)S(1)}, bf16[128,640]{1,0:T(8,128)(2,1)S(1)}, u32[]{:S(2)}, u32[]{:S(2)}) collective-permute-start(bf16[128,640]{1,0:T(8,128)(2,1)S(1)} %bitcast.214), channel_id=1, source_target_pairs={{0,63},{1,64},{2,65},{3,66},{4,67},{5,68},{6,69},{7,70},{8,71},{9,... | collective-permute-start | bytes 491528 | tf_op jit(solution)/shard_map/ppermute | solution.py:12
  70.9 24.1 %collective-permute-start.6 = (bf16[128,640]{1,0:T(8,128)(2,1)S(1)}, bf16[128,640]{1,0:T(8,128)(2,1)S(1)}, u32[]{:S(2)}, u32[]{:S(2)}) collective-permute-start(bf16[128,640]{1,0:T(8,128)(2,1)S(1)} %bitcast.212), channel_id=1, source_target_pairs={{0,49},{1,50},{2,51},{3,52},{4,53},{5,54},{6,55},{7,56},{8,57},{9,... | collective-permute-start | bytes 491528 | tf_op jit(solution)/shard_map/ppermute | solution.py:12
  77.1 19.8 %collective-permute-start.7 = (bf16[128,640]{1,0:T(8,128)(2,1)S(1)}, bf16[128,640]{1,0:T(8,128)(2,1)S(1)}, u32[]{:S(2)}, u32[]{:S(2)}) collective-permute-start(bf16[128,640]{1,0:T(8,128)(2,1)S(1)} %bitcast.216), channel_id=1, source_target_pairs={{0,48},{1,49},{2,50},{3,51},{4,52},{5,53},{6,54},{7,55},{8,56},{9,... | collective-permute-start | bytes 491528 | tf_op jit(solution)/shard_map/ppermute | solution.py:12
  80.7 23.9 %collective-permute-start.8 = (bf16[128,640]{1,0:T(8,128)(2,1)S(1)}, bf16[128,640]{1,0:T(8,128)(2,1)S(1)}, u32[]{:S(2)}, u32[]{:S(2)}) collective-permute-start(bf16[128,640]{1,0:T(8,128)(2,1)S(1)} %bitcast.215), channel_id=1, source_target_pairs={{0,47},{1,48},{2,49},{3,50},{4,51},{5,52},{6,53},{7,54},{8,55},{9,... | collective-permute-start | bytes 491528 | tf_op jit(solution)/shard_map/ppermute | solution.py:12
  84.8 21.8 %collective-permute-start.9 = (bf16[128,640]{1,0:T(8,128)(2,1)S(1)}, bf16[128,640]{1,0:T(8,128)(2,1)S(1)}, u32[]{:S(2)}, u32[]{:S(2)}) collective-permute-start(bf16[128,640]{1,0:T(8,128)(2,1)S(1)} %bitcast.213), channel_id=1, source_target_pairs={{0,17},{1,18},{2,19},{3,20},{4,21},{5,22},{6,23},{7,24},{8,25},{9,... | collective-permute-start | bytes 491528 | tf_op jit(solution)/shard_map/ppermute | solution.py:12
  93.0 20.4 %collective-permute-start.10 = (bf16[128,640]{1,0:T(8,128)(2,1)S(1)}, bf16[128,640]{1,0:T(8,128)(2,1)S(1)}, u32[]{:S(2)}, u32[]{:S(2)}) collective-permute-start(bf16[128,640]{1,0:T(8,128)(2,1)S(1)} %bitcast.211), channel_id=1, source_target_pairs={{0,16},{1,17},{2,18},{3,19},{4,20},{5,21},{6,22},{7,23},{8,24},{9,... | collective-permute-start | bytes 491528 | tf_op jit(solution)/shard_map/ppermute | solution.py:12
  95.0 21.9 %collective-permute-start.11 = (bf16[128,640]{1,0:T(8,128)(2,1)S(1)}, bf16[128,640]{1,0:T(8,128)(2,1)S(1)}, u32[]{:S(2)}, u32[]{:S(2)}) collective-permute-start(bf16[128,640]{1,0:T(8,128)(2,1)S(1)} %bitcast.210), channel_id=1, source_target_pairs={{0,15},{1,16},{2,17},{3,18},{4,19},{5,20},{6,21},{7,22},{8,23},{9,... | collective-permute-start | bytes 491528 | tf_op jit(solution)/shard_map/ppermute | solution.py:12
  97.0 24.1 %collective-permute-start.12 = (bf16[128,640]{1,0:T(8,128)(2,1)S(1)}, bf16[128,640]{1,0:T(8,128)(2,1)S(1)}, u32[]{:S(2)}, u32[]{:S(2)}) collective-permute-start(bf16[128,640]{1,0:T(8,128)(2,1)S(1)} %bitcast.209), channel_id=1, source_target_pairs={{0,1},{1,2},{2,3},{3,4},{4,5},{5,6},{6,7},{7,8},{8,9},{9,10},{10,1... | collective-permute-start | bytes 491528 | tf_op jit(solution)/shard_map/ppermute | solution.py:12
  104.7 25.1 %collective-permute-start.13 = (bf16[128,640]{1,0:T(8,128)(2,1)S(1)}, bf16[128,640]{1,0:T(8,128)(2,1)S(1)}, u32[]{:S(2)}, u32[]{:S(2)}) collective-permute-start(bf16[128,640]{1,0:T(8,128)(2,1)S(1)} %bitcast.208), channel_id=1, source_target_pairs={{0,511},{1,0},{2,1},{3,2},{4,3},{5,4},{6,5},{7,6},{8,7},{9,8},{10,... | collective-permute-start | bytes 491528 | tf_op jit(solution)/shard_map/ppermute | solution.py:12
  106.6 27.3 %collective-permute-start.14 = (bf16[128,640]{1,0:T(8,128)(2,1)S(1)}, bf16[128,640]{1,0:T(8,128)(2,1)S(1)}, u32[]{:S(2)}, u32[]{:S(2)}) collective-permute-start(bf16[128,640]{1,0:T(8,128)(2,1)S(1)} %bitcast.207), channel_id=1, source_target_pairs={{0,497},{1,498},{2,499},{3,500},{4,501},{5,502},{6,503},{7,504},{8... | collective-permute-start | bytes 491528 | tf_op jit(solution)/shard_map/ppermute | solution.py:12
  113.4 22.4 %collective-permute-start.15 = (bf16[128,640]{1,0:T(8,128)(2,1)S(1)}, bf16[128,640]{1,0:T(8,128)(2,1)S(1)}, u32[]{:S(2)}, u32[]{:S(2)}) collective-permute-start(bf16[128,640]{1,0:T(8,128)(2,1)S(1)} %bitcast.206), channel_id=1, source_target_pairs={{0,496},{1,497},{2,498},{3,499},{4,500},{5,501},{6,502},{7,503},{8... | collective-permute-start | bytes 491528 | tf_op jit(solution)/shard_map/ppermute | solution.py:12
  116.9 28.0 %collective-permute-start.16 = (bf16[128,640]{1,0:T(8,128)(2,1)S(1)}, bf16[128,640]{1,0:T(8,128)(2,1)S(1)}, u32[]{:S(2)}, u32[]{:S(2)}) collective-permute-start(bf16[128,640]{1,0:T(8,128)(2,1)S(1)} %bitcast.205), channel_id=1, source_target_pairs={{0,495},{1,496},{2,497},{3,498},{4,499},{5,500},{6,501},{7,502},{8... | collective-permute-start | bytes 491528 | tf_op jit(solution)/shard_map/ppermute | solution.py:12
  121.1 27.3 %collective-permute-start.17 = (bf16[128,640]{1,0:T(8,128)(2,1)S(1)}, bf16[128,640]{1,0:T(8,128)(2,1)S(1)}, u32[]{:S(2)}, u32[]{:S(2)}) collective-permute-start(bf16[128,640]{1,0:T(8,128)(2,1)S(1)} %bitcast.204), channel_id=1, source_target_pairs={{0,465},{1,466},{2,467},{3,468},{4,469},{5,470},{6,471},{7,472},{8... | collective-permute-start | bytes 491528 | tf_op jit(solution)/shard_map/ppermute | solution.py:12
  129.7 20.6 %collective-permute-start.18 = (bf16[128,640]{1,0:T(8,128)(2,1)S(1)}, bf16[128,640]{1,0:T(8,128)(2,1)S(1)}, u32[]{:S(2)}, u32[]{:S(2)}) collective-permute-start(bf16[128,640]{1,0:T(8,128)(2,1)S(1)} %bitcast.203), channel_id=1, source_target_pairs={{0,464},{1,465},{2,466},{3,467},{4,468},{5,469},{6,470},{7,471},{8... | collective-permute-start | bytes 491528 | tf_op jit(solution)/shard_map/ppermute | solution.py:12
  133.9 24.7 %collective-permute-start.19 = (bf16[128,640]{1,0:T(8,128)(2,1)S(1)}, bf16[128,640]{1,0:T(8,128)(2,1)S(1)}, u32[]{:S(2)}, u32[]{:S(2)}) collective-permute-start(bf16[128,640]{1,0:T(8,128)(2,1)S(1)} %bitcast.202), channel_id=1, source_target_pairs={{0,463},{1,464},{2,465},{3,466},{4,467},{5,468},{6,469},{7,470},{8... | collective-permute-start | bytes 491528 | tf_op jit(solution)/shard_map/ppermute | solution.py:12
  135.9 24.7 %collective-permute-start.20 = (bf16[128,640]{1,0:T(8,128)(2,1)S(1)}, bf16[128,640]{1,0:T(8,128)(2,1)S(1)}, u32[]{:S(2)}, u32[]{:S(2)}) collective-permute-start(bf16[128,640]{1,0:T(8,128)(2,1)S(1)} %bitcast.201), channel_id=1, source_target_pairs={{0,449},{1,450},{2,451},{3,452},{4,453},{5,454},{6,455},{7,456},{8... | collective-permute-start | bytes 491528 | tf_op jit(solution)/shard_map/ppermute | solution.py:12
  145.0 17.7 %collective-permute-start.21 = (bf16[128,640]{1,0:T(8,128)(2,1)S(1)}, bf16[128,640]{1,0:T(8,128)(2,1)S(1)}, u32[]{:S(2)}, u32[]{:S(2)}) collective-permute-start(bf16[128,640]{1,0:T(8,128)(2,1)S(1)} %bitcast.200), channel_id=1, source_target_pairs={{0,448},{1,449},{2,450},{3,451},{4,452},{5,453},{6,454},{7,455},{8... | collective-permute-start | bytes 491528 | tf_op jit(solution)/shard_map/ppermute | solution.py:12
  148.4 14.4 %collective-permute-start.22 = (bf16[128,640]{1,0:T(8,128)(2,1)S(1)}, bf16[128,640]{1,0:T(8,128)(2,1)S(1)}, u32[]{:S(2)}, u32[]{:S(2)}) collective-permute-start(bf16[128,640]{1,0:T(8,128)(2,1)S(1)} %bitcast.199), channel_id=1, source_target_pairs={{0,447},{1,448},{2,449},{3,450},{4,451},{5,452},{6,453},{7,454},{8... | collective-permute-start | bytes 491528 | tf_op jit(solution)/shard_map/ppermute | solution.py:12
  150.4 18.1 %collective-permute-start.23 = (bf16[128,640]{1,0:T(8,128)(2,1)S(1)}, bf16[128,640]{1,0:T(8,128)(2,1)S(1)}, u32[]{:S(2)}, u32[]{:S(2)}) collective-permute-start(bf16[128,640]{1,0:T(8,128)(2,1)S(1)} %bitcast.198), channel_id=1, source_target_pairs={{0,433},{1,434},{2,435},{3,436},{4,437},{5,438},{6,439},{7,440},{8... | collective-permute-start | bytes 491528 | tf_op jit(solution)/shard_map/ppermute | solution.py:12
  158.6 14.2 %collective-permute-start.24 = (bf16[128,640]{1,0:T(8,128)(2,1)S(1)}, bf16[128,640]{1,0:T(8,128)(2,1)S(1)}, u32[]{:S(2)}, u32[]{:S(2)}) collective-permute-start(bf16[128,640]{1,0:T(8,128)(2,1)S(1)} %bitcast.197), channel_id=1, source_target_pairs={{0,432},{1,433},{2,434},{3,435},{4,436},{5,437},{6,438},{7,439},{8... | collective-permute-start | bytes 491528 | tf_op jit(solution)/shard_map/ppermute | solution.py:12
  160.6 24.9 %collective-permute-start.25 = (bf16[128,640]{1,0:T(8,128)(2,1)S(1)}, bf16[128,640]{1,0:T(8,128)(2,1)S(1)}, u32[]{:S(2)}, u32[]{:S(2)}) collective-permute-start(bf16[128,640]{1,0:T(8,128)(2,1)S(1)} %bitcast.196), channel_id=1, source_target_pairs={{0,431},{1,432},{2,433},{3,434},{4,435},{5,436},{6,437},{7,438},{8... | collective-permute-start | bytes 491528 | tf_op jit(solution)/shard_map/ppermute | solution.py:12
  189.0 3.1 %copy-start.3 = (bf16[1,1,1,1024,1024]{4,3,2,1,0:T(8,128)(2,1)S(1)}, bf16[1,1,1,1024,1024]{4,3,2,1,0:T(8,128)(2,1)}, u32[]{:S(2)}) copy-start(bf16[1,1,1,1024,1024]{4,3,2,1,0:T(8,128)(2,1)} %param.55) | copy-start | bytes 6291460
where the time goes:
time: 197 us; the launch traced here: 196 us
  starting transfers between devices  116 us (59%)
  local copies, waits for them, and re-layouts  41.4 us (21%)
  waiting for transfers between devices  24.4 us (12%)
  matrix products  12.1 us (6%)
    ppermute x26, starting transfers between devices, from_behind(): return lax.ppermute(value, axis, pairs)  116 us
    ppermute x26, waiting for transfers between devices, from_behind(): return lax.ppermute(value, axis, pairs)  24.4 us
    slice x2, local copies, waits for them, and re-layouts, local(): moved = from_behind(outgoing[target], ('gx', 'gy', 'gz'), -stride)  16.2 us
    unnamed x58, local copies, waits for them, and re-layouts  15.6 us
    scatter x26, local copies, waits for them, and re-layouts, local(): received = received.at[target].set(moved)  4.81 us
  transfers between devices with their start and end apart: 26, of which 4 were waited for; matrix products, arithmetic and copies ran while one was open for 15% of the time, Pallas kernels for 0%

commit v1 on v0

v1 whole, which is shorter than its diff:
```python
import functools

import jax
import jax.numpy as jnp
from jax import lax
from jax.experimental import pallas as pl
from jax.experimental.pallas import tpu as pltpu
from jax.sharding import PartitionSpec as P

BLOCK = 128
HALF = BLOCK // 2
AXES = ("gx", "gy", "gz")
STEPS = (-1, 0, 1)
SIDES = (-1, 1)


def link(a, b, c):
    place = 9 * (a + 1) + 3 * (b + 1) + (c + 1)
    return place if place < 13 else place - 1


def cell(first, second):
    return 3 * (first + 1) + (second + 1)


def shift(value, axis, step, wrap):
    count = lax.axis_size(axis)
    pairs = [
        (source, (source + step) % count)
        for source in range(count)
        if wrap or 0 <= source + step < count
    ]
    return lax.ppermute(value, axis, pairs)


def head_kernel(links, schur, vectors, payload, low_b, high_b, low_c, high_c):
    blocks = payload.shape[0]
    right_side = vectors[...]
    for k in range(blocks):
        rows = slice(k * BLOCK, (k + 1) * BLOCK)
        payload[k, :, BLOCK:] = jnp.dot(
            schur[rows, :], right_side, preferred_element_type=jnp.float32
        ).astype(jnp.bfloat16)
        payload[k, :, :BLOCK] = schur[rows, rows]
    for b, out in zip(SIDES, (low_b, high_b)):
        for a in STEPS:
            for c in STEPS:
                out[cell(a, c)] = payload[links[link(a, b, c)], :HALF, :]
    for c, out in zip(SIDES, (low_c, high_c)):
        for a in STEPS:
            for b in STEPS:
                out[cell(a, b)] = payload[links[link(a, b, c)], HALF:, :]


def first_a_kernel(links, payload, from_low_b, from_high_b, low_a, high_a):
    for a, out in zip(SIDES, (low_a, high_a)):
        for c in STEPS:
            out[cell(-1, c)] = from_low_b[cell(a, c)]
            out[cell(1, c)] = from_high_b[cell(a, c)]
            out[cell(0, c)] = payload[links[link(a, 0, c)], :HALF, :]


def first_c_kernel(links, payload, from_low_b, from_high_b, from_low_a, from_high_a, low_c, high_c):
    for c, out in zip(SIDES, (low_c, high_c)):
        for b in STEPS:
            out[cell(-1, b)] = from_low_a[cell(b, c)]
            out[cell(1, b)] = from_high_a[cell(b, c)]
        out[cell(0, -1)] = from_low_b[cell(0, c)]
        out[cell(0, 1)] = from_high_b[cell(0, c)]
        out[cell(0, 0)] = payload[links[link(0, 0, c)], :HALF, :]


def second_a_kernel(links, payload, from_low_c, from_high_c, low_a, high_a):
    for a, out in zip(SIDES, (low_a, high_a)):
        for b in STEPS:
            out[cell(b, -1)] = from_low_c[cell(a, b)]
            out[cell(b, 1)] = from_high_c[cell(a, b)]
            out[cell(b, 0)] = payload[links[link(a, b, 0)], HALF:, :]


def second_b_kernel(links, payload, from_low_c, from_high_c, from_low_a, from_high_a, low_b, high_b):
    for b, out in zip(SIDES, (low_b, high_b)):
        for c in STEPS:
            out[cell(-1, c)] = from_low_a[cell(b, c)]
            out[cell(1, c)] = from_high_a[cell(b, c)]
        out[cell(0, -1)] = from_low_c[cell(0, b)]
        out[cell(0, 1)] = from_high_c[cell(0, b)]
        out[cell(0, 0)] = payload[links[link(0, b, 0)], HALF:, :]


def add_into(totals, slot, rows, piece):
    totals[slot, rows, :] = totals[slot, rows, :] + piece.astype(jnp.float32)


def early_kernel(
    links,
    payload,
    first_low_b,
    first_high_b,
    first_low_a,
    first_high_a,
    second_low_c,
    second_high_c,
    second_low_a,
    second_high_a,
    totals,
):
    top, bottom = slice(0, HALF), slice(HALF, BLOCK)
    totals[...] = payload[...].astype(jnp.float32)
    for b, piece in zip(SIDES, (first_low_b, first_high_b)):
        add_into(totals, links[link(0, -b, 0)], top, piece[cell(0, 0)])
    for a, piece in zip(SIDES, (first_low_a, first_high_a)):
        for b in STEPS:
            add_into(totals, links[link(-a, -b, 0)], top, piece[cell(b, 0)])
    for c, piece in zip(SIDES, (second_low_c, second_high_c)):
        add_into(totals, links[link(0, 0, -c)], bottom, piece[cell(0, 0)])
    for a, piece in zip(SIDES, (second_low_a, second_high_a)):
        for c in STEPS:
            add_into(totals, links[link(-a, 0, -c)], bottom, piece[cell(0, c)])


def tail_kernel(
    columns,
    layers,
    links,
    place,
    early,
    first_low_c,
    first_high_c,
    second_low_b,
    second_high_b,
    schur,
    assembled,
    update,
    totals,
    scaled,
    counts,
):
    blocks = early.shape[0]
    top, bottom = slice(0, HALF), slice(HALF, BLOCK)
    row, layer = place[0], place[1]
    for k in range(blocks):
        counts[k] = 1
    for a in STEPS:
        for b in STEPS:
            for c in STEPS:
                if (a, b, c) == (0, 0, 0):
                    continue
                slot = links[link(a, b, c)]
                alive = (row + b >= 0) & (row + b < columns) & (layer + c >= 0) & (layer + c < layers)
                counts[slot] = counts[slot] + jnp.where(alive, 1, 0)
    totals[...] = early[...]
    for c, piece in zip(SIDES, (first_low_c, first_high_c)):
        for a in STEPS:
            for b in STEPS:
                add_into(totals, links[link(-a, -b, -c)], top, piece[cell(a, b)])
    for b, piece in zip(SIDES, (second_low_b, second_high_b)):
        for a in STEPS:
            for c in STEPS:
                add_into(totals, links[link(-a, -b, -c)], bottom, piece[cell(a, c)])
    for k in range(blocks):
        rows = slice(k * BLOCK, (k + 1) * BLOCK)
        coupling = totals[k, :, :BLOCK]
        summed = totals[k, :, BLOCK:]
        summed_high = summed.astype(jnp.bfloat16)
        summed_low = (summed - summed_high.astype(jnp.float32)).astype(jnp.bfloat16)
        coupling_high = coupling.astype(jnp.bfloat16)
        coupling_low = (coupling - coupling_high.astype(jnp.float32)).astype(jnp.bfloat16)
        assembled[rows, :] = summed_high
        mixed = jnp.dot(coupling_high, summed_high, preferred_element_type=jnp.float32)
        mixed += jnp.dot(coupling_high, summed_low, preferred_element_type=jnp.float32)
        mixed += jnp.dot(coupling_low, summed_high, preferred_element_type=jnp.float32)
        share = jnp.full((BLOCK, 1), counts[k], jnp.int32).astype(jnp.float32)
        scaled[rows, :] = (mixed / share).astype(jnp.bfloat16)
    for k in range(blocks):
        rows = slice(k * BLOCK, (k + 1) * BLOCK)
        update[rows, :] = jnp.dot(
            schur[rows, :], scaled[...], preferred_element_type=jnp.float32
        ).astype(jnp.bfloat16)


def call(kernel, name, outs, *operands, smem=1, scratch=()):
    specs = [
        pl.BlockSpec(memory_space=pltpu.SMEM if i < smem else pltpu.VMEM) for i in range(len(operands))
    ]
    return pl.pallas_call(
        kernel,
        name=name,
        out_shape=outs,
        in_specs=specs,
        out_specs=[pl.BlockSpec(memory_space=pltpu.VMEM) for _ in outs],
        scratch_shapes=list(scratch),
        compiler_params=pltpu.CompilerParams(vmem_limit_bytes=40 * 1024 * 1024),
    )(*operands)


def local(schur, block_map, vectors):
    matrix = schur[0, 0, 0]
    right_side = vectors[0, 0, 0]
    links = block_map[0, 0, 0]
    order, width = right_side.shape
    blocks = order // BLOCK
    full = BLOCK + width
    bundle = jax.ShapeDtypeStruct((9, HALF, full), jnp.bfloat16)
    place = jnp.stack([lax.axis_index("gy"), lax.axis_index("gz")]).astype(jnp.int32)

    payload, b_low, b_high, c_low, c_high = call(
        head_kernel,
        "head",
        [jax.ShapeDtypeStruct((blocks, BLOCK, full), jnp.bfloat16)] + [bundle] * 4,
        links,
        matrix,
        right_side,
    )
    first_b = [shift(v, "gy", s, False) for s, v in zip(SIDES, (b_low, b_high))]
    second_c = [shift(v, "gz", s, False) for s, v in zip(SIDES, (c_low, c_high))]
    sent = call(second_a_kernel, "second_a", [bundle] * 2, links, payload, *second_c)
    second_a = [shift(v, "gx", s, True) for s, v in zip(SIDES, sent)]
    sent = call(first_a_kernel, "first_a", [bundle] * 2, links, payload, *first_b)
    first_a = [shift(v, "gx", s, True) for s, v in zip(SIDES, sent)]
    sent = call(second_b_kernel, "second_b", [bundle] * 2, links, payload, *second_c, *second_a)
    second_b = [shift(v, "gy", s, False) for s, v in zip(SIDES, sent)]
    sent = call(first_c_kernel, "first_c", [bundle] * 2, links, payload, *first_b, *first_a)
    first_c = [shift(v, "gz", s, False) for s, v in zip(SIDES, sent)]
    (early,) = call(
        early_kernel,
        "early",
        [jax.ShapeDtypeStruct((blocks, BLOCK, full), jnp.float32)],
        links,
        payload,
        *first_b,
        *first_a,
        *second_c,
        *second_a,
    )
    assembled, update = call(
        functools.partial(tail_kernel, lax.axis_size("gy"), lax.axis_size("gz")),
        "tail",
        [jax.ShapeDtypeStruct((order, width), jnp.bfloat16)] * 2,
        links,
        place,
        early,
        *first_c,
        *second_b,
        matrix,
        smem=2,
        scratch=[
            pltpu.VMEM((blocks, BLOCK, full), jnp.float32),
            pltpu.VMEM((order, width), jnp.bfloat16),
            pltpu.SMEM((blocks,), jnp.int32),
        ],
    )
    return (assembled[None, None, None], update[None, None, None])


def solution(mesh):
    placed = (
        P("gx", "gy", "gz", None, None),
        P("gx", "gy", "gz", None),
        P("gx", "gy", "gz", None, None),
    )
    return jax.shard_map(
        local,
        mesh=mesh,
        in_specs=placed,
        out_specs=(P("gx", "gy", "gz", None, None), P("gx", "gy", "gz", None, None)),
        check_vma=False,
    )
```

time: 197 us -> 121 us (0.61)
  the two profiles are of different devices: /device:TPU:47 before, /device:TPU:40 now
where the time goes in v1:
time: 121 us; the launch traced here: 120 us
  starting transfers between devices  52 us (43%)
  waiting for transfers between devices  44.4 us (37%)
  Pallas kernels  13.5 us (11%)
  local copies, waits for them, and re-layouts  9.07 us (7%)
    ppermute x12, starting transfers between devices, shift(): return lax.ppermute(value, axis, pairs)  52 us
    ppermute x12, waiting for transfers between devices, shift(): return lax.ppermute(value, axis, pairs)  44.4 us
    pallas_call x7, Pallas kernels, call(): pl.pallas_call(kernel, name=name, out_shape=outs, in_specs=specs, out_spe...  13.5 us
    unnamed x30, local copies, waits for them, and re-layouts  9.07 us
  transfers between devices with their start and end apart: 12, of which 8 were waited for; matrix products, arithmetic and copies ran while one was open for 0% of the time, Pallas kernels for 5%

profile of v1, /device:TPU:40, one launch (start us, length us, event | category | flops | bytes accessed | tf_op | source)
XLA Modules:
  0.0 119.8 jit_solution(1324340966877198842)
XLA Ops:
  0.6 0.0 copy-start
  0.6 1.6 %copy-done = bf16[1,1,1,1024,1024]{4,3,2,1,0:T(8,128)(2,1)S(1)} copy-done((bf16[1,1,1,1024,1024]{4,3,2,1,0:T(8,128)(2,1)S(1)}, bf16[1,1,1,1024,1024]{4,3,2,1,0:T(8,128)(2,1)}, u32[]{:S(2)}) %copy-start) | copy-done | bytes 2097176
  2.2 1.2 %copy-done.12 = bf16[1,1,1,1024,512]{4,3,2,1,0:T(8,128)(2,1)S(1)} copy-done((bf16[1,1,1,1024,512]{4,3,2,1,0:T(8,128)(2,1)S(1)}, bf16[1,1,1,1024,512]{4,3,2,1,0:T(8,128)(2,1)}, u32[]{:S(2)}) %copy-start.12) | copy-done | bytes 1048600
  3.5 0.7 copy-done.13
  4.1 2.0 %head.1 = (bf16[8,128,640]{2,1,0:T(8,128)(2,1)S(1)}, bf16[9,64,640]{2,1,0:T(8,128)(2,1)S(1)}, bf16[9,64,640]{2,1,0:T(8,128)(2,1)S(1)}, bf16[9,64,640]{2,1,0:T(8,128)(2,1)S(1)}, bf16[9,64,640]{2,1,0:T(8,128)(2,1)S(1)}) custom-call(s32[26]{0:T(128)S(1)} %bitcast.10, bf16[1024,1024]{1,0:T(8,128)(2,1)S(1)} %bitcast.7, bf16[1024,512]{1,0:T(8,128)(2,1)S(1)} %bitcast.9), custom_call_target="tpu_custom_call" | custom-call | tf_op jit(solution)/shard_map/head/pallas_call | solution.py:186
  6.1 4.9 %collective-permute-start.4 = (bf16[9,64,640]{2,1,0:T(8,128)(2,1)S(1)}, bf16[9,64,640]{2,1,0:T(8,128)(2,1)S(1)}, u32[]{:S(2)}, u32[]{:S(2)}) collective-permute-start(bf16[9,64,640]{2,1,0:T(8,128)(2,1)S(1)} %get-tuple-element.22), channel_id=1, source_target_pairs={{1,0},{2,1},{3,2},{4,3},{5,4},{6,5},{7,6},{8,7},{9,8},{10,9},{11,1... | collective-permute-start | bytes 2211848 | tf_op jit(solution)/shard_map/ppermute | solution.py:33
  11.0 1.9 %collective-permute-start.5 = (bf16[9,64,640]{2,1,0:T(8,128)(2,1)S(1)}, bf16[9,64,640]{2,1,0:T(8,128)(2,1)S(1)}, u32[]{:S(2)}, u32[]{:S(2)}) collective-permute-start(bf16[9,64,640]{2,1,0:T(8,128)(2,1)S(1)} %get-tuple-element.23), channel_id=1, source_target_pairs={{0,1},{1,2},{2,3},{3,4},{4,5},{5,6},{6,7},{7,8},{8,9},{9,10},{10,1... | collective-permute-start | bytes 2211848 | tf_op jit(solution)/shard_map/ppermute | solution.py:33
  13.0 2.2 %collective-permute-start = (bf16[9,64,640]{2,1,0:T(8,128)(2,1)S(1)}, bf16[9,64,640]{2,1,0:T(8,128)(2,1)S(1)}, u32[]{:S(2)}, u32[]{:S(2)}) collective-permute-start(bf16[9,64,640]{2,1,0:T(8,128)(2,1)S(1)} %get-tuple-element.18), channel_id=1, source_target_pairs={{16,0},{32,16},{48,32},{17,1},{33,17},{49,33},{18,2},{34,18},{50,3... | collective-permute-start | bytes 2211848 | tf_op jit(solution)/shard_map/ppermute | solution.py:33
  15.2 4.5 %collective-permute-start.1 = (bf16[9,64,640]{2,1,0:T(8,128)(2,1)S(1)}, bf16[9,64,640]{2,1,0:T(8,128)(2,1)S(1)}, u32[]{:S(2)}, u32[]{:S(2)}) collective-permute-start(bf16[9,64,640]{2,1,0:T(8,128)(2,1)S(1)} %get-tuple-element.19), channel_id=1, source_target_pairs={{0,16},{16,32},{32,48},{1,17},{17,33},{33,49},{2,18},{18,34},{34,5... | collective-permute-start | bytes 2211848 | tf_op jit(solution)/shard_map/ppermute | solution.py:33
  19.8 10.0 %collective-permute-done.4.from_low_c.second_low_c = bf16[9,64,640]{2,1,0:T(8,128)(2,1)S(1)} collective-permute-done((bf16[9,64,640]{2,1,0:T(8,128)(2,1)S(1)}, bf16[9,64,640]{2,1,0:T(8,128)(2,1)S(1)}, u32[]{:S(2)}, u32[]{:S(2)}) %collective-permute-start.4) | collective-permute-done | bytes 737312 | tf_op jit(solution)/shard_map/ppermute | solution.py:33
  29.7 10.1 %collective-permute-done.5.from_high_c.second_high_c = bf16[9,64,640]{2,1,0:T(8,128)(2,1)S(1)} collective-permute-done((bf16[9,64,640]{2,1,0:T(8,128)(2,1)S(1)}, bf16[9,64,640]{2,1,0:T(8,128)(2,1)S(1)}, u32[]{:S(2)}, u32[]{:S(2)}) %collective-permute-start.5) | collective-permute-done | bytes 737312 | tf_op jit(solution)/shard_map/ppermute | solution.py:33
  39.8 0.7 second_a.1
  40.5 10.9 %collective-permute-start.6 = (bf16[9,64,640]{2,1,0:T(8,128)(2,1)S(1)}, bf16[9,64,640]{2,1,0:T(8,128)(2,1)S(1)}, u32[]{:S(2)}, u32[]{:S(2)}) collective-permute-start(bf16[9,64,640]{2,1,0:T(8,128)(2,1)S(1)} %get-tuple-element.24), channel_id=1, source_target_pairs={{0,448},{64,0},{128,64},{192,128},{256,192},{320,256},{384,320},{4... | collective-permute-start | bytes 2211848 | tf_op jit(solution)/shard_map/ppermute | solution.py:33
  51.4 1.9 %collective-permute-start.7 = (bf16[9,64,640]{2,1,0:T(8,128)(2,1)S(1)}, bf16[9,64,640]{2,1,0:T(8,128)(2,1)S(1)}, u32[]{:S(2)}, u32[]{:S(2)}) collective-permute-start(bf16[9,64,640]{2,1,0:T(8,128)(2,1)S(1)} %get-tuple-element.25), channel_id=1, source_target_pairs={{0,64},{64,128},{128,192},{192,256},{256,320},{320,384},{384,448},... | collective-permute-start | bytes 2211848 | tf_op jit(solution)/shard_map/ppermute | solution.py:33
  53.4 0.0 collective-permute-done.from_low_b.first_low_b
  53.4 0.0 collective-permute-done.1.from_high_b.first_high_b
  53.4 0.0 copy-start.2
  53.4 0.7 first_a.1
  54.1 9.2 %collective-permute-start.2 = (bf16[9,64,640]{2,1,0:T(8,128)(2,1)S(1)}, bf16[9,64,640]{2,1,0:T(8,128)(2,1)S(1)}, u32[]{:S(2)}, u32[]{:S(2)}) collective-permute-start(bf16[9,64,640]{2,1,0:T(8,128)(2,1)S(1)} %get-tuple-element.20), channel_id=1, source_target_pairs={{0,448},{64,0},{128,64},{192,128},{256,192},{320,256},{384,320},{4... | collective-permute-start | bytes 2211848 | tf_op jit(solution)/shard_map/ppermute | solution.py:33
  63.3 1.9 %collective-permute-start.3 = (bf16[9,64,640]{2,1,0:T(8,128)(2,1)S(1)}, bf16[9,64,640]{2,1,0:T(8,128)(2,1)S(1)}, u32[]{:S(2)}, u32[]{:S(2)}) collective-permute-start(bf16[9,64,640]{2,1,0:T(8,128)(2,1)S(1)} %get-tuple-element.21), channel_id=1, source_target_pairs={{0,64},{64,128},{128,192},{192,256},{256,320},{320,384},{384,448},... | collective-permute-start | bytes 2211848 | tf_op jit(solution)/shard_map/ppermute | solution.py:33
  65.2 0.0 collective-permute-done.6.second_low_a.from_low_a
  65.2 0.0 copy-start.4
  65.2 0.8 collective-permute-done.7.second_high_a.from_high_a
  66.0 1.8 %second_b.1 = (bf16[9,64,640]{2,1,0:T(8,128)(2,1)}, bf16[9,64,640]{2,1,0:T(8,128)(2,1)}) custom-call(s32[26]{0:T(128)S(1)} %bitcast.13, bf16[8,128,640]{2,1,0:T(8,128)(2,1)S(1)} %get-tuple-element.17.payload, bf16[9,64,640]{2,1,0:T(8,128)(2,1)S(1)} %collective-permute-done.4.from_low_c.second_low_c, ...), custom_call_target="tpu_custom_call" | custom-call | tf_op jit(solution)/shard_map/second_b/pallas_call | solution.py:186
  67.8 0.0 copy-done.4
  67.8 0.0 copy-done.6
  67.8 5.7 %collective-permute-start.10 = (bf16[9,64,640]{2,1,0:T(8,128)(2,1)}, bf16[9,64,640]{2,1,0:T(8,128)(2,1)}, u32[]{:S(2)}, u32[]{:S(2)}) collective-permute-start(bf16[9,64,640]{2,1,0:T(8,128)(2,1)} %get-tuple-element.28), channel_id=1, source_target_pairs={{16,0},{32,16},{48,32},{17,1},{33,17},{49,33},{18,2},{34,18},{50,3... | collective-permute-start | bytes 2211848 | tf_op jit(solution)/shard_map/ppermute | solution.py:33
  73.5 0.0 copy-start.14
  73.5 2.0 %collective-permute-start.11 = (bf16[9,64,640]{2,1,0:T(8,128)(2,1)}, bf16[9,64,640]{2,1,0:T(8,128)(2,1)}, u32[]{:S(2)}, u32[]{:S(2)}) collective-permute-start(bf16[9,64,640]{2,1,0:T(8,128)(2,1)} %get-tuple-element.29), channel_id=1, source_target_pairs={{0,16},{16,32},{32,48},{1,17},{17,33},{33,49},{2,18},{18,34},{34,5... | collective-permute-start | bytes 2211848 | tf_op jit(solution)/shard_map/ppermute | solution.py:33
  75.5 3.3 %collective-permute-done.2.first_low_a.from_low_a = bf16[9,64,640]{2,1,0:T(8,128)(2,1)S(1)} collective-permute-done((bf16[9,64,640]{2,1,0:T(8,128)(2,1)S(1)}, bf16[9,64,640]{2,1,0:T(8,128)(2,1)S(1)}, u32[]{:S(2)}, u32[]{:S(2)}) %collective-permute-start.2) | collective-permute-done | bytes 737312 | tf_op jit(solution)/shard_map/ppermute | solution.py:33
  78.8 5.3 %collective-permute-done.3.first_high_a.from_high_a = bf16[9,64,640]{2,1,0:T(8,128)(2,1)S(1)} collective-permute-done((bf16[9,64,640]{2,1,0:T(8,128)(2,1)S(1)}, bf16[9,64,640]{2,1,0:T(8,128)(2,1)S(1)}, u32[]{:S(2)}, u32[]{:S(2)}) %collective-permute-start.3) | collective-permute-done | bytes 737312 | tf_op jit(solution)/shard_map/ppermute | solution.py:33
  84.2 0.0 copy-done.2
  84.2 1.8 %first_c.1 = (bf16[9,64,640]{2,1,0:T(8,128)(2,1)}, bf16[9,64,640]{2,1,0:T(8,128)(2,1)}) custom-call(s32[26]{0:T(128)S(1)} %bitcast.14, bf16[8,128,640]{2,1,0:T(8,128)(2,1)S(1)} %get-tuple-element.17.payload, bf16[9,64,640]{2,1,0:T(8,128)(2,1)S(1)} %collective-permute-done.from_low_b.first_low_b, ...), custom_call_target="tpu_custom_call" | custom-call | tf_op jit(solution)/shard_map/first_c/pallas_call | solution.py:186
  86.0 0.0 copy-done.10
  86.0 4.8 %collective-permute-start.8 = (bf16[9,64,640]{2,1,0:T(8,128)(2,1)}, bf16[9,64,640]{2,1,0:T(8,128)(2,1)}, u32[]{:S(2)}, u32[]{:S(2)}) collective-permute-start(bf16[9,64,640]{2,1,0:T(8,128)(2,1)} %get-tuple-element.26), channel_id=1, source_target_pairs={{1,0},{2,1},{3,2},{4,3},{5,4},{6,5},{7,6},{8,7},{9,8},{10,9},{11,1... | collective-permute-start | bytes 2211848 | tf_op jit(solution)/shard_map/ppermute | solution.py:33
  90.7 1.9 %collective-permute-start.9 = (bf16[9,64,640]{2,1,0:T(8,128)(2,1)}, bf16[9,64,640]{2,1,0:T(8,128)(2,1)}, u32[]{:S(2)}, u32[]{:S(2)}) collective-permute-start(bf16[9,64,640]{2,1,0:T(8,128)(2,1)} %get-tuple-element.27), channel_id=1, source_target_pairs={{0,1},{1,2},{2,3},{3,4},{4,5},{5,6},{6,7},{7,8},{8,9},{9,10},{10,1... | collective-permute-start | bytes 2211848 | tf_op jit(solution)/shard_map/ppermute | solution.py:33
  92.6 0.1 pad_add_fusion.place
  92.7 1.1 copy-done.3
  93.8 1.1 copy-done.5
  95.0 1.1 copy-done.7
  96.1 1.1 copy-done.9
  97.2 1.1 copy-done.11
  98.3 1.0 early.1
  99.3 0.0 collective-permute-done.10.second_low_b
  99.3 5.7 %collective-permute-done.11.second_high_b = bf16[9,64,640]{2,1,0:T(8,128)(2,1)} collective-permute-done((bf16[9,64,640]{2,1,0:T(8,128)(2,1)}, bf16[9,64,640]{2,1,0:T(8,128)(2,1)}, u32[]{:S(2)}, u32[]{:S(2)}) %collective-permute-start.11) | collective-permute-done | bytes 737312 | tf_op jit(solution)/shard_map/ppermute | solution.py:33
  105.0 5.6 %collective-permute-done.8.first_low_c = bf16[9,64,640]{2,1,0:T(8,128)(2,1)} collective-permute-done((bf16[9,64,640]{2,1,0:T(8,128)(2,1)}, bf16[9,64,640]{2,1,0:T(8,128)(2,1)}, u32[]{:S(2)}, u32[]{:S(2)}) %collective-permute-start.8) | collective-permute-done | bytes 737312 | tf_op jit(solution)/shard_map/ppermute | solution.py:33
  110.6 3.6 %collective-permute-done.9.first_high_c = bf16[9,64,640]{2,1,0:T(8,128)(2,1)} collective-permute-done((bf16[9,64,640]{2,1,0:T(8,128)(2,1)}, bf16[9,64,640]{2,1,0:T(8,128)(2,1)}, u32[]{:S(2)}, u32[]{:S(2)}) %collective-permute-start.9) | collective-permute-done | bytes 737312 | tf_op jit(solution)/shard_map/ppermute | solution.py:33
  114.2 5.7 %tail.1 = (bf16[1024,512]{1,0:T(8,128)(2,1)}, bf16[1024,512]{1,0:T(8,128)(2,1)}) custom-call(s32[26]{0:T(128)S(1)} %bitcast.16, s32[2]{0:T(128)S(1)} %pad_add_fusion.place, f32[8,128,640]{2,1,0:T(8,128)S(1)} %early.1, bf16[9,64,640]{2,1,0:T(8,128)(2,1)} %collective-permute-done.8.first_low_c, bf16[9,64,640]{2,1,0:T(8,128)(2,1)} %collective-permute-done.9.first_high_c, ...), custom_call_target="tpu_custom_call" | custom-call | tf_op jit(solution)/shard_map/tail/pallas_call | solution.py:186
  (14 shorter events, 0.0 us)
Async XLA Ops:
  0.6 1.6 %copy-start = (bf16[1,1,1,1024,1024]{4,3,2,1,0:T(8,128)(2,1)S(1)}, bf16[1,1,1,1024,1024]{4,3,2,1,0:T(8,128)(2,1)}, u32[]{:S(2)}) copy-start(bf16[1,1,1,1024,1024]{4,3,2,1,0:T(8,128)(2,1)} %param.3) | copy-start | bytes 6291460
  2.2 1.2 %copy-start.12 = (bf16[1,1,1,1024,512]{4,3,2,1,0:T(8,128)(2,1)S(1)}, bf16[1,1,1,1024,512]{4,3,2,1,0:T(8,128)(2,1)}, u32[]{:S(2)}) copy-start(bf16[1,1,1,1024,512]{4,3,2,1,0:T(8,128)(2,1)} %param.5) | copy-start | bytes 3145732
  3.4 0.7 copy-start.13
  6.1 23.6 %collective-permute-start.4 = (bf16[9,64,640]{2,1,0:T(8,128)(2,1)S(1)}, bf16[9,64,640]{2,1,0:T(8,128)(2,1)S(1)}, u32[]{:S(2)}, u32[]{:S(2)}) collective-permute-start(bf16[9,64,640]{2,1,0:T(8,128)(2,1)S(1)} %get-tuple-element.22), channel_id=1, source_target_pairs={{1,0},{2,1},{3,2},{4,3},{5,4},{6,5},{7,6},{8,7},{9,8},{10,9},{11,1... | collective-permute-start | bytes 2211848 | tf_op jit(solution)/shard_map/ppermute | solution.py:33
  11.0 28.8 %collective-permute-start.5 = (bf16[9,64,640]{2,1,0:T(8,128)(2,1)S(1)}, bf16[9,64,640]{2,1,0:T(8,128)(2,1)S(1)}, u32[]{:S(2)}, u32[]{:S(2)}) collective-permute-start(bf16[9,64,640]{2,1,0:T(8,128)(2,1)S(1)} %get-tuple-element.23), channel_id=1, source_target_pairs={{0,1},{1,2},{2,3},{3,4},{4,5},{5,6},{6,7},{7,8},{8,9},{9,10},{10,1... | collective-permute-start | bytes 2211848 | tf_op jit(solution)/shard_map/ppermute | solution.py:33
  13.0 40.4 %collective-permute-start = (bf16[9,64,640]{2,1,0:T(8,128)(2,1)S(1)}, bf16[9,64,640]{2,1,0:T(8,128)(2,1)S(1)}, u32[]{:S(2)}, u32[]{:S(2)}) collective-permute-start(bf16[9,64,640]{2,1,0:T(8,128)(2,1)S(1)} %get-tuple-element.18), channel_id=1, source_target_pairs={{16,0},{32,16},{48,32},{17,1},{33,17},{49,33},{18,2},{34,18},{50,3... | collective-permute-start | bytes 2211848 | tf_op jit(solution)/shard_map/ppermute | solution.py:33
  15.2 38.2 %collective-permute-start.1 = (bf16[9,64,640]{2,1,0:T(8,128)(2,1)S(1)}, bf16[9,64,640]{2,1,0:T(8,128)(2,1)S(1)}, u32[]{:S(2)}, u32[]{:S(2)}) collective-permute-start(bf16[9,64,640]{2,1,0:T(8,128)(2,1)S(1)} %get-tuple-element.19), channel_id=1, source_target_pairs={{0,16},{16,32},{32,48},{1,17},{17,33},{33,49},{2,18},{18,34},{34,5... | collective-permute-start | bytes 2211848 | tf_op jit(solution)/shard_map/ppermute | solution.py:33
  40.5 24.7 %collective-permute-start.6 = (bf16[9,64,640]{2,1,0:T(8,128)(2,1)S(1)}, bf16[9,64,640]{2,1,0:T(8,128)(2,1)S(1)}, u32[]{:S(2)}, u32[]{:S(2)}) collective-permute-start(bf16[9,64,640]{2,1,0:T(8,128)(2,1)S(1)} %get-tuple-element.24), channel_id=1, source_target_pairs={{0,448},{64,0},{128,64},{192,128},{256,192},{320,256},{384,320},{4... | collective-permute-start | bytes 2211848 | tf_op jit(solution)/shard_map/ppermute | solution.py:33
  51.4 14.6 %collective-permute-start.7 = (bf16[9,64,640]{2,1,0:T(8,128)(2,1)S(1)}, bf16[9,64,640]{2,1,0:T(8,128)(2,1)S(1)}, u32[]{:S(2)}, u32[]{:S(2)}) collective-permute-start(bf16[9,64,640]{2,1,0:T(8,128)(2,1)S(1)} %get-tuple-element.25), channel_id=1, source_target_pairs={{0,64},{64,128},{128,192},{192,256},{256,320},{320,384},{384,448},... | collective-permute-start | bytes 2211848 | tf_op jit(solution)/shard_map/ppermute | solution.py:33
  53.4 30.8 %copy-start.2 = (bf16[9,64,640]{2,1,0:T(8,128)(2,1)}, bf16[9,64,640]{2,1,0:T(8,128)(2,1)S(1)}, u32[]{:S(2)}) copy-start(bf16[9,64,640]{2,1,0:T(8,128)(2,1)S(1)} %collective-permute-done.1.from_high_b.first_high_b) | copy-start | bytes 2211844
  54.1 24.8 %collective-permute-start.2 = (bf16[9,64,640]{2,1,0:T(8,128)(2,1)S(1)}, bf16[9,64,640]{2,1,0:T(8,128)(2,1)S(1)}, u32[]{:S(2)}, u32[]{:S(2)}) collective-permute-start(bf16[9,64,640]{2,1,0:T(8,128)(2,1)S(1)} %get-tuple-element.20), channel_id=1, source_target_pairs={{0,448},{64,0},{128,64},{192,128},{256,192},{320,256},{384,320},{4... | collective-permute-start | bytes 2211848 | tf_op jit(solution)/shard_map/ppermute | solution.py:33
  63.3 20.9 %collective-permute-start.3 = (bf16[9,64,640]{2,1,0:T(8,128)(2,1)S(1)}, bf16[9,64,640]{2,1,0:T(8,128)(2,1)S(1)}, u32[]{:S(2)}, u32[]{:S(2)}) collective-permute-start(bf16[9,64,640]{2,1,0:T(8,128)(2,1)S(1)} %get-tuple-element.21), channel_id=1, source_target_pairs={{0,64},{64,128},{128,192},{192,256},{256,320},{320,384},{384,448},... | collective-permute-start | bytes 2211848 | tf_op jit(solution)/shard_map/ppermute | solution.py:33
  65.2 2.6 %copy-start.4 = (bf16[9,64,640]{2,1,0:T(8,128)(2,1)}, bf16[9,64,640]{2,1,0:T(8,128)(2,1)S(1)}, u32[]{:S(2)}) copy-start(bf16[9,64,640]{2,1,0:T(8,128)(2,1)S(1)} %collective-permute-done.6.second_low_a.from_low_a) | copy-start | bytes 2211844
  66.0 1.8 %copy-start.6 = (bf16[9,64,640]{2,1,0:T(8,128)(2,1)}, bf16[9,64,640]{2,1,0:T(8,128)(2,1)S(1)}, u32[]{:S(2)}) copy-start(bf16[9,64,640]{2,1,0:T(8,128)(2,1)S(1)} %collective-permute-done.7.second_high_a.from_high_a) | copy-start | bytes 2211844
  67.8 31.5 %collective-permute-start.10 = (bf16[9,64,640]{2,1,0:T(8,128)(2,1)}, bf16[9,64,640]{2,1,0:T(8,128)(2,1)}, u32[]{:S(2)}, u32[]{:S(2)}) collective-permute-start(bf16[9,64,640]{2,1,0:T(8,128)(2,1)} %get-tuple-element.28), channel_id=1, source_target_pairs={{16,0},{32,16},{48,32},{17,1},{33,17},{49,33},{18,2},{34,18},{50,3... | collective-permute-start | bytes 2211848 | tf_op jit(solution)/shard_map/ppermute | solution.py:33
  73.5 19.2 %copy-start.14 = (s32[1,1,1,26]{3,2,1,0:T(1,128)S(1)}, s32[1,1,1,26]{3,2,1,0:T(1,128)}, u32[]{:S(2)}) copy-start(s32[1,1,1,26]{3,2,1,0:T(1,128)} %param.4) | copy-start | bytes 316
  73.5 31.4 %collective-permute-start.11 = (bf16[9,64,640]{2,1,0:T(8,128)(2,1)}, bf16[9,64,640]{2,1,0:T(8,128)(2,1)}, u32[]{:S(2)}, u32[]{:S(2)}) collective-permute-start(bf16[9,64,640]{2,1,0:T(8,128)(2,1)} %get-tuple-element.29), channel_id=1, source_target_pairs={{0,16},{16,32},{32,48},{1,17},{17,33},{33,49},{2,18},{18,34},{34,5... | collective-permute-start | bytes 2211848 | tf_op jit(solution)/shard_map/ppermute | solution.py:33
  78.8 7.1 %copy-start.8 = (bf16[9,64,640]{2,1,0:T(8,128)(2,1)}, bf16[9,64,640]{2,1,0:T(8,128)(2,1)S(1)}, u32[]{:S(2)}) copy-start(bf16[9,64,640]{2,1,0:T(8,128)(2,1)S(1)} %collective-permute-done.2.first_low_a.from_low_a) | copy-start | bytes 2211844
  84.2 1.8 %copy-start.10 = (bf16[9,64,640]{2,1,0:T(8,128)(2,1)}, bf16[9,64,640]{2,1,0:T(8,128)(2,1)S(1)}, u32[]{:S(2)}) copy-start(bf16[9,64,640]{2,1,0:T(8,128)(2,1)S(1)} %collective-permute-done.3.first_high_a.from_high_a) | copy-start | bytes 2211844
  86.0 24.6 %collective-permute-start.8 = (bf16[9,64,640]{2,1,0:T(8,128)(2,1)}, bf16[9,64,640]{2,1,0:T(8,128)(2,1)}, u32[]{:S(2)}, u32[]{:S(2)}) collective-permute-start(bf16[9,64,640]{2,1,0:T(8,128)(2,1)} %get-tuple-element.26), channel_id=1, source_target_pairs={{1,0},{2,1},{3,2},{4,3},{5,4},{6,5},{7,6},{8,7},{9,8},{10,9},{11,1... | collective-permute-start | bytes 2211848 | tf_op jit(solution)/shard_map/ppermute | solution.py:33
  90.7 23.5 %collective-permute-start.9 = (bf16[9,64,640]{2,1,0:T(8,128)(2,1)}, bf16[9,64,640]{2,1,0:T(8,128)(2,1)}, u32[]{:S(2)}, u32[]{:S(2)}) collective-permute-start(bf16[9,64,640]{2,1,0:T(8,128)(2,1)} %get-tuple-element.27), channel_id=1, source_target_pairs={{0,1},{1,2},{2,3},{3,4},{4,5},{5,6},{6,7},{7,8},{8,9},{9,10},{10,1... | collective-permute-start | bytes 2211848 | tf_op jit(solution)/shard_map/ppermute | solution.py:33
  92.7 1.1 copy-start.3
  93.8 1.1 copy-start.5
  95.0 1.1 copy-start.7
  96.1 1.1 copy-start.9
  97.2 1.1 copy-start.11
  98.3 15.9 %copy-start.1 = (bf16[1,1,1,1024,1024]{4,3,2,1,0:T(8,128)(2,1)S(1)}, bf16[1,1,1,1024,1024]{4,3,2,1,0:T(8,128)(2,1)}, u32[]{:S(2)}) copy-start(bf16[1,1,1,1024,1024]{4,3,2,1,0:T(8,128)(2,1)} %param.3) | copy-start | bytes 6291460

commit v2 on v1

v2 whole, which is shorter than its diff:
```python
import functools

import jax
import jax.numpy as jnp
from jax import lax
from jax.experimental import pallas as pl
from jax.experimental.pallas import tpu as pltpu
from jax.sharding import PartitionSpec as P


BLOCK = 128
HALF = BLOCK // 2
STEPS = (-1, 0, 1)
SIDES = (-1, 1)
MIB = 1024 * 1024


def link(a, b, c):
    place = 9 * (a + 1) + 3 * (b + 1) + (c + 1)
    return place if place < 13 else place - 1


def cell(first, second):
    return 3 * (first + 1) + (second + 1)


def shift(value, axis, step, wrap):
    count = lax.axis_size(axis)
    pairs = [
        (source, (source + step) % count)
        for source in range(count)
        if wrap or 0 <= source + step < count
    ]
    return lax.ppermute(value, axis, pairs)


def head_kernel(links, matrix, right_side, top, bottom, low_c, high_c):
    for k in range(top.shape[0]):
        rows = slice(k * BLOCK, (k + 1) * BLOCK)
        product = jnp.dot(
            matrix[rows, :], right_side[...], preferred_element_type=jnp.float32
        ).astype(jnp.bfloat16)
        diagonal = matrix[rows, rows]
        top[k, :, BLOCK:] = product[:HALF]
        top[k, :, :BLOCK] = diagonal[:HALF]
        bottom[k, :, BLOCK:] = product[HALF:]
        bottom[k, :, :BLOCK] = diagonal[HALF:]
    for c, out in zip(SIDES, (low_c, high_c)):
        for a in STEPS:
            for b in STEPS:
                out[cell(a, b)] = bottom[links[link(a, b, c)]]


def first_a_kernel(links, low_links, high_links, top, from_low_b, from_high_b, low_a, high_a):
    for a, out in zip(SIDES, (low_a, high_a)):
        for c in STEPS:
            out[cell(-1, c)] = from_low_b[low_links[link(a, -1, c)]]
            out[cell(0, c)] = top[links[link(a, 0, c)]]
            out[cell(1, c)] = from_high_b[high_links[link(a, 1, c)]]


def first_c_kernel(
    links, low_links, high_links, top, from_low_b, from_high_b, from_low_a, from_high_a, low_c, high_c
):
    for c, out in zip(SIDES, (low_c, high_c)):
        for b in STEPS:
            out[cell(-1, b)] = from_low_a[cell(b, c)]
            out[cell(1, b)] = from_high_a[cell(b, c)]
        out[cell(0, -1)] = from_low_b[low_links[link(0, -1, c)]]
        out[cell(0, 0)] = top[links[link(0, 0, c)]]
        out[cell(0, 1)] = from_high_b[high_links[link(0, 1, c)]]


def second_a_kernel(links, bottom, from_low_c, from_high_c, low_a, high_a):
    for a, out in zip(SIDES, (low_a, high_a)):
        for b in STEPS:
            out[cell(b, -1)] = from_low_c[cell(a, b)]
            out[cell(b, 0)] = bottom[links[link(a, b, 0)]]
            out[cell(b, 1)] = from_high_c[cell(a, b)]


def second_b_kernel(
    links,
    low_links,
    high_links,
    bottom,
    from_low_c,
    from_high_c,
    from_low_a,
    from_high_a,
    low_b,
    high_b,
    sums,
):
    for b, out, there in zip(SIDES, (low_b, high_b), (high_links, low_links)):
        sums[...] = jnp.zeros_like(sums)
        for a, source in zip(SIDES, (from_low_a, from_high_a)):
            for c in STEPS:
                add_into(sums, there[link(-a, -b, -c)], source[cell(b, c)])
        for c, source in zip(SIDES, (from_low_c, from_high_c)):
            add_into(sums, there[link(0, -b, -c)], source[cell(0, b)])
        add_into(sums, there[link(0, -b, 0)], bottom[links[link(0, b, 0)]])
        out[...] = sums[...].astype(jnp.bfloat16)


def add_into(sums, slot, piece):
    sums[slot] = sums[slot] + piece.astype(jnp.float32)


def lower_kernel(links, bottom, from_low_c, from_high_c, from_low_a, from_high_a, lower):
    lower[...] = bottom[...].astype(jnp.float32)
    for c, source in zip(SIDES, (from_low_c, from_high_c)):
        add_into(lower, links[link(0, 0, -c)], source[cell(0, 0)])
    for a, source in zip(SIDES, (from_low_a, from_high_a)):
        for c in STEPS:
            add_into(lower, links[link(-a, 0, -c)], source[cell(0, c)])


def upper_kernel(
    links, low_links, high_links, top, from_low_b, from_high_b, from_low_a, from_high_a, upper
):
    upper[...] = top[...].astype(jnp.float32)
    for b, source, there in zip(SIDES, (from_low_b, from_high_b), (low_links, high_links)):
        add_into(upper, links[link(0, -b, 0)], source[there[link(0, b, 0)]])
    for a, source in zip(SIDES, (from_low_a, from_high_a)):
        for b in STEPS:
            add_into(upper, links[link(-a, -b, 0)], source[cell(b, 0)])


def tail_kernel(
    columns,
    layers,
    links,
    row_here,
    layer_here,
    upper,
    lower,
    first_low_c,
    first_high_c,
    second_low_b,
    second_high_b,
    schur,
    assembled,
    update,
    totals,
    scaled,
    counts,
):
    blocks = upper.shape[0]
    row, layer = row_here[0], layer_here[0]
    for k in range(blocks):
        counts[k] = 1
    for a in STEPS:
        for b in STEPS:
            for c in STEPS:
                if (a, b, c) == (0, 0, 0):
                    continue
                slot = links[link(a, b, c)]
                alive = (row + b >= 0) & (row + b < columns) & (layer + c >= 0) & (layer + c < layers)
                counts[slot] = counts[slot] + jnp.where(alive, 1, 0)
    totals[...] = upper[...]
    for c, source in zip(SIDES, (first_low_c, first_high_c)):
        for a in STEPS:
            for b in STEPS:
                add_into(totals, links[link(-a, -b, -c)], source[cell(a, b)])
    for k in range(blocks):
        rows = slice(k * BLOCK, (k + 1) * BLOCK)
        under = (
            lower[k]
            + second_low_b[k].astype(jnp.float32)
            + second_high_b[k].astype(jnp.float32)
        )
        whole = jnp.concatenate([totals[k], under], axis=0)
        coupling = whole[:, :BLOCK]
        summed = whole[:, BLOCK:]
        summed_high = summed.astype(jnp.bfloat16)
        summed_low = (summed - summed_high.astype(jnp.float32)).astype(jnp.bfloat16)
        coupling_high = coupling.astype(jnp.bfloat16)
        coupling_low = (coupling - coupling_high.astype(jnp.float32)).astype(jnp.bfloat16)
        assembled[rows, :] = summed_high
        mixed = jnp.dot(coupling_high, summed_high, preferred_element_type=jnp.float32)
        mixed += jnp.dot(coupling_high, summed_low, preferred_element_type=jnp.float32)
        mixed += jnp.dot(coupling_low, summed_high, preferred_element_type=jnp.float32)
        share = jnp.full((BLOCK, 1), counts[k], jnp.int32).astype(jnp.float32)
        scaled[rows, :] = (mixed / share).astype(jnp.bfloat16)
    for k in range(blocks):
        rows = slice(k * BLOCK, (k + 1) * BLOCK)
        update[rows, :] = jnp.dot(
            schur[rows, :], scaled[...], preferred_element_type=jnp.float32
        ).astype(jnp.bfloat16)


def call(kernel, outs, *operands, smem=1, scratch=(), room=4):
    specs = [pl.BlockSpec(memory_space=pltpu.SMEM)] * smem
    specs += [pl.BlockSpec(memory_space=pltpu.VMEM)] * (len(operands) - smem)
    return pl.pallas_call(
        kernel,
        out_shape=outs,
        in_specs=specs,
        out_specs=[pl.BlockSpec(memory_space=pltpu.VMEM) for _ in outs],
        scratch_shapes=list(scratch),
        compiler_params=pltpu.CompilerParams(vmem_limit_bytes=room * MIB),
    )(*operands)


def local(schur, block_map, vectors):
    matrix = schur[0, 0, 0]
    right_side = vectors[0, 0, 0]
    links = block_map[0, 0, 0]
    order, width = right_side.shape
    blocks = order // BLOCK
    full = BLOCK + width
    nine = [jax.ShapeDtypeStruct((9, HALF, full), jnp.bfloat16)] * 2
    eight = [jax.ShapeDtypeStruct((blocks, HALF, full), jnp.bfloat16)] * 2
    half = [jax.ShapeDtypeStruct((blocks, HALF, full), jnp.float32)]
    maps = [links] + [shift(links, "gy", s, False) for s in SIDES]
    top, bottom, *sent = call(head_kernel, eight + nine, links, matrix, right_side, room=4)
    second_c = [shift(v, "gz", s, False) for s, v in zip(SIDES, sent)]
    first_b = [shift(top, "gy", s, False) for s in SIDES]
    sent = call(second_a_kernel, nine, links, bottom, *second_c)
    second_a = [shift(v, "gx", s, True) for s, v in zip(SIDES, sent)]
    sent = call(
        second_b_kernel,
        eight,
        *maps,
        bottom,
        *second_c,
        *second_a,
        smem=3,
        scratch=[pltpu.VMEM((blocks, HALF, full), jnp.float32)],
    )
    second_b = [shift(v, "gy", s, False) for s, v in zip(SIDES, sent)]
    sent = call(first_a_kernel, nine, *maps, top, *first_b, smem=3)
    first_a = [shift(v, "gx", s, True) for s, v in zip(SIDES, sent)]
    (lower,) = call(lower_kernel, half, links, bottom, *second_c, *second_a)
    sent = call(first_c_kernel, nine, *maps, top, *first_b, *first_a, smem=3)
    first_c = [shift(v, "gz", s, False) for s, v in zip(SIDES, sent)]
    (upper,) = call(upper_kernel, half, *maps, top, *first_b, *first_a, smem=3)
    assembled, update = call(
        functools.partial(tail_kernel, lax.axis_size("gy"), lax.axis_size("gz")),
        [jax.ShapeDtypeStruct((order, width), jnp.bfloat16)] * 2,
        links,
        lax.axis_index("gy").astype(jnp.int32).reshape(1),
        lax.axis_index("gz").astype(jnp.int32).reshape(1),
        upper,
        lower,
        *first_c,
        *second_b,
        matrix,
        smem=3,
        scratch=[
            pltpu.VMEM((blocks, HALF, full), jnp.float32),
            pltpu.VMEM((order, width), jnp.bfloat16),
            pltpu.SMEM((blocks,), jnp.int32),
        ],
        room=12,
    )
    return (assembled[None, None, None], update[None, None, None])


def solution(mesh):
    placed = (
        P("gx", "gy", "gz", None, None),
        P("gx", "gy", "gz", None),
        P("gx", "gy", "gz", None, None),
    )

    return jax.shard_map(
        local,
        mesh=mesh,
        in_specs=placed,
        out_specs=(P("gx", "gy", "gz", None, None), P("gx", "gy", "gz", None, None)),
        check_vma=False,
    )
```

time: 121 us -> 144 us (1.19)
  the two profiles are of different devices: /device:TPU:40 before, /device:TPU:48 now
where the time goes in v2:
time: 144 us; the launch traced here: 143 us
  waiting for transfers between devices  67.4 us (47%)
  starting transfers between devices  54 us (38%)
  Pallas kernels  13.9 us (10%)
  local copies, waits for them, and re-layouts  7.38 us (5%)
    ppermute x14, waiting for transfers between devices, shift(): return lax.ppermute(value, axis, pairs)  67.4 us
    ppermute x14, starting transfers between devices, shift(): return lax.ppermute(value, axis, pairs)  54 us
    pallas_call x8, Pallas kernels, call(): pl.pallas_call(kernel, out_shape=outs, in_specs=specs, out_specs=[pl.Bloc...  13.9 us
    unnamed x30, local copies, waits for them, and re-layouts  7.38 us
  transfers between devices with their start and end apart: 14, of which 8 were waited for; matrix products, arithmetic and copies ran while one was open for 0% of the time, Pallas kernels for 5%

profile of v2, /device:TPU:48, one launch (start us, length us, event | category | flops | bytes accessed | tf_op | source)
XLA Modules:
  0.0 143.5 jit_solution(12275964516449794674)
XLA Ops:
  0.6 0.0 copy-start
  0.6 1.6 %copy-done = bf16[1,1,1,1024,1024]{4,3,2,1,0:T(8,128)(2,1)S(1)} copy-done((bf16[1,1,1,1024,1024]{4,3,2,1,0:T(8,128)(2,1)S(1)}, bf16[1,1,1,1024,1024]{4,3,2,1,0:T(8,128)(2,1)}, u32[]{:S(2)}) %copy-start) | copy-done | bytes 2097176
  2.2 1.2 copy-done.12
  3.5 0.7 copy-done.13
  4.1 1.9 %shard_map.50 = (bf16[8,64,640]{2,1,0:T(8,128)(2,1)S(1)}, bf16[8,64,640]{2,1,0:T(8,128)(2,1)S(1)}, bf16[9,64,640]{2,1,0:T(8,128)(2,1)S(1)}, bf16[9,64,640]{2,1,0:T(8,128)(2,1)S(1)}) custom-call(s32[26]{0:T(128)S(1)} %bitcast.10, bf16[1024,1024]{1,0:T(8,128)(2,1)S(1)} %bitcast.7, bf16[1024,512]{1,0:T(8,128)(2,1)S(1)} %bitcast.9), custom_call_target="tpu_custom_call" | custom-call | tf_op jit(solution)/shard_map/pallas_call | solution.py:196
  6.0 1.3 collective-permute-start.6
  7.3 3.1 %collective-permute-start.7 = (bf16[9,64,640]{2,1,0:T(8,128)(2,1)S(1)}, bf16[9,64,640]{2,1,0:T(8,128)(2,1)S(1)}, u32[]{:S(2)}, u32[]{:S(2)}) collective-permute-start(bf16[9,64,640]{2,1,0:T(8,128)(2,1)S(1)} %get-tuple-element.21), channel_id=1, source_target_pairs={{0,1},{1,2},{2,3},{3,4},{4,5},{5,6},{6,7},{7,8},{8,9},{9,10},{10,1... | collective-permute-start | bytes 2211848 | tf_op jit(solution)/shard_map/ppermute | solution.py:34
  10.4 1.3 collective-permute-start.3
  11.7 5.5 %collective-permute-start.2 = (bf16[8,64,640]{2,1,0:T(8,128)(2,1)S(1)}, bf16[8,64,640]{2,1,0:T(8,128)(2,1)S(1)}, u32[]{:S(2)}, u32[]{:S(2)}) collective-permute-start(bf16[8,64,640]{2,1,0:T(8,128)(2,1)S(1)} %get-tuple-element.16.top), channel_id=1, source_target_pairs={{16,0},{32,16},{48,32},{17,1},{33,17},{49,33},{18,2},{34,18},{50,3... | collective-permute-start | bytes 1966088 | tf_op jit(solution)/shard_map/ppermute | solution.py:34
  17.2 1.3 collective-permute-start.1
  18.5 13.3 %collective-permute-done.1.high_links = s32[26]{0:T(128)S(1)} collective-permute-done((s32[26]{0:T(128)S(1)}, s32[26]{0:T(128)S(1)}, u32[]{:S(2)}, u32[]{:S(2)}) %collective-permute-start.1) | collective-permute-done | bytes 136 | tf_op jit(solution)/shard_map/ppermute | solution.py:34
  31.8 4.4 %collective-permute-start = (s32[26]{0:T(128)S(1)}, s32[26]{0:T(128)S(1)}, u32[]{:S(2)}, u32[]{:S(2)}) collective-permute-start(s32[26]{0:T(128)S(1)} %bitcast.12), channel_id=1, source_target_pairs={{16,0},{32,16},{48,32},{17,1},{33,17},{49,33},{18,2},{34,18},{50,3... | collective-permute-start | bytes 320 | tf_op jit(solution)/shard_map/ppermute | solution.py:34
  36.2 10.1 %collective-permute-done.low_links = s32[26]{0:T(128)S(1)} collective-permute-done((s32[26]{0:T(128)S(1)}, s32[26]{0:T(128)S(1)}, u32[]{:S(2)}, u32[]{:S(2)}) %collective-permute-start) | collective-permute-done | bytes 136 | tf_op jit(solution)/shard_map/ppermute | solution.py:34
  46.2 0.0 collective-permute-done.3.from_high_b
  46.2 0.0 collective-permute-done.2.from_low_b
  46.2 0.7 shard_map.51
  46.9 16.1 %collective-permute-start.4 = (bf16[9,64,640]{2,1,0:T(8,128)(2,1)S(1)}, bf16[9,64,640]{2,1,0:T(8,128)(2,1)S(1)}, u32[]{:S(2)}, u32[]{:S(2)}) collective-permute-start(bf16[9,64,640]{2,1,0:T(8,128)(2,1)S(1)} %get-tuple-element.17), channel_id=1, source_target_pairs={{0,448},{64,0},{128,64},{192,128},{256,192},{320,256},{384,320},{4... | collective-permute-start | bytes 2211848 | tf_op jit(solution)/shard_map/ppermute | solution.py:34
  63.0 1.9 %collective-permute-start.5 = (bf16[9,64,640]{2,1,0:T(8,128)(2,1)S(1)}, bf16[9,64,640]{2,1,0:T(8,128)(2,1)S(1)}, u32[]{:S(2)}, u32[]{:S(2)}) collective-permute-start(bf16[9,64,640]{2,1,0:T(8,128)(2,1)S(1)} %get-tuple-element.18), channel_id=1, source_target_pairs={{0,64},{64,128},{128,192},{192,256},{256,320},{320,384},{384,448},... | collective-permute-start | bytes 2211848 | tf_op jit(solution)/shard_map/ppermute | solution.py:34
  64.9 0.0 collective-permute-done.6.from_low_c
  64.9 0.0 collective-permute-done.7.from_high_c
  64.9 0.7 shard_map.53
  65.6 5.1 %collective-permute-start.8 = (bf16[9,64,640]{2,1,0:T(8,128)(2,1)S(1)}, bf16[9,64,640]{2,1,0:T(8,128)(2,1)S(1)}, u32[]{:S(2)}, u32[]{:S(2)}) collective-permute-start(bf16[9,64,640]{2,1,0:T(8,128)(2,1)S(1)} %get-tuple-element.22), channel_id=1, source_target_pairs={{0,448},{64,0},{128,64},{192,128},{256,192},{320,256},{384,320},{4... | collective-permute-start | bytes 2211848 | tf_op jit(solution)/shard_map/ppermute | solution.py:34
  70.7 1.9 %collective-permute-start.9 = (bf16[9,64,640]{2,1,0:T(8,128)(2,1)S(1)}, bf16[9,64,640]{2,1,0:T(8,128)(2,1)S(1)}, u32[]{:S(2)}, u32[]{:S(2)}) collective-permute-start(bf16[9,64,640]{2,1,0:T(8,128)(2,1)S(1)} %get-tuple-element.23), channel_id=1, source_target_pairs={{0,64},{64,128},{128,192},{192,256},{256,320},{320,384},{384,448},... | collective-permute-start | bytes 2211848 | tf_op jit(solution)/shard_map/ppermute | solution.py:34
  72.7 7.2 %collective-permute-done.4.from_low_a = bf16[9,64,640]{2,1,0:T(8,128)(2,1)S(1)} collective-permute-done((bf16[9,64,640]{2,1,0:T(8,128)(2,1)S(1)}, bf16[9,64,640]{2,1,0:T(8,128)(2,1)S(1)}, u32[]{:S(2)}, u32[]{:S(2)}) %collective-permute-start.4) | collective-permute-done | bytes 737312 | tf_op jit(solution)/shard_map/ppermute | solution.py:34
  79.9 5.6 %collective-permute-done.5.from_high_a = bf16[9,64,640]{2,1,0:T(8,128)(2,1)S(1)} collective-permute-done((bf16[9,64,640]{2,1,0:T(8,128)(2,1)S(1)}, bf16[9,64,640]{2,1,0:T(8,128)(2,1)S(1)}, u32[]{:S(2)}, u32[]{:S(2)}) %collective-permute-start.5) | collective-permute-done | bytes 737312 | tf_op jit(solution)/shard_map/ppermute | solution.py:34
  85.5 0.0 copy-done.2
  85.5 1.8 %shard_map.55 = (bf16[9,64,640]{2,1,0:T(8,128)(2,1)}, bf16[9,64,640]{2,1,0:T(8,128)(2,1)}) custom-call(s32[26]{0:T(128)S(1)} %bitcast.15, s32[26]{0:T(128)S(1)} %collective-permute-done.low_links, s32[26]{0:T(128)S(1)} %collective-permute-done.1.high_links, bf16[8,64,640]{2,1,0:T(8,128)(2,1)S(1)} %get-tuple-element.16.top, ...), custom_call_target="tpu_custom_call" | custom-call | tf_op jit(solution)/shard_map/pallas_call | solution.py:196
  87.3 0.0 copy-done.8
  87.3 1.3 collective-permute-start.10
  88.6 0.0 copy-start.14
  88.6 3.9 %collective-permute-start.11 = (bf16[9,64,640]{2,1,0:T(8,128)(2,1)}, bf16[9,64,640]{2,1,0:T(8,128)(2,1)}, u32[]{:S(2)}, u32[]{:S(2)}) collective-permute-start(bf16[9,64,640]{2,1,0:T(8,128)(2,1)} %get-tuple-element.25), channel_id=1, source_target_pairs={{0,1},{1,2},{2,3},{3,4},{4,5},{5,6},{6,7},{7,8},{8,9},{9,10},{10,1... | collective-permute-start | bytes 2211848 | tf_op jit(solution)/shard_map/ppermute | solution.py:34
  92.5 1.4 collective-permute-done.8.from_low_a
  93.9 5.3 %collective-permute-done.9.from_high_a = bf16[9,64,640]{2,1,0:T(8,128)(2,1)S(1)} collective-permute-done((bf16[9,64,640]{2,1,0:T(8,128)(2,1)S(1)}, bf16[9,64,640]{2,1,0:T(8,128)(2,1)S(1)}, u32[]{:S(2)}, u32[]{:S(2)}) %collective-permute-start.9) | collective-permute-done | bytes 737312 | tf_op jit(solution)/shard_map/ppermute | solution.py:34
  99.2 2.1 %shard_map.56 = (bf16[8,64,640]{2,1,0:T(8,128)(2,1)}, bf16[8,64,640]{2,1,0:T(8,128)(2,1)}) custom-call(s32[26]{0:T(128)S(1)} %bitcast.16, s32[26]{0:T(128)S(1)} %collective-permute-done.low_links, s32[26]{0:T(128)S(1)} %collective-permute-done.1.high_links, bf16[8,64,640]{2,1,0:T(8,128)(2,1)S(1)} %get-tuple-element.19.bottom, ...), custom_call_target="tpu_custom_call" | custom-call | tf_op jit(solution)/shard_map/pallas_call | solution.py:196
  101.3 5.6 %collective-permute-start.12 = (bf16[8,64,640]{2,1,0:T(8,128)(2,1)}, bf16[8,64,640]{2,1,0:T(8,128)(2,1)}, u32[]{:S(2)}, u32[]{:S(2)}) collective-permute-start(bf16[8,64,640]{2,1,0:T(8,128)(2,1)} %get-tuple-element.26), channel_id=1, source_target_pairs={{16,0},{32,16},{48,32},{17,1},{33,17},{49,33},{18,2},{34,18},{50,3... | collective-permute-start | bytes 1966088 | tf_op jit(solution)/shard_map/ppermute | solution.py:34
  106.9 1.3 collective-permute-start.13
  108.2 1.1 copy-done.3
  109.3 1.1 copy-done.9
  110.4 1.1 copy-done.11
  111.5 0.8 shard_map.52.upper
  112.3 0.3 copy-done.5
  112.6 0.2 copy-done.7
  112.9 0.7 shard_map.54.lower
  113.6 17.4 %collective-permute-done.12.second_low_b = bf16[8,64,640]{2,1,0:T(8,128)(2,1)} collective-permute-done((bf16[8,64,640]{2,1,0:T(8,128)(2,1)}, bf16[8,64,640]{2,1,0:T(8,128)(2,1)}, u32[]{:S(2)}, u32[]{:S(2)}) %collective-permute-start.12) | collective-permute-done | bytes 655392 | tf_op jit(solution)/shard_map/ppermute | solution.py:34
  131.1 7.1 %collective-permute-done.13.second_high_b = bf16[8,64,640]{2,1,0:T(8,128)(2,1)} collective-permute-done((bf16[8,64,640]{2,1,0:T(8,128)(2,1)}, bf16[8,64,640]{2,1,0:T(8,128)(2,1)}, u32[]{:S(2)}, u32[]{:S(2)}) %collective-permute-start.13) | collective-permute-done | bytes 655392 | tf_op jit(solution)/shard_map/ppermute | solution.py:34
  138.2 0.0 collective-permute-done.10.first_low_c
  138.2 0.0 collective-permute-done.11.first_high_c
  138.2 5.3 %shard_map.57 = (bf16[1024,512]{1,0:T(8,128)(2,1)}, bf16[1024,512]{1,0:T(8,128)(2,1)}) custom-call(s32[26]{0:T(128)S(1)} %bitcast.19, s32[1]{0:T(128)} %bitcast.1.row_here, s32[1]{0:T(128)} %bitcast.2.layer_here, f32[8,64,640]{2,1,0:T(8,128)S(1)} %shard_map.52.upper, f32[8,64,640]{2,1,0:T(8,128)S(1)} %shard_map.54.lower, ...), custom_call_target="tpu_custom_call" | custom-call | tf_op jit(solution)/shard_map/pallas_call | solution.py:196
  (18 shorter events, 0.0 us)
Async XLA Ops:
  0.6 1.6 %copy-start = (bf16[1,1,1,1024,1024]{4,3,2,1,0:T(8,128)(2,1)S(1)}, bf16[1,1,1,1024,1024]{4,3,2,1,0:T(8,128)(2,1)}, u32[]{:S(2)}) copy-start(bf16[1,1,1,1024,1024]{4,3,2,1,0:T(8,128)(2,1)} %param.3) | copy-start | bytes 6291460
  2.2 1.2 copy-start.12
  3.4 0.7 copy-start.13
  6.0 58.9 %collective-permute-start.6 = (bf16[9,64,640]{2,1,0:T(8,128)(2,1)S(1)}, bf16[9,64,640]{2,1,0:T(8,128)(2,1)S(1)}, u32[]{:S(2)}, u32[]{:S(2)}) collective-permute-start(bf16[9,64,640]{2,1,0:T(8,128)(2,1)S(1)} %get-tuple-element.20), channel_id=1, source_target_pairs={{1,0},{2,1},{3,2},{4,3},{5,4},{6,5},{7,6},{8,7},{9,8},{10,9},{11,1... | collective-permute-start | bytes 2211848 | tf_op jit(solution)/shard_map/ppermute | solution.py:34
  7.3 57.6 %collective-permute-start.7 = (bf16[9,64,640]{2,1,0:T(8,128)(2,1)S(1)}, bf16[9,64,640]{2,1,0:T(8,128)(2,1)S(1)}, u32[]{:S(2)}, u32[]{:S(2)}) collective-permute-start(bf16[9,64,640]{2,1,0:T(8,128)(2,1)S(1)} %get-tuple-element.21), channel_id=1, source_target_pairs={{0,1},{1,2},{2,3},{3,4},{4,5},{5,6},{6,7},{7,8},{8,9},{9,10},{10,1... | collective-permute-start | bytes 2211848 | tf_op jit(solution)/shard_map/ppermute | solution.py:34
  10.4 35.8 %collective-permute-start.3 = (bf16[8,64,640]{2,1,0:T(8,128)(2,1)S(1)}, bf16[8,64,640]{2,1,0:T(8,128)(2,1)S(1)}, u32[]{:S(2)}, u32[]{:S(2)}) collective-permute-start(bf16[8,64,640]{2,1,0:T(8,128)(2,1)S(1)} %get-tuple-element.16.top), channel_id=1, source_target_pairs={{0,16},{16,32},{32,48},{1,17},{17,33},{33,49},{2,18},{18,34},{34,5... | collective-permute-start | bytes 1966088 | tf_op jit(solution)/shard_map/ppermute | solution.py:34
  11.7 34.5 %collective-permute-start.2 = (bf16[8,64,640]{2,1,0:T(8,128)(2,1)S(1)}, bf16[8,64,640]{2,1,0:T(8,128)(2,1)S(1)}, u32[]{:S(2)}, u32[]{:S(2)}) collective-permute-start(bf16[8,64,640]{2,1,0:T(8,128)(2,1)S(1)} %get-tuple-element.16.top), channel_id=1, source_target_pairs={{16,0},{32,16},{48,32},{17,1},{33,17},{49,33},{18,2},{34,18},{50,3... | collective-permute-start | bytes 1966088 | tf_op jit(solution)/shard_map/ppermute | solution.py:34
  17.2 14.6 %collective-permute-start.1 = (s32[26]{0:T(128)S(1)}, s32[26]{0:T(128)S(1)}, u32[]{:S(2)}, u32[]{:S(2)}) collective-permute-start(s32[26]{0:T(128)S(1)} %bitcast.11), channel_id=1, source_target_pairs={{0,16},{16,32},{32,48},{1,17},{17,33},{33,49},{2,18},{18,34},{34,5... | collective-permute-start | bytes 320 | tf_op jit(solution)/shard_map/ppermute | solution.py:34
  31.8 14.5 %collective-permute-start = (s32[26]{0:T(128)S(1)}, s32[26]{0:T(128)S(1)}, u32[]{:S(2)}, u32[]{:S(2)}) collective-permute-start(s32[26]{0:T(128)S(1)} %bitcast.12), channel_id=1, source_target_pairs={{16,0},{32,16},{48,32},{17,1},{33,17},{49,33},{18,2},{34,18},{50,3... | collective-permute-start | bytes 320 | tf_op jit(solution)/shard_map/ppermute | solution.py:34
  46.2 39.2 %copy-start.2 = (bf16[8,64,640]{2,1,0:T(8,128)(2,1)}, bf16[8,64,640]{2,1,0:T(8,128)(2,1)S(1)}, u32[]{:S(2)}) copy-start(bf16[8,64,640]{2,1,0:T(8,128)(2,1)S(1)} %collective-permute-done.2.from_low_b) | copy-start | bytes 1966084
  46.9 32.9 %collective-permute-start.4 = (bf16[9,64,640]{2,1,0:T(8,128)(2,1)S(1)}, bf16[9,64,640]{2,1,0:T(8,128)(2,1)S(1)}, u32[]{:S(2)}, u32[]{:S(2)}) collective-permute-start(bf16[9,64,640]{2,1,0:T(8,128)(2,1)S(1)} %get-tuple-element.17), channel_id=1, source_target_pairs={{0,448},{64,0},{128,64},{192,128},{256,192},{320,256},{384,320},{4... | collective-permute-start | bytes 2211848 | tf_op jit(solution)/shard_map/ppermute | solution.py:34
  63.0 22.5 %collective-permute-start.5 = (bf16[9,64,640]{2,1,0:T(8,128)(2,1)S(1)}, bf16[9,64,640]{2,1,0:T(8,128)(2,1)S(1)}, u32[]{:S(2)}, u32[]{:S(2)}) collective-permute-start(bf16[9,64,640]{2,1,0:T(8,128)(2,1)S(1)} %get-tuple-element.18), channel_id=1, source_target_pairs={{0,64},{64,128},{128,192},{192,256},{256,320},{320,384},{384,448},... | collective-permute-start | bytes 2211848 | tf_op jit(solution)/shard_map/ppermute | solution.py:34
  65.6 28.3 %collective-permute-start.8 = (bf16[9,64,640]{2,1,0:T(8,128)(2,1)S(1)}, bf16[9,64,640]{2,1,0:T(8,128)(2,1)S(1)}, u32[]{:S(2)}, u32[]{:S(2)}) collective-permute-start(bf16[9,64,640]{2,1,0:T(8,128)(2,1)S(1)} %get-tuple-element.22), channel_id=1, source_target_pairs={{0,448},{64,0},{128,64},{192,128},{256,192},{320,256},{384,320},{4... | collective-permute-start | bytes 2211848 | tf_op jit(solution)/shard_map/ppermute | solution.py:34
  70.7 28.4 %collective-permute-start.9 = (bf16[9,64,640]{2,1,0:T(8,128)(2,1)S(1)}, bf16[9,64,640]{2,1,0:T(8,128)(2,1)S(1)}, u32[]{:S(2)}, u32[]{:S(2)}) collective-permute-start(bf16[9,64,640]{2,1,0:T(8,128)(2,1)S(1)} %get-tuple-element.23), channel_id=1, source_target_pairs={{0,64},{64,128},{128,192},{192,256},{256,320},{320,384},{384,448},... | collective-permute-start | bytes 2211848 | tf_op jit(solution)/shard_map/ppermute | solution.py:34
  79.8 7.4 %copy-start.8 = (bf16[9,64,640]{2,1,0:T(8,128)(2,1)}, bf16[9,64,640]{2,1,0:T(8,128)(2,1)S(1)}, u32[]{:S(2)}) copy-start(bf16[9,64,640]{2,1,0:T(8,128)(2,1)S(1)} %collective-permute-done.4.from_low_a) | copy-start | bytes 2211844
  85.5 1.8 %copy-start.10 = (bf16[9,64,640]{2,1,0:T(8,128)(2,1)}, bf16[9,64,640]{2,1,0:T(8,128)(2,1)S(1)}, u32[]{:S(2)}) copy-start(bf16[9,64,640]{2,1,0:T(8,128)(2,1)S(1)} %collective-permute-done.5.from_high_a) | copy-start | bytes 2211844
  87.3 50.9 %collective-permute-start.10 = (bf16[9,64,640]{2,1,0:T(8,128)(2,1)}, bf16[9,64,640]{2,1,0:T(8,128)(2,1)}, u32[]{:S(2)}, u32[]{:S(2)}) collective-permute-start(bf16[9,64,640]{2,1,0:T(8,128)(2,1)} %get-tuple-element.24), channel_id=1, source_target_pairs={{1,0},{2,1},{3,2},{4,3},{5,4},{6,5},{7,6},{8,7},{9,8},{10,9},{11,1... | collective-permute-start | bytes 2211848 | tf_op jit(solution)/shard_map/ppermute | solution.py:34
  88.6 19.6 %copy-start.14 = (s32[1,1,1,26]{3,2,1,0:T(1,128)S(1)}, s32[1,1,1,26]{3,2,1,0:T(1,128)}, u32[]{:S(2)}) copy-start(s32[1,1,1,26]{3,2,1,0:T(1,128)} %param.4) | copy-start | bytes 316
  88.6 49.6 %collective-permute-start.11 = (bf16[9,64,640]{2,1,0:T(8,128)(2,1)}, bf16[9,64,640]{2,1,0:T(8,128)(2,1)}, u32[]{:S(2)}, u32[]{:S(2)}) collective-permute-start(bf16[9,64,640]{2,1,0:T(8,128)(2,1)} %get-tuple-element.25), channel_id=1, source_target_pairs={{0,1},{1,2},{2,3},{3,4},{4,5},{5,6},{6,7},{7,8},{8,9},{9,10},{10,1... | collective-permute-start | bytes 2211848 | tf_op jit(solution)/shard_map/ppermute | solution.py:34
  93.9 7.4 %copy-start.4 = (bf16[9,64,640]{2,1,0:T(8,128)(2,1)}, bf16[9,64,640]{2,1,0:T(8,128)(2,1)S(1)}, u32[]{:S(2)}) copy-start(bf16[9,64,640]{2,1,0:T(8,128)(2,1)S(1)} %collective-permute-done.8.from_low_a) | copy-start | bytes 2211844
  99.2 2.1 %copy-start.6 = (bf16[9,64,640]{2,1,0:T(8,128)(2,1)}, bf16[9,64,640]{2,1,0:T(8,128)(2,1)S(1)}, u32[]{:S(2)}) copy-start(bf16[9,64,640]{2,1,0:T(8,128)(2,1)S(1)} %collective-permute-done.9.from_high_a) | copy-start | bytes 2211844
  101.3 29.8 %collective-permute-start.12 = (bf16[8,64,640]{2,1,0:T(8,128)(2,1)}, bf16[8,64,640]{2,1,0:T(8,128)(2,1)}, u32[]{:S(2)}, u32[]{:S(2)}) collective-permute-start(bf16[8,64,640]{2,1,0:T(8,128)(2,1)} %get-tuple-element.26), channel_id=1, source_target_pairs={{16,0},{32,16},{48,32},{17,1},{33,17},{49,33},{18,2},{34,18},{50,3... | collective-permute-start | bytes 1966088 | tf_op jit(solution)/shard_map/ppermute | solution.py:34
  106.9 31.3 %collective-permute-start.13 = (bf16[8,64,640]{2,1,0:T(8,128)(2,1)}, bf16[8,64,640]{2,1,0:T(8,128)(2,1)}, u32[]{:S(2)}, u32[]{:S(2)}) collective-permute-start(bf16[8,64,640]{2,1,0:T(8,128)(2,1)} %get-tuple-element.27), channel_id=1, source_target_pairs={{0,16},{16,32},{32,48},{1,17},{17,33},{33,49},{2,18},{18,34},{34,5... | collective-permute-start | bytes 1966088 | tf_op jit(solution)/shard_map/ppermute | solution.py:34
  108.2 1.1 copy-start.3
  109.3 1.1 copy-start.9
  110.4 1.1 copy-start.11
  111.5 1.1 copy-start.5
  111.5 1.3 copy-start.7
  112.9 25.3 %copy-start.1 = (bf16[1,1,1,1024,1024]{4,3,2,1,0:T(8,128)(2,1)S(1)}, bf16[1,1,1,1024,1024]{4,3,2,1,0:T(8,128)(2,1)}, u32[]{:S(2)}) copy-start(bf16[1,1,1,1024,1024]{4,3,2,1,0:T(8,128)(2,1)} %param.3) | copy-start | bytes 6291460

commit v3 on v2

--- a/solution.py
+++ b/solution.py
@@ -34,7 +34,7 @@
     return lax.ppermute(value, axis, pairs)
 
 
-def head_kernel(links, matrix, right_side, top, bottom, low_c, high_c):
+def head_kernel(links, row_here, layer_here, matrix, right_side, top, bottom, low_a, high_a):
     for k in range(top.shape[0]):
         rows = slice(k * BLOCK, (k + 1) * BLOCK)
         product = jnp.dot(
@@ -45,10 +45,10 @@
         top[k, :, :BLOCK] = diagonal[:HALF]
         bottom[k, :, BLOCK:] = product[HALF:]
         bottom[k, :, :BLOCK] = diagonal[HALF:]
-    for c, out in zip(SIDES, (low_c, high_c)):
-        for a in STEPS:
-            for b in STEPS:
-                out[cell(a, b)] = bottom[links[link(a, b, c)]]
+    for a, out in zip(SIDES, (low_a, high_a)):
+        for b in STEPS:
+            for c in STEPS:
+                out[cell(b, c)] = bottom[links[link(a, b, c)]]
 
 
 def first_a_kernel(links, low_links, high_links, top, from_low_b, from_high_b, low_a, high_a):
@@ -71,49 +71,37 @@
         out[cell(0, 1)] = from_high_b[high_links[link(0, 1, c)]]
 
 
-def second_a_kernel(links, bottom, from_low_c, from_high_c, low_a, high_a):
-    for a, out in zip(SIDES, (low_a, high_a)):
-        for b in STEPS:
-            out[cell(b, -1)] = from_low_c[cell(a, b)]
-            out[cell(b, 0)] = bottom[links[link(a, b, 0)]]
-            out[cell(b, 1)] = from_high_c[cell(a, b)]
+def second_c_kernel(links, bottom, from_low_a, from_high_a, low_c, high_c):
+    for c, out in zip(SIDES, (low_c, high_c)):
+        for b in STEPS:
+            out[cell(-1, b)] = from_low_a[cell(b, c)]
+            out[cell(0, b)] = bottom[links[link(0, b, c)]]
+            out[cell(1, b)] = from_high_a[cell(b, c)]
 
 
 def second_b_kernel(
-    links,
-    low_links,
-    high_links,
-    bottom,
-    from_low_c,
-    from_high_c,
-    from_low_a,
-    from_high_a,
-    low_b,
-    high_b,
-    sums,
-):
-    for b, out, there in zip(SIDES, (low_b, high_b), (high_links, low_links)):
-        sums[...] = jnp.zeros_like(sums)
-        for a, source in zip(SIDES, (from_low_a, from_high_a)):
-            for c in STEPS:
-                add_into(sums, there[link(-a, -b, -c)], source[cell(b, c)])
-        for c, source in zip(SIDES, (from_low_c, from_high_c)):
-            add_into(sums, there[link(0, -b, -c)], source[cell(0, b)])
-        add_into(sums, there[link(0, -b, 0)], bottom[links[link(0, b, 0)]])
-        out[...] = sums[...].astype(jnp.bfloat16)
+    links, bottom, from_low_a, from_high_a, from_low_c, from_high_c, low_b, high_b
+):
+    for b, out in zip(SIDES, (low_b, high_b)):
+        for a in STEPS:
+            out[cell(a, -1)] = from_low_c[cell(a, b)]
+            out[cell(a, 1)] = from_high_c[cell(a, b)]
+        out[cell(-1, 0)] = from_low_a[cell(b, 0)]
+        out[cell(0, 0)] = bottom[links[link(0, b, 0)]]
+        out[cell(1, 0)] = from_high_a[cell(b, 0)]
 
 
 def add_into(sums, slot, piece):
     sums[slot] = sums[slot] + piece.astype(jnp.float32)
 
 
-def lower_kernel(links, bottom, from_low_c, from_high_c, from_low_a, from_high_a, lower):
+def lower_kernel(links, bottom, from_low_a, from_high_a, from_low_c, from_high_c, lower):
     lower[...] = bottom[...].astype(jnp.float32)
+    for a, source in zip(SIDES, (from_low_a, from_high_a)):
+        add_into(lower, links[link(-a, 0, 0)], source[cell(0, 0)])
     for c, source in zip(SIDES, (from_low_c, from_high_c)):
-        add_into(lower, links[link(0, 0, -c)], source[cell(0, 0)])
-    for a, source in zip(SIDES, (from_low_a, from_high_a)):
-        for c in STEPS:
-            add_into(lower, links[link(-a, 0, -c)], source[cell(0, c)])
+        for a in STEPS:
+            add_into(lower, links[link(-a, 0, -c)], source[cell(a, 0)])
 
 
 def upper_kernel(
@@ -142,7 +130,8 @@
     schur,
     assembled,
     update,
-    totals,
+    over,
+    under,
     scaled,
     counts,
 ):
@@ -158,19 +147,19 @@
                 slot = links[link(a, b, c)]
                 alive = (row + b >= 0) & (row + b < columns) & (layer + c >= 0) & (layer + c < layers)
                 counts[slot] = counts[slot] + jnp.where(alive, 1, 0)
-    totals[...] = upper[...]
+    over[...] = upper[...]
+    under[...] = lower[...]
     for c, source in zip(SIDES, (first_low_c, first_high_c)):
         for a in STEPS:
             for b in STEPS:
-                add_into(totals, links[link(-a, -b, -c)], source[cell(a, b)])
+                add_into(over, links[link(-a, -b, -c)], source[cell(a, b)])
+    for b, source in zip(SIDES, (second_low_b, second_high_b)):
+        for a in STEPS:
+            for c in STEPS:
+                add_into(under, links[link(-a, -b, -c)], source[cell(a, c)])
     for k in range(blocks):
         rows = slice(k * BLOCK, (k + 1) * BLOCK)
-        under = (
-            lower[k]
-            + second_low_b[k].astype(jnp.float32)
-            + second_high_b[k].astype(jnp.float32)
-        )
-        whole = jnp.concatenate([totals[k], under], axis=0)
+        whole = jnp.concatenate([over[k], under[k]], axis=0)
         coupling = whole[:, :BLOCK]
         summed = whole[:, BLOCK:]
         summed_high = summed.astype(jnp.bfloat16)
@@ -213,35 +202,25 @@
     nine = [jax.ShapeDtypeStruct((9, HALF, full), jnp.bfloat16)] * 2
     eight = [jax.ShapeDtypeStruct((blocks, HALF, full), jnp.bfloat16)] * 2
     half = [jax.ShapeDtypeStruct((blocks, HALF, full), jnp.float32)]
+    here = [links] + [lax.axis_index(axis).astype(jnp.int32).reshape(1) for axis in ("gy", "gz")]
     maps = [links] + [shift(links, "gy", s, False) for s in SIDES]
-    top, bottom, *sent = call(head_kernel, eight + nine, links, matrix, right_side, room=4)
+    top, bottom, *sent = call(head_kernel, eight + nine, *here, matrix, right_side, smem=3)
+    second_a = [shift(v, "gx", s, True) for s, v in zip(SIDES, sent)]
+    first_b = [shift(top, "gy", s, False) for s in SIDES]
+    sent = call(second_c_kernel, nine, links, bottom, *second_a)
     second_c = [shift(v, "gz", s, False) for s, v in zip(SIDES, sent)]
-    first_b = [shift(top, "gy", s, False) for s in SIDES]
-    sent = call(second_a_kernel, nine, links, bottom, *second_c)
-    second_a = [shift(v, "gx", s, True) for s, v in zip(SIDES, sent)]
-    sent = call(
-        second_b_kernel,
-        eight,
-        *maps,
-        bottom,
-        *second_c,
-        *second_a,
-        smem=3,
-        scratch=[pltpu.VMEM((blocks, HALF, full), jnp.float32)],
-    )
+    sent = call(second_b_kernel, nine, links, bottom, *second_a, *second_c)
     second_b = [shift(v, "gy", s, False) for s, v in zip(SIDES, sent)]
     sent = call(first_a_kernel, nine, *maps, top, *first_b, smem=3)
     first_a = [shift(v, "gx", s, True) for s, v in zip(SIDES, sent)]
-    (lower,) = call(lower_kernel, half, links, bottom, *second_c, *second_a)
+    (lower,) = call(lower_kernel, half, links, bottom, *second_a, *second_c)
     sent = call(first_c_kernel, nine, *maps, top, *first_b, *first_a, smem=3)
     first_c = [shift(v, "gz", s, False) for s, v in zip(SIDES, sent)]
     (upper,) = call(upper_kernel, half, *maps, top, *first_b, *first_a, smem=3)
     assembled, update = call(
         functools.partial(tail_kernel, lax.axis_size("gy"), lax.axis_size("gz")),
         [jax.ShapeDtypeStruct((order, width), jnp.bfloat16)] * 2,
-        links,
-        lax.axis_index("gy").astype(jnp.int32).reshape(1),
-        lax.axis_index("gz").astype(jnp.int32).reshape(1),
+        *here,
         upper,
         lower,
         *first_c,
@@ -250,6 +229,7 @@
         smem=3,
         scratch=[
             pltpu.VMEM((blocks, HALF, full), jnp.float32),
+            pltpu.VMEM((blocks, HALF, full), jnp.float32),
             pltpu.VMEM((order, width), jnp.bfloat16),
             pltpu.SMEM((blocks,), jnp.int32),
         ],

time: 144 us -> 137 us (0.951)
  the two profiles are of different devices: /device:TPU:48 before, /device:TPU:39 now
where the time goes in v3:
time: 137 us; the launch traced here: 136 us
  waiting for transfers between devices  61.7 us (45%)
  starting transfers between devices  59.8 us (44%)
  Pallas kernels  10.4 us (8%)
  local copies, waits for them, and re-layouts  3.48 us (3%)
    ppermute x14, waiting for transfers between devices, shift(): return lax.ppermute(value, axis, pairs)  61.7 us
    ppermute x14, starting transfers between devices, shift(): return lax.ppermute(value, axis, pairs)  59.8 us
    pallas_call x8, Pallas kernels, call(): pl.pallas_call(kernel, out_shape=outs, in_specs=specs, out_specs=[pl.Bloc...  10.4 us
    unnamed x10, local copies, waits for them, and re-layouts  3.48 us
  transfers between devices with their start and end apart: 14, of which 6 were waited for; matrix products, arithmetic and copies ran while one was open for 0% of the time, Pallas kernels for 3%

profile of v3, /device:TPU:39, one launch (start us, length us, event | category | flops | bytes accessed | tf_op | source)
XLA Modules:
  0.0 136.3 jit_solution(15032734256537924515)
XLA Ops:
  0.6 0.0 copy-start
  0.6 1.6 %copy-done = bf16[1,1,1,1024,1024]{4,3,2,1,0:T(8,128)(2,1)S(1)} copy-done((bf16[1,1,1,1024,1024]{4,3,2,1,0:T(8,128)(2,1)S(1)}, bf16[1,1,1,1024,1024]{4,3,2,1,0:T(8,128)(2,1)}, u32[]{:S(2)}) %copy-start) | copy-done | bytes 2097176
  2.2 0.0 copy-start.2
  2.2 1.2 copy-done.2
  3.5 0.0 copy-start.3
  3.5 0.7 copy-done.3
  4.1 1.9 %shard_map.50 = (bf16[8,64,640]{2,1,0:T(8,128)(2,1)S(1)}, bf16[8,64,640]{2,1,0:T(8,128)(2,1)S(1)}, bf16[9,64,640]{2,1,0:T(8,128)(2,1)S(1)}, bf16[9,64,640]{2,1,0:T(8,128)(2,1)S(1)}) custom-call(s32[26]{0:T(128)S(1)} %bitcast.10, s32[1]{0:T(128)} %bitcast.1.row_here, s32[1]{0:T(128)} %bitcast.2.layer_here, bf16[1024,1024]{1,0:T(8,128)(2,1)S(1)} %bitcast.7, ...), custom_call_target="tpu_custom_call" | custom-call | tf_op jit(solution)/shard_map/pallas_call | solution.py:185
  6.0 10.7 %collective-permute-start.6 = (bf16[9,64,640]{2,1,0:T(8,128)(2,1)S(1)}, bf16[9,64,640]{2,1,0:T(8,128)(2,1)S(1)}, u32[]{:S(2)}, u32[]{:S(2)}) collective-permute-start(bf16[9,64,640]{2,1,0:T(8,128)(2,1)S(1)} %get-tuple-element.20), channel_id=1, source_target_pairs={{0,448},{64,0},{128,64},{192,128},{256,192},{320,256},{384,320},{4... | collective-permute-start | bytes 2211848 | tf_op jit(solution)/shard_map/ppermute | solution.py:34
  16.7 1.9 %collective-permute-start.7 = (bf16[9,64,640]{2,1,0:T(8,128)(2,1)S(1)}, bf16[9,64,640]{2,1,0:T(8,128)(2,1)S(1)}, u32[]{:S(2)}, u32[]{:S(2)}) collective-permute-start(bf16[9,64,640]{2,1,0:T(8,128)(2,1)S(1)} %get-tuple-element.21), channel_id=1, source_target_pairs={{0,64},{64,128},{128,192},{192,256},{256,320},{320,384},{384,448},... | collective-permute-start | bytes 2211848 | tf_op jit(solution)/shard_map/ppermute | solution.py:34
  18.6 2.4 %collective-permute-start.3 = (bf16[8,64,640]{2,1,0:T(8,128)(2,1)S(1)}, bf16[8,64,640]{2,1,0:T(8,128)(2,1)S(1)}, u32[]{:S(2)}, u32[]{:S(2)}) collective-permute-start(bf16[8,64,640]{2,1,0:T(8,128)(2,1)S(1)} %get-tuple-element.16.top), channel_id=1, source_target_pairs={{0,16},{16,32},{32,48},{1,17},{17,33},{33,49},{2,18},{18,34},{34,5... | collective-permute-start | bytes 1966088 | tf_op jit(solution)/shard_map/ppermute | solution.py:34
  21.1 5.0 %collective-permute-start.2 = (bf16[8,64,640]{2,1,0:T(8,128)(2,1)S(1)}, bf16[8,64,640]{2,1,0:T(8,128)(2,1)S(1)}, u32[]{:S(2)}, u32[]{:S(2)}) collective-permute-start(bf16[8,64,640]{2,1,0:T(8,128)(2,1)S(1)} %get-tuple-element.16.top), channel_id=1, source_target_pairs={{16,0},{32,16},{48,32},{17,1},{33,17},{49,33},{18,2},{34,18},{50,3... | collective-permute-start | bytes 1966088 | tf_op jit(solution)/shard_map/ppermute | solution.py:34
  26.1 1.9 %collective-permute-start.1 = (s32[26]{0:T(128)S(1)}, s32[26]{0:T(128)S(1)}, u32[]{:S(2)}, u32[]{:S(2)}) collective-permute-start(s32[26]{0:T(128)S(1)} %bitcast.11), channel_id=1, source_target_pairs={{0,16},{16,32},{32,48},{1,17},{17,33},{33,49},{2,18},{18,34},{34,5... | collective-permute-start | bytes 320 | tf_op jit(solution)/shard_map/ppermute | solution.py:34
  28.0 10.1 %collective-permute-done.1.high_links = s32[26]{0:T(128)S(1)} collective-permute-done((s32[26]{0:T(128)S(1)}, s32[26]{0:T(128)S(1)}, u32[]{:S(2)}, u32[]{:S(2)}) %collective-permute-start.1) | collective-permute-done | bytes 136 | tf_op jit(solution)/shard_map/ppermute | solution.py:34
  38.1 1.9 %collective-permute-start = (s32[26]{0:T(128)S(1)}, s32[26]{0:T(128)S(1)}, u32[]{:S(2)}, u32[]{:S(2)}) collective-permute-start(s32[26]{0:T(128)S(1)} %bitcast.12), channel_id=1, source_target_pairs={{16,0},{32,16},{48,32},{17,1},{33,17},{49,33},{18,2},{34,18},{50,3... | collective-permute-start | bytes 320 | tf_op jit(solution)/shard_map/ppermute | solution.py:34
  40.0 14.5 %collective-permute-done.low_links = s32[26]{0:T(128)S(1)} collective-permute-done((s32[26]{0:T(128)S(1)}, s32[26]{0:T(128)S(1)}, u32[]{:S(2)}, u32[]{:S(2)}) %collective-permute-start) | collective-permute-done | bytes 136 | tf_op jit(solution)/shard_map/ppermute | solution.py:34
  54.5 0.0 collective-permute-done.3.from_high_b
  54.5 0.0 collective-permute-done.2.from_low_b
  54.5 0.7 shard_map.51
  55.2 4.6 %collective-permute-start.4 = (bf16[9,64,640]{2,1,0:T(8,128)(2,1)S(1)}, bf16[9,64,640]{2,1,0:T(8,128)(2,1)S(1)}, u32[]{:S(2)}, u32[]{:S(2)}) collective-permute-start(bf16[9,64,640]{2,1,0:T(8,128)(2,1)S(1)} %get-tuple-element.17), channel_id=1, source_target_pairs={{0,448},{64,0},{128,64},{192,128},{256,192},{320,256},{384,320},{4... | collective-permute-start | bytes 2211848 | tf_op jit(solution)/shard_map/ppermute | solution.py:34
  59.8 1.9 %collective-permute-start.5 = (bf16[9,64,640]{2,1,0:T(8,128)(2,1)S(1)}, bf16[9,64,640]{2,1,0:T(8,128)(2,1)S(1)}, u32[]{:S(2)}, u32[]{:S(2)}) collective-permute-start(bf16[9,64,640]{2,1,0:T(8,128)(2,1)S(1)} %get-tuple-element.18), channel_id=1, source_target_pairs={{0,64},{64,128},{128,192},{192,256},{256,320},{320,384},{384,448},... | collective-permute-start | bytes 2211848 | tf_op jit(solution)/shard_map/ppermute | solution.py:34
  61.7 0.0 collective-permute-done.6.from_low_a
  61.7 0.0 collective-permute-done.7.from_high_a
  61.7 0.7 shard_map.53
  62.4 7.9 %collective-permute-start.8 = (bf16[9,64,640]{2,1,0:T(8,128)(2,1)S(1)}, bf16[9,64,640]{2,1,0:T(8,128)(2,1)S(1)}, u32[]{:S(2)}, u32[]{:S(2)}) collective-permute-start(bf16[9,64,640]{2,1,0:T(8,128)(2,1)S(1)} %get-tuple-element.22), channel_id=1, source_target_pairs={{1,0},{2,1},{3,2},{4,3},{5,4},{6,5},{7,6},{8,7},{9,8},{10,9},{11,1... | collective-permute-start | bytes 2211848 | tf_op jit(solution)/shard_map/ppermute | solution.py:34
  70.3 1.9 %collective-permute-start.9 = (bf16[9,64,640]{2,1,0:T(8,128)(2,1)S(1)}, bf16[9,64,640]{2,1,0:T(8,128)(2,1)S(1)}, u32[]{:S(2)}, u32[]{:S(2)}) collective-permute-start(bf16[9,64,640]{2,1,0:T(8,128)(2,1)S(1)} %get-tuple-element.23), channel_id=1, source_target_pairs={{0,1},{1,2},{2,3},{3,4},{4,5},{5,6},{6,7},{7,8},{8,9},{9,10},{10,1... | collective-permute-start | bytes 2211848 | tf_op jit(solution)/shard_map/ppermute | solution.py:34
  72.2 0.0 collective-permute-done.4.from_low_a
  72.3 2.6 %collective-permute-done.5.from_high_a = bf16[9,64,640]{2,1,0:T(8,128)(2,1)S(1)} collective-permute-done((bf16[9,64,640]{2,1,0:T(8,128)(2,1)S(1)}, bf16[9,64,640]{2,1,0:T(8,128)(2,1)S(1)}, u32[]{:S(2)}, u32[]{:S(2)}) %collective-permute-start.5) | collective-permute-done | bytes 737312 | tf_op jit(solution)/shard_map/ppermute | solution.py:34
  74.9 0.7 shard_map.55
  75.6 8.8 %collective-permute-start.10 = (bf16[9,64,640]{2,1,0:T(8,128)(2,1)S(1)}, bf16[9,64,640]{2,1,0:T(8,128)(2,1)S(1)}, u32[]{:S(2)}, u32[]{:S(2)}) collective-permute-start(bf16[9,64,640]{2,1,0:T(8,128)(2,1)S(1)} %get-tuple-element.24), channel_id=1, source_target_pairs={{1,0},{2,1},{3,2},{4,3},{5,4},{6,5},{7,6},{8,7},{9,8},{10,9},{11,1... | collective-permute-start | bytes 2211848 | tf_op jit(solution)/shard_map/ppermute | solution.py:34
  84.4 4.1 %collective-permute-start.11 = (bf16[9,64,640]{2,1,0:T(8,128)(2,1)S(1)}, bf16[9,64,640]{2,1,0:T(8,128)(2,1)S(1)}, u32[]{:S(2)}, u32[]{:S(2)}) collective-permute-start(bf16[9,64,640]{2,1,0:T(8,128)(2,1)S(1)} %get-tuple-element.25), channel_id=1, source_target_pairs={{0,1},{1,2},{2,3},{3,4},{4,5},{5,6},{6,7},{7,8},{8,9},{9,10},{10,1... | collective-permute-start | bytes 2211848 | tf_op jit(solution)/shard_map/ppermute | solution.py:34
  88.5 0.0 collective-permute-done.8.from_low_c
  88.5 0.0 collective-permute-done.9.from_high_c
  88.5 0.7 shard_map.56
  89.2 4.9 %collective-permute-start.12 = (bf16[9,64,640]{2,1,0:T(8,128)(2,1)S(1)}, bf16[9,64,640]{2,1,0:T(8,128)(2,1)S(1)}, u32[]{:S(2)}, u32[]{:S(2)}) collective-permute-start(bf16[9,64,640]{2,1,0:T(8,128)(2,1)S(1)} %get-tuple-element.26), channel_id=1, source_target_pairs={{16,0},{32,16},{48,32},{17,1},{33,17},{49,33},{18,2},{34,18},{50,3... | collective-permute-start | bytes 2211848 | tf_op jit(solution)/shard_map/ppermute | solution.py:34
  94.0 1.9 %collective-permute-start.13 = (bf16[9,64,640]{2,1,0:T(8,128)(2,1)S(1)}, bf16[9,64,640]{2,1,0:T(8,128)(2,1)S(1)}, u32[]{:S(2)}, u32[]{:S(2)}) collective-permute-start(bf16[9,64,640]{2,1,0:T(8,128)(2,1)S(1)} %get-tuple-element.27), channel_id=1, source_target_pairs={{0,16},{16,32},{32,48},{1,17},{17,33},{33,49},{2,18},{18,34},{34,5... | collective-permute-start | bytes 2211848 | tf_op jit(solution)/shard_map/ppermute | solution.py:34
  96.0 0.8 shard_map.52.upper
  96.7 0.0 copy-start.1
  96.8 0.0 copy-start.4
  96.8 0.7 shard_map.54.lower
  97.5 2.0 %collective-permute-done.10.first_low_c = bf16[9,64,640]{2,1,0:T(8,128)(2,1)S(1)} collective-permute-done((bf16[9,64,640]{2,1,0:T(8,128)(2,1)S(1)}, bf16[9,64,640]{2,1,0:T(8,128)(2,1)S(1)}, u32[]{:S(2)}, u32[]{:S(2)}) %collective-permute-start.10) | collective-permute-done | bytes 737312 | tf_op jit(solution)/shard_map/ppermute | solution.py:34
  99.5 0.0 collective-permute-done.11.first_high_c
  99.5 25.8 %collective-permute-done.12.second_low_b = bf16[9,64,640]{2,1,0:T(8,128)(2,1)S(1)} collective-permute-done((bf16[9,64,640]{2,1,0:T(8,128)(2,1)S(1)}, bf16[9,64,640]{2,1,0:T(8,128)(2,1)S(1)}, u32[]{:S(2)}, u32[]{:S(2)}) %collective-permute-start.12) | collective-permute-done | bytes 737312 | tf_op jit(solution)/shard_map/ppermute | solution.py:34
  125.3 6.6 %collective-permute-done.13.second_high_b = bf16[9,64,640]{2,1,0:T(8,128)(2,1)S(1)} collective-permute-done((bf16[9,64,640]{2,1,0:T(8,128)(2,1)S(1)}, bf16[9,64,640]{2,1,0:T(8,128)(2,1)S(1)}, u32[]{:S(2)}, u32[]{:S(2)}) %collective-permute-start.13) | collective-permute-done | bytes 737312 | tf_op jit(solution)/shard_map/ppermute | solution.py:34
  131.9 0.0 copy-done.1
  131.9 0.0 copy-done.4
  131.9 4.4 %shard_map.57 = (bf16[1024,512]{1,0:T(8,128)(2,1)}, bf16[1024,512]{1,0:T(8,128)(2,1)}) custom-call(s32[26]{0:T(128)S(1)} %bitcast.19, s32[1]{0:T(128)} %bitcast.1.row_here, s32[1]{0:T(128)} %bitcast.2.layer_here, f32[8,64,640]{2,1,0:T(8,128)S(1)} %shard_map.52.upper, f32[8,64,640]{2,1,0:T(8,128)S(1)} %shard_map.54.lower, ...), custom_call_target="tpu_custom_call" | custom-call | tf_op jit(solution)/shard_map/pallas_call | solution.py:185
Async XLA Ops:
  0.6 1.6 %copy-start = (bf16[1,1,1,1024,1024]{4,3,2,1,0:T(8,128)(2,1)S(1)}, bf16[1,1,1,1024,1024]{4,3,2,1,0:T(8,128)(2,1)}, u32[]{:S(2)}) copy-start(bf16[1,1,1,1024,1024]{4,3,2,1,0:T(8,128)(2,1)} %param.3) | copy-start | bytes 6291460
  2.2 1.2 copy-start.2
  3.5 0.7 copy-start.3
  6.0 55.7 %collective-permute-start.6 = (bf16[9,64,640]{2,1,0:T(8,128)(2,1)S(1)}, bf16[9,64,640]{2,1,0:T(8,128)(2,1)S(1)}, u32[]{:S(2)}, u32[]{:S(2)}) collective-permute-start(bf16[9,64,640]{2,1,0:T(8,128)(2,1)S(1)} %get-tuple-element.20), channel_id=1, source_target_pairs={{0,448},{64,0},{128,64},{192,128},{256,192},{320,256},{384,320},{4... | collective-permute-start | bytes 2211848 | tf_op jit(solution)/shard_map/ppermute | solution.py:34
  16.7 45.0 %collective-permute-start.7 = (bf16[9,64,640]{2,1,0:T(8,128)(2,1)S(1)}, bf16[9,64,640]{2,1,0:T(8,128)(2,1)S(1)}, u32[]{:S(2)}, u32[]{:S(2)}) collective-permute-start(bf16[9,64,640]{2,1,0:T(8,128)(2,1)S(1)} %get-tuple-element.21), channel_id=1, source_target_pairs={{0,64},{64,128},{128,192},{192,256},{256,320},{320,384},{384,448},... | collective-permute-start | bytes 2211848 | tf_op jit(solution)/shard_map/ppermute | solution.py:34
  18.6 35.9 %collective-permute-start.3 = (bf16[8,64,640]{2,1,0:T(8,128)(2,1)S(1)}, bf16[8,64,640]{2,1,0:T(8,128)(2,1)S(1)}, u32[]{:S(2)}, u32[]{:S(2)}) collective-permute-start(bf16[8,64,640]{2,1,0:T(8,128)(2,1)S(1)} %get-tuple-element.16.top), channel_id=1, source_target_pairs={{0,16},{16,32},{32,48},{1,17},{17,33},{33,49},{2,18},{18,34},{34,5... | collective-permute-start | bytes 1966088 | tf_op jit(solution)/shard_map/ppermute | solution.py:34
  21.1 33.4 %collective-permute-start.2 = (bf16[8,64,640]{2,1,0:T(8,128)(2,1)S(1)}, bf16[8,64,640]{2,1,0:T(8,128)(2,1)S(1)}, u32[]{:S(2)}, u32[]{:S(2)}) collective-permute-start(bf16[8,64,640]{2,1,0:T(8,128)(2,1)S(1)} %get-tuple-element.16.top), channel_id=1, source_target_pairs={{16,0},{32,16},{48,32},{17,1},{33,17},{49,33},{18,2},{34,18},{50,3... | collective-permute-start | bytes 1966088 | tf_op jit(solution)/shard_map/ppermute | solution.py:34
  26.1 12.0 %collective-permute-start.1 = (s32[26]{0:T(128)S(1)}, s32[26]{0:T(128)S(1)}, u32[]{:S(2)}, u32[]{:S(2)}) collective-permute-start(s32[26]{0:T(128)S(1)} %bitcast.11), channel_id=1, source_target_pairs={{0,16},{16,32},{32,48},{1,17},{17,33},{33,49},{2,18},{18,34},{34,5... | collective-permute-start | bytes 320 | tf_op jit(solution)/shard_map/ppermute | solution.py:34
  38.1 16.4 %collective-permute-start = (s32[26]{0:T(128)S(1)}, s32[26]{0:T(128)S(1)}, u32[]{:S(2)}, u32[]{:S(2)}) collective-permute-start(s32[26]{0:T(128)S(1)} %bitcast.12), channel_id=1, source_target_pairs={{16,0},{32,16},{48,32},{17,1},{33,17},{49,33},{18,2},{34,18},{50,3... | collective-permute-start | bytes 320 | tf_op jit(solution)/shard_map/ppermute | solution.py:34
  55.2 17.1 %collective-permute-start.4 = (bf16[9,64,640]{2,1,0:T(8,128)(2,1)S(1)}, bf16[9,64,640]{2,1,0:T(8,128)(2,1)S(1)}, u32[]{:S(2)}, u32[]{:S(2)}) collective-permute-start(bf16[9,64,640]{2,1,0:T(8,128)(2,1)S(1)} %get-tuple-element.17), channel_id=1, source_target_pairs={{0,448},{64,0},{128,64},{192,128},{256,192},{320,256},{384,320},{4... | collective-permute-start | bytes 2211848 | tf_op jit(solution)/shard_map/ppermute | solution.py:34
  59.8 15.1 %collective-permute-start.5 = (bf16[9,64,640]{2,1,0:T(8,128)(2,1)S(1)}, bf16[9,64,640]{2,1,0:T(8,128)(2,1)S(1)}, u32[]{:S(2)}, u32[]{:S(2)}) collective-permute-start(bf16[9,64,640]{2,1,0:T(8,128)(2,1)S(1)} %get-tuple-element.18), channel_id=1, source_target_pairs={{0,64},{64,128},{128,192},{192,256},{256,320},{320,384},{384,448},... | collective-permute-start | bytes 2211848 | tf_op jit(solution)/shard_map/ppermute | solution.py:34
  62.4 26.1 %collective-permute-start.8 = (bf16[9,64,640]{2,1,0:T(8,128)(2,1)S(1)}, bf16[9,64,640]{2,1,0:T(8,128)(2,1)S(1)}, u32[]{:S(2)}, u32[]{:S(2)}) collective-permute-start(bf16[9,64,640]{2,1,0:T(8,128)(2,1)S(1)} %get-tuple-element.22), channel_id=1, source_target_pairs={{1,0},{2,1},{3,2},{4,3},{5,4},{6,5},{7,6},{8,7},{9,8},{10,9},{11,1... | collective-permute-start | bytes 2211848 | tf_op jit(solution)/shard_map/ppermute | solution.py:34
  70.3 18.2 %collective-permute-start.9 = (bf16[9,64,640]{2,1,0:T(8,128)(2,1)S(1)}, bf16[9,64,640]{2,1,0:T(8,128)(2,1)S(1)}, u32[]{:S(2)}, u32[]{:S(2)}) collective-permute-start(bf16[9,64,640]{2,1,0:T(8,128)(2,1)S(1)} %get-tuple-element.23), channel_id=1, source_target_pairs={{0,1},{1,2},{2,3},{3,4},{4,5},{5,6},{6,7},{7,8},{8,9},{9,10},{10,1... | collective-permute-start | bytes 2211848 | tf_op jit(solution)/shard_map/ppermute | solution.py:34
  75.6 23.9 %collective-permute-start.10 = (bf16[9,64,640]{2,1,0:T(8,128)(2,1)S(1)}, bf16[9,64,640]{2,1,0:T(8,128)(2,1)S(1)}, u32[]{:S(2)}, u32[]{:S(2)}) collective-permute-start(bf16[9,64,640]{2,1,0:T(8,128)(2,1)S(1)} %get-tuple-element.24), channel_id=1, source_target_pairs={{1,0},{2,1},{3,2},{4,3},{5,4},{6,5},{7,6},{8,7},{9,8},{10,9},{11,1... | collective-permute-start | bytes 2211848 | tf_op jit(solution)/shard_map/ppermute | solution.py:34
  84.4 15.1 %collective-permute-start.11 = (bf16[9,64,640]{2,1,0:T(8,128)(2,1)S(1)}, bf16[9,64,640]{2,1,0:T(8,128)(2,1)S(1)}, u32[]{:S(2)}, u32[]{:S(2)}) collective-permute-start(bf16[9,64,640]{2,1,0:T(8,128)(2,1)S(1)} %get-tuple-element.25), channel_id=1, source_target_pairs={{0,1},{1,2},{2,3},{3,4},{4,5},{5,6},{6,7},{7,8},{8,9},{9,10},{10,1... | collective-permute-start | bytes 2211848 | tf_op jit(solution)/shard_map/ppermute | solution.py:34
  89.2 36.2 %collective-permute-start.12 = (bf16[9,64,640]{2,1,0:T(8,128)(2,1)S(1)}, bf16[9,64,640]{2,1,0:T(8,128)(2,1)S(1)}, u32[]{:S(2)}, u32[]{:S(2)}) collective-permute-start(bf16[9,64,640]{2,1,0:T(8,128)(2,1)S(1)} %get-tuple-element.26), channel_id=1, source_target_pairs={{16,0},{32,16},{48,32},{17,1},{33,17},{49,33},{18,2},{34,18},{50,3... | collective-permute-start | bytes 2211848 | tf_op jit(solution)/shard_map/ppermute | solution.py:34
  94.0 37.9 %collective-permute-start.13 = (bf16[9,64,640]{2,1,0:T(8,128)(2,1)S(1)}, bf16[9,64,640]{2,1,0:T(8,128)(2,1)S(1)}, u32[]{:S(2)}, u32[]{:S(2)}) collective-permute-start(bf16[9,64,640]{2,1,0:T(8,128)(2,1)S(1)} %get-tuple-element.27), channel_id=1, source_target_pairs={{0,16},{16,32},{32,48},{1,17},{17,33},{33,49},{2,18},{18,34},{34,5... | collective-permute-start | bytes 2211848 | tf_op jit(solution)/shard_map/ppermute | solution.py:34
  96.7 35.2 %copy-start.1 = (bf16[1,1,1,1024,1024]{4,3,2,1,0:T(8,128)(2,1)S(1)}, bf16[1,1,1,1024,1024]{4,3,2,1,0:T(8,128)(2,1)}, u32[]{:S(2)}) copy-start(bf16[1,1,1,1024,1024]{4,3,2,1,0:T(8,128)(2,1)} %param.3) | copy-start | bytes 6291460
  96.8 35.2 %copy-start.4 = (s32[1,1,1,26]{3,2,1,0:T(1,128)S(1)}, s32[1,1,1,26]{3,2,1,0:T(1,128)}, u32[]{:S(2)}) copy-start(s32[1,1,1,26]{3,2,1,0:T(1,128)} %param.4) | copy-start | bytes 316

commit v4 on v3

--- a/solution.py
+++ b/solution.py
@@ -71,37 +71,41 @@
         out[cell(0, 1)] = from_high_b[high_links[link(0, 1, c)]]
 
 
-def second_c_kernel(links, bottom, from_low_a, from_high_a, low_c, high_c):
+def second_b_kernel(links, bottom, from_low_a, from_high_a, low_b, high_b):
+    for b, out in zip(SIDES, (low_b, high_b)):
+        for c in STEPS:
+            out[cell(-1, c)] = from_low_a[cell(b, c)]
+            out[cell(0, c)] = bottom[links[link(0, b, c)]]
+            out[cell(1, c)] = from_high_a[cell(b, c)]
+
+
+def second_c_kernel(
+    links, bottom, from_low_a, from_high_a, from_low_b, from_high_b, low_c, high_c
+):
     for c, out in zip(SIDES, (low_c, high_c)):
-        for b in STEPS:
-            out[cell(-1, b)] = from_low_a[cell(b, c)]
-            out[cell(0, b)] = bottom[links[link(0, b, c)]]
-            out[cell(1, b)] = from_high_a[cell(b, c)]
-
-
-def second_b_kernel(
-    links, bottom, from_low_a, from_high_a, from_low_c, from_high_c, low_b, high_b
-):
-    for b, out in zip(SIDES, (low_b, high_b)):
         for a in STEPS:
-            out[cell(a, -1)] = from_low_c[cell(a, b)]
-            out[cell(a, 1)] = from_high_c[cell(a, b)]
-        out[cell(-1, 0)] = from_low_a[cell(b, 0)]
-        out[cell(0, 0)] = bottom[links[link(0, b, 0)]]
-        out[cell(1, 0)] = from_high_a[cell(b, 0)]
+            out[cell(a, -1)] = from_low_b[cell(a, c)]
+            out[cell(a, 1)] = from_high_b[cell(a, c)]
+        out[cell(-1, 0)] = from_low_a[cell(0, c)]
+        out[cell(0, 0)] = bottom[links[link(0, 0, c)]]
+        out[cell(1, 0)] = from_high_a[cell(0, c)]
 
 
 def add_into(sums, slot, piece):
     sums[slot] = sums[slot] + piece.astype(jnp.float32)
 
 
-def lower_kernel(links, bottom, from_low_a, from_high_a, from_low_c, from_high_c, lower):
+def seed_kernel(links, bottom, from_low_a, from_high_a, lower):
     lower[...] = bottom[...].astype(jnp.float32)
     for a, source in zip(SIDES, (from_low_a, from_high_a)):
         add_into(lower, links[link(-a, 0, 0)], source[cell(0, 0)])
-    for c, source in zip(SIDES, (from_low_c, from_high_c)):
+
+
+def lower_kernel(links, seed, from_low_b, from_high_b, lower):
+    lower[...] = seed[...]
+    for b, source in zip(SIDES, (from_low_b, from_high_b)):
         for a in STEPS:
-            add_into(lower, links[link(-a, 0, -c)], source[cell(a, 0)])
+            add_into(lower, links[link(-a, -b, 0)], source[cell(a, 0)])
 
 
 def upper_kernel(
@@ -125,8 +129,8 @@
     lower,
     first_low_c,
     first_high_c,
-    second_low_b,
-    second_high_b,
+    second_low_c,
+    second_high_c,
     schur,
     assembled,
     update,
@@ -149,14 +153,14 @@
                 counts[slot] = counts[slot] + jnp.where(alive, 1, 0)
     over[...] = upper[...]
     under[...] = lower[...]
-    for c, source in zip(SIDES, (first_low_c, first_high_c)):
-        for a in STEPS:
-            for b in STEPS:
-                add_into(over, links[link(-a, -b, -c)], source[cell(a, b)])
-    for b, source in zip(SIDES, (second_low_b, second_high_b)):
-        for a in STEPS:
-            for c in STEPS:
-                add_into(under, links[link(-a, -b, -c)], source[cell(a, c)])
+    for sums, low, high in (
+        (over, first_low_c, first_high_c),
+        (under, second_low_c, second_high_c),
+    ):
+        for c, source in zip(SIDES, (low, high)):
+            for a in STEPS:
+                for b in STEPS:
+                    add_into(sums, links[link(-a, -b, -c)], source[cell(a, b)])
     for k in range(blocks):
         rows = slice(k * BLOCK, (k + 1) * BLOCK)
         whole = jnp.concatenate([over[k], under[k]], axis=0)
@@ -205,18 +209,19 @@
     here = [links] + [lax.axis_index(axis).astype(jnp.int32).reshape(1) for axis in ("gy", "gz")]
     maps = [links] + [shift(links, "gy", s, False) for s in SIDES]
     top, bottom, *sent = call(head_kernel, eight + nine, *here, matrix, right_side, smem=3)
+    first_b = [shift(top, "gy", s, False) for s in SIDES]
     second_a = [shift(v, "gx", s, True) for s, v in zip(SIDES, sent)]
-    first_b = [shift(top, "gy", s, False) for s in SIDES]
-    sent = call(second_c_kernel, nine, links, bottom, *second_a)
-    second_c = [shift(v, "gz", s, False) for s, v in zip(SIDES, sent)]
-    sent = call(second_b_kernel, nine, links, bottom, *second_a, *second_c)
+    sent = call(second_b_kernel, nine, links, bottom, *second_a)
     second_b = [shift(v, "gy", s, False) for s, v in zip(SIDES, sent)]
+    (seed,) = call(seed_kernel, half, links, bottom, *second_a)
     sent = call(first_a_kernel, nine, *maps, top, *first_b, smem=3)
     first_a = [shift(v, "gx", s, True) for s, v in zip(SIDES, sent)]
-    (lower,) = call(lower_kernel, half, links, bottom, *second_a, *second_c)
     sent = call(first_c_kernel, nine, *maps, top, *first_b, *first_a, smem=3)
     first_c = [shift(v, "gz", s, False) for s, v in zip(SIDES, sent)]
+    sent = call(second_c_kernel, nine, links, bottom, *second_a, *second_b)
+    second_c = [shift(v, "gz", s, False) for s, v in zip(SIDES, sent)]
     (upper,) = call(upper_kernel, half, *maps, top, *first_b, *first_a, smem=3)
+    (lower,) = call(lower_kernel, half, links, seed, *second_b)
     assembled, update = call(
         functools.partial(tail_kernel, lax.axis_size("gy"), lax.axis_size("gz")),
         [jax.ShapeDtypeStruct((order, width), jnp.bfloat16)] * 2,
@@ -224,7 +229,7 @@
         upper,
         lower,
         *first_c,
-        *second_b,
+        *second_c,
         matrix,
         smem=3,
         scratch=[

time: 137 us -> 129 us (0.942)
  the two profiles are of different devices: /device:TPU:39 before, /device:TPU:40 now
where the time goes in v4:
time: 129 us
  waiting for transfers between devices  65.2 us (51%)
  starting transfers between devices  48.1 us (37%)
  Pallas kernels  11.1 us (9%)
  local copies, waits for them, and re-layouts  3.48 us (3%)
    ppermute x14, waiting for transfers between devices, shift(): return lax.ppermute(value, axis, pairs)  65.2 us
    ppermute x14, starting transfers between devices, shift(): return lax.ppermute(value, axis, pairs)  48.1 us
    pallas_call x9, Pallas kernels, call(): pl.pallas_call(kernel, out_shape=outs, in_specs=specs, out_specs=[pl.Bloc...  11.1 us
    unnamed x10, local copies, waits for them, and re-layouts  3.48 us
  transfers between devices with their start and end apart: 14, of which 9 were waited for; matrix products, arithmetic and copies ran while one was open for 0% of the time, Pallas kernels for 4%

profile of v4, /device:TPU:40, one launch (start us, length us, event | category | flops | bytes accessed | tf_op | source)
XLA Modules:
  0.0 128.7 jit_solution(14303705524229472189)
XLA Ops:
  0.6 0.0 copy-start
  0.6 1.6 %copy-done = bf16[1,1,1,1024,1024]{4,3,2,1,0:T(8,128)(2,1)S(1)} copy-done((bf16[1,1,1,1024,1024]{4,3,2,1,0:T(8,128)(2,1)S(1)}, bf16[1,1,1,1024,1024]{4,3,2,1,0:T(8,128)(2,1)}, u32[]{:S(2)}) %copy-start) | copy-done | bytes 2097176
  2.2 0.0 copy-start.2
  2.2 1.2 copy-done.2
  3.5 0.0 copy-start.3
  3.5 0.7 copy-done.3
  4.1 1.9 %shard_map.50 = (bf16[8,64,640]{2,1,0:T(8,128)(2,1)S(1)}, bf16[8,64,640]{2,1,0:T(8,128)(2,1)S(1)}, bf16[9,64,640]{2,1,0:T(8,128)(2,1)S(1)}, bf16[9,64,640]{2,1,0:T(8,128)(2,1)S(1)}) custom-call(s32[26]{0:T(128)S(1)} %bitcast.10, s32[1]{0:T(128)} %bitcast.1.row_here, s32[1]{0:T(128)} %bitcast.2.layer_here, bf16[1024,1024]{1,0:T(8,128)(2,1)S(1)} %bitcast.7, ...), custom_call_target="tpu_custom_call" | custom-call | tf_op jit(solution)/shard_map/pallas_call | solution.py:189
  6.0 10.9 %collective-permute-start.6 = (bf16[9,64,640]{2,1,0:T(8,128)(2,1)S(1)}, bf16[9,64,640]{2,1,0:T(8,128)(2,1)S(1)}, u32[]{:S(2)}, u32[]{:S(2)}) collective-permute-start(bf16[9,64,640]{2,1,0:T(8,128)(2,1)S(1)} %get-tuple-element.20), channel_id=1, source_target_pairs={{0,448},{64,0},{128,64},{192,128},{256,192},{320,256},{384,320},{4... | collective-permute-start | bytes 2211848 | tf_op jit(solution)/shard_map/ppermute | solution.py:34
  17.0 1.9 %collective-permute-start.7 = (bf16[9,64,640]{2,1,0:T(8,128)(2,1)S(1)}, bf16[9,64,640]{2,1,0:T(8,128)(2,1)S(1)}, u32[]{:S(2)}, u32[]{:S(2)}) collective-permute-start(bf16[9,64,640]{2,1,0:T(8,128)(2,1)S(1)} %get-tuple-element.21), channel_id=1, source_target_pairs={{0,64},{64,128},{128,192},{192,256},{256,320},{320,384},{384,448},... | collective-permute-start | bytes 2211848 | tf_op jit(solution)/shard_map/ppermute | solution.py:34
  18.9 2.7 %collective-permute-start.3 = (bf16[8,64,640]{2,1,0:T(8,128)(2,1)S(1)}, bf16[8,64,640]{2,1,0:T(8,128)(2,1)S(1)}, u32[]{:S(2)}, u32[]{:S(2)}) collective-permute-start(bf16[8,64,640]{2,1,0:T(8,128)(2,1)S(1)} %get-tuple-element.16.top), channel_id=1, source_target_pairs={{0,16},{16,32},{32,48},{1,17},{17,33},{33,49},{2,18},{18,34},{34,5... | collective-permute-start | bytes 1966088 | tf_op jit(solution)/shard_map/ppermute | solution.py:34
  21.6 5.2 %collective-permute-start.2 = (bf16[8,64,640]{2,1,0:T(8,128)(2,1)S(1)}, bf16[8,64,640]{2,1,0:T(8,128)(2,1)S(1)}, u32[]{:S(2)}, u32[]{:S(2)}) collective-permute-start(bf16[8,64,640]{2,1,0:T(8,128)(2,1)S(1)} %get-tuple-element.16.top), channel_id=1, source_target_pairs={{16,0},{32,16},{48,32},{17,1},{33,17},{49,33},{18,2},{34,18},{50,3... | collective-permute-start | bytes 1966088 | tf_op jit(solution)/shard_map/ppermute | solution.py:34
  26.9 1.9 %collective-permute-start.1 = (s32[26]{0:T(128)S(1)}, s32[26]{0:T(128)S(1)}, u32[]{:S(2)}, u32[]{:S(2)}) collective-permute-start(s32[26]{0:T(128)S(1)} %bitcast.11), channel_id=1, source_target_pairs={{0,16},{16,32},{32,48},{1,17},{17,33},{33,49},{2,18},{18,34},{34,5... | collective-permute-start | bytes 320 | tf_op jit(solution)/shard_map/ppermute | solution.py:34
  28.8 23.2 %collective-permute-done.1.high_links = s32[26]{0:T(128)S(1)} collective-permute-done((s32[26]{0:T(128)S(1)}, s32[26]{0:T(128)S(1)}, u32[]{:S(2)}, u32[]{:S(2)}) %collective-permute-start.1) | collective-permute-done | bytes 136 | tf_op jit(solution)/shard_map/ppermute | solution.py:34
  52.0 3.2 %collective-permute-start = (s32[26]{0:T(128)S(1)}, s32[26]{0:T(128)S(1)}, u32[]{:S(2)}, u32[]{:S(2)}) collective-permute-start(s32[26]{0:T(128)S(1)} %bitcast.12), channel_id=1, source_target_pairs={{16,0},{32,16},{48,32},{17,1},{33,17},{49,33},{18,2},{34,18},{50,3... | collective-permute-start | bytes 320 | tf_op jit(solution)/shard_map/ppermute | solution.py:34
  55.2 3.2 %collective-permute-done.low_links = s32[26]{0:T(128)S(1)} collective-permute-done((s32[26]{0:T(128)S(1)}, s32[26]{0:T(128)S(1)}, u32[]{:S(2)}, u32[]{:S(2)}) %collective-permute-start) | collective-permute-done | bytes 136 | tf_op jit(solution)/shard_map/ppermute | solution.py:34
  58.3 0.0 collective-permute-done.3.from_high_b
  58.3 0.0 collective-permute-done.2.from_low_b
  58.4 0.7 shard_map.51
  59.0 4.9 %collective-permute-start.4 = (bf16[9,64,640]{2,1,0:T(8,128)(2,1)S(1)}, bf16[9,64,640]{2,1,0:T(8,128)(2,1)S(1)}, u32[]{:S(2)}, u32[]{:S(2)}) collective-permute-start(bf16[9,64,640]{2,1,0:T(8,128)(2,1)S(1)} %get-tuple-element.17), channel_id=1, source_target_pairs={{0,448},{64,0},{128,64},{192,128},{256,192},{320,256},{384,320},{4... | collective-permute-start | bytes 2211848 | tf_op jit(solution)/shard_map/ppermute | solution.py:34
  63.9 1.9 %collective-permute-start.5 = (bf16[9,64,640]{2,1,0:T(8,128)(2,1)S(1)}, bf16[9,64,640]{2,1,0:T(8,128)(2,1)S(1)}, u32[]{:S(2)}, u32[]{:S(2)}) collective-permute-start(bf16[9,64,640]{2,1,0:T(8,128)(2,1)S(1)} %get-tuple-element.18), channel_id=1, source_target_pairs={{0,64},{64,128},{128,192},{192,256},{256,320},{320,384},{384,448},... | collective-permute-start | bytes 2211848 | tf_op jit(solution)/shard_map/ppermute | solution.py:34
  65.8 0.0 collective-permute-done.6.from_low_a
  65.8 0.0 collective-permute-done.7.from_high_a
  65.8 0.7 shard_map.54
  66.5 4.4 %collective-permute-start.8 = (bf16[9,64,640]{2,1,0:T(8,128)(2,1)S(1)}, bf16[9,64,640]{2,1,0:T(8,128)(2,1)S(1)}, u32[]{:S(2)}, u32[]{:S(2)}) collective-permute-start(bf16[9,64,640]{2,1,0:T(8,128)(2,1)S(1)} %get-tuple-element.22), channel_id=1, source_target_pairs={{16,0},{32,16},{48,32},{17,1},{33,17},{49,33},{18,2},{34,18},{50,3... | collective-permute-start | bytes 2211848 | tf_op jit(solution)/shard_map/ppermute | solution.py:34
  70.9 2.4 %collective-permute-start.9 = (bf16[9,64,640]{2,1,0:T(8,128)(2,1)S(1)}, bf16[9,64,640]{2,1,0:T(8,128)(2,1)S(1)}, u32[]{:S(2)}, u32[]{:S(2)}) collective-permute-start(bf16[9,64,640]{2,1,0:T(8,128)(2,1)S(1)} %get-tuple-element.23), channel_id=1, source_target_pairs={{0,16},{16,32},{32,48},{1,17},{17,33},{33,49},{2,18},{18,34},{34,5... | collective-permute-start | bytes 2211848 | tf_op jit(solution)/shard_map/ppermute | solution.py:34
  73.3 4.5 %collective-permute-done.4.from_low_a = bf16[9,64,640]{2,1,0:T(8,128)(2,1)S(1)} collective-permute-done((bf16[9,64,640]{2,1,0:T(8,128)(2,1)S(1)}, bf16[9,64,640]{2,1,0:T(8,128)(2,1)S(1)}, u32[]{:S(2)}, u32[]{:S(2)}) %collective-permute-start.4) | collective-permute-done | bytes 737312 | tf_op jit(solution)/shard_map/ppermute | solution.py:34
  77.8 5.3 %collective-permute-done.5.from_high_a = bf16[9,64,640]{2,1,0:T(8,128)(2,1)S(1)} collective-permute-done((bf16[9,64,640]{2,1,0:T(8,128)(2,1)S(1)}, bf16[9,64,640]{2,1,0:T(8,128)(2,1)S(1)}, u32[]{:S(2)}, u32[]{:S(2)}) %collective-permute-start.5) | collective-permute-done | bytes 737312 | tf_op jit(solution)/shard_map/ppermute | solution.py:34
  83.1 0.7 shard_map.56
  83.8 1.9 %collective-permute-start.10 = (bf16[9,64,640]{2,1,0:T(8,128)(2,1)S(1)}, bf16[9,64,640]{2,1,0:T(8,128)(2,1)S(1)}, u32[]{:S(2)}, u32[]{:S(2)}) collective-permute-start(bf16[9,64,640]{2,1,0:T(8,128)(2,1)S(1)} %get-tuple-element.24), channel_id=1, source_target_pairs={{1,0},{2,1},{3,2},{4,3},{5,4},{6,5},{7,6},{8,7},{9,8},{10,9},{11,1... | collective-permute-start | bytes 2211848 | tf_op jit(solution)/shard_map/ppermute | solution.py:34
  85.7 2.4 %collective-permute-start.11 = (bf16[9,64,640]{2,1,0:T(8,128)(2,1)S(1)}, bf16[9,64,640]{2,1,0:T(8,128)(2,1)S(1)}, u32[]{:S(2)}, u32[]{:S(2)}) collective-permute-start(bf16[9,64,640]{2,1,0:T(8,128)(2,1)S(1)} %get-tuple-element.25), channel_id=1, source_target_pairs={{0,1},{1,2},{2,3},{3,4},{4,5},{5,6},{6,7},{7,8},{8,9},{9,10},{10,1... | collective-permute-start | bytes 2211848 | tf_op jit(solution)/shard_map/ppermute | solution.py:34
  88.1 10.8 %collective-permute-done.8.from_low_b = bf16[9,64,640]{2,1,0:T(8,128)(2,1)S(1)} collective-permute-done((bf16[9,64,640]{2,1,0:T(8,128)(2,1)S(1)}, bf16[9,64,640]{2,1,0:T(8,128)(2,1)S(1)}, u32[]{:S(2)}, u32[]{:S(2)}) %collective-permute-start.8) | collective-permute-done | bytes 737312 | tf_op jit(solution)/shard_map/ppermute | solution.py:34
  98.9 6.3 %collective-permute-done.9.from_high_b = bf16[9,64,640]{2,1,0:T(8,128)(2,1)S(1)} collective-permute-done((bf16[9,64,640]{2,1,0:T(8,128)(2,1)S(1)}, bf16[9,64,640]{2,1,0:T(8,128)(2,1)S(1)}, u32[]{:S(2)}, u32[]{:S(2)}) %collective-permute-start.9) | collective-permute-done | bytes 737312 | tf_op jit(solution)/shard_map/ppermute | solution.py:34
  105.2 0.7 shard_map.57
  105.9 1.9 %collective-permute-start.12 = (bf16[9,64,640]{2,1,0:T(8,128)(2,1)S(1)}, bf16[9,64,640]{2,1,0:T(8,128)(2,1)S(1)}, u32[]{:S(2)}, u32[]{:S(2)}) collective-permute-start(bf16[9,64,640]{2,1,0:T(8,128)(2,1)S(1)} %get-tuple-element.26), channel_id=1, source_target_pairs={{1,0},{2,1},{3,2},{4,3},{5,4},{6,5},{7,6},{8,7},{9,8},{10,9},{11,1... | collective-permute-start | bytes 2211848 | tf_op jit(solution)/shard_map/ppermute | solution.py:34
  107.8 2.4 %collective-permute-start.13 = (bf16[9,64,640]{2,1,0:T(8,128)(2,1)S(1)}, bf16[9,64,640]{2,1,0:T(8,128)(2,1)S(1)}, u32[]{:S(2)}, u32[]{:S(2)}) collective-permute-start(bf16[9,64,640]{2,1,0:T(8,128)(2,1)S(1)} %get-tuple-element.27), channel_id=1, source_target_pairs={{0,1},{1,2},{2,3},{3,4},{4,5},{5,6},{6,7},{7,8},{8,9},{9,10},{10,1... | collective-permute-start | bytes 2211848 | tf_op jit(solution)/shard_map/ppermute | solution.py:34
  110.2 0.7 shard_map.53.seed
  110.9 0.8 shard_map.52.upper
  111.6 0.0 copy-start.1
  111.7 0.0 copy-start.4
  111.7 0.7 shard_map.55.lower
  112.4 0.0 collective-permute-done.10.first_low_c
  112.4 2.9 %collective-permute-done.11.first_high_c = bf16[9,64,640]{2,1,0:T(8,128)(2,1)S(1)} collective-permute-done((bf16[9,64,640]{2,1,0:T(8,128)(2,1)S(1)}, bf16[9,64,640]{2,1,0:T(8,128)(2,1)S(1)}, u32[]{:S(2)}, u32[]{:S(2)}) %collective-permute-start.11) | collective-permute-done | bytes 737312 | tf_op jit(solution)/shard_map/ppermute | solution.py:34
  115.3 1.5 %collective-permute-done.12.second_low_c = bf16[9,64,640]{2,1,0:T(8,128)(2,1)S(1)} collective-permute-done((bf16[9,64,640]{2,1,0:T(8,128)(2,1)S(1)}, bf16[9,64,640]{2,1,0:T(8,128)(2,1)S(1)}, u32[]{:S(2)}, u32[]{:S(2)}) %collective-permute-start.12) | collective-permute-done | bytes 737312 | tf_op jit(solution)/shard_map/ppermute | solution.py:34
  116.8 7.6 %collective-permute-done.13.second_high_c = bf16[9,64,640]{2,1,0:T(8,128)(2,1)S(1)} collective-permute-done((bf16[9,64,640]{2,1,0:T(8,128)(2,1)S(1)}, bf16[9,64,640]{2,1,0:T(8,128)(2,1)S(1)}, u32[]{:S(2)}, u32[]{:S(2)}) %collective-permute-start.13) | collective-permute-done | bytes 737312 | tf_op jit(solution)/shard_map/ppermute | solution.py:34
  124.3 0.0 copy-done.1
  124.3 0.0 copy-done.4
  124.3 4.4 %shard_map.58 = (bf16[1024,512]{1,0:T(8,128)(2,1)}, bf16[1024,512]{1,0:T(8,128)(2,1)}) custom-call(s32[26]{0:T(128)S(1)} %bitcast.20, s32[1]{0:T(128)} %bitcast.1.row_here, s32[1]{0:T(128)} %bitcast.2.layer_here, f32[8,64,640]{2,1,0:T(8,128)S(1)} %shard_map.52.upper, f32[8,64,640]{2,1,0:T(8,128)S(1)} %shard_map.55.lower, ...), custom_call_target="tpu_custom_call" | custom-call | tf_op jit(solution)/shard_map/pallas_call | solution.py:189
Async XLA Ops:
  0.6 1.6 %copy-start = (bf16[1,1,1,1024,1024]{4,3,2,1,0:T(8,128)(2,1)S(1)}, bf16[1,1,1,1024,1024]{4,3,2,1,0:T(8,128)(2,1)}, u32[]{:S(2)}) copy-start(bf16[1,1,1,1024,1024]{4,3,2,1,0:T(8,128)(2,1)} %param.3) | copy-start | bytes 6291460
  2.2 1.2 copy-start.2
  3.5 0.7 copy-start.3
  6.0 59.8 %collective-permute-start.6 = (bf16[9,64,640]{2,1,0:T(8,128)(2,1)S(1)}, bf16[9,64,640]{2,1,0:T(8,128)(2,1)S(1)}, u32[]{:S(2)}, u32[]{:S(2)}) collective-permute-start(bf16[9,64,640]{2,1,0:T(8,128)(2,1)S(1)} %get-tuple-element.20), channel_id=1, source_target_pairs={{0,448},{64,0},{128,64},{192,128},{256,192},{320,256},{384,320},{4... | collective-permute-start | bytes 2211848 | tf_op jit(solution)/shard_map/ppermute | solution.py:34
  17.0 48.8 %collective-permute-start.7 = (bf16[9,64,640]{2,1,0:T(8,128)(2,1)S(1)}, bf16[9,64,640]{2,1,0:T(8,128)(2,1)S(1)}, u32[]{:S(2)}, u32[]{:S(2)}) collective-permute-start(bf16[9,64,640]{2,1,0:T(8,128)(2,1)S(1)} %get-tuple-element.21), channel_id=1, source_target_pairs={{0,64},{64,128},{128,192},{192,256},{256,320},{320,384},{384,448},... | collective-permute-start | bytes 2211848 | tf_op jit(solution)/shard_map/ppermute | solution.py:34
  18.9 39.4 %collective-permute-start.3 = (bf16[8,64,640]{2,1,0:T(8,128)(2,1)S(1)}, bf16[8,64,640]{2,1,0:T(8,128)(2,1)S(1)}, u32[]{:S(2)}, u32[]{:S(2)}) collective-permute-start(bf16[8,64,640]{2,1,0:T(8,128)(2,1)S(1)} %get-tuple-element.16.top), channel_id=1, source_target_pairs={{0,16},{16,32},{32,48},{1,17},{17,33},{33,49},{2,18},{18,34},{34,5... | collective-permute-start | bytes 1966088 | tf_op jit(solution)/shard_map/ppermute | solution.py:34
  21.6 36.7 %collective-permute-start.2 = (bf16[8,64,640]{2,1,0:T(8,128)(2,1)S(1)}, bf16[8,64,640]{2,1,0:T(8,128)(2,1)S(1)}, u32[]{:S(2)}, u32[]{:S(2)}) collective-permute-start(bf16[8,64,640]{2,1,0:T(8,128)(2,1)S(1)} %get-tuple-element.16.top), channel_id=1, source_target_pairs={{16,0},{32,16},{48,32},{17,1},{33,17},{49,33},{18,2},{34,18},{50,3... | collective-permute-start | bytes 1966088 | tf_op jit(solution)/shard_map/ppermute | solution.py:34
  26.9 25.1 %collective-permute-start.1 = (s32[26]{0:T(128)S(1)}, s32[26]{0:T(128)S(1)}, u32[]{:S(2)}, u32[]{:S(2)}) collective-permute-start(s32[26]{0:T(128)S(1)} %bitcast.11), channel_id=1, source_target_pairs={{0,16},{16,32},{32,48},{1,17},{17,33},{33,49},{2,18},{18,34},{34,5... | collective-permute-start | bytes 320 | tf_op jit(solution)/shard_map/ppermute | solution.py:34
  52.0 6.3 %collective-permute-start = (s32[26]{0:T(128)S(1)}, s32[26]{0:T(128)S(1)}, u32[]{:S(2)}, u32[]{:S(2)}) collective-permute-start(s32[26]{0:T(128)S(1)} %bitcast.12), channel_id=1, source_target_pairs={{16,0},{32,16},{48,32},{17,1},{33,17},{49,33},{18,2},{34,18},{50,3... | collective-permute-start | bytes 320 | tf_op jit(solution)/shard_map/ppermute | solution.py:34
  59.0 18.7 %collective-permute-start.4 = (bf16[9,64,640]{2,1,0:T(8,128)(2,1)S(1)}, bf16[9,64,640]{2,1,0:T(8,128)(2,1)S(1)}, u32[]{:S(2)}, u32[]{:S(2)}) collective-permute-start(bf16[9,64,640]{2,1,0:T(8,128)(2,1)S(1)} %get-tuple-element.17), channel_id=1, source_target_pairs={{0,448},{64,0},{128,64},{192,128},{256,192},{320,256},{384,320},{4... | collective-permute-start | bytes 2211848 | tf_op jit(solution)/shard_map/ppermute | solution.py:34
  63.9 19.2 %collective-permute-start.5 = (bf16[9,64,640]{2,1,0:T(8,128)(2,1)S(1)}, bf16[9,64,640]{2,1,0:T(8,128)(2,1)S(1)}, u32[]{:S(2)}, u32[]{:S(2)}) collective-permute-start(bf16[9,64,640]{2,1,0:T(8,128)(2,1)S(1)} %get-tuple-element.18), channel_id=1, source_target_pairs={{0,64},{64,128},{128,192},{192,256},{256,320},{320,384},{384,448},... | collective-permute-start | bytes 2211848 | tf_op jit(solution)/shard_map/ppermute | solution.py:34
  66.5 32.4 %collective-permute-start.8 = (bf16[9,64,640]{2,1,0:T(8,128)(2,1)S(1)}, bf16[9,64,640]{2,1,0:T(8,128)(2,1)S(1)}, u32[]{:S(2)}, u32[]{:S(2)}) collective-permute-start(bf16[9,64,640]{2,1,0:T(8,128)(2,1)S(1)} %get-tuple-element.22), channel_id=1, source_target_pairs={{16,0},{32,16},{48,32},{17,1},{33,17},{49,33},{18,2},{34,18},{50,3... | collective-permute-start | bytes 2211848 | tf_op jit(solution)/shard_map/ppermute | solution.py:34
  70.9 34.3 %collective-permute-start.9 = (bf16[9,64,640]{2,1,0:T(8,128)(2,1)S(1)}, bf16[9,64,640]{2,1,0:T(8,128)(2,1)S(1)}, u32[]{:S(2)}, u32[]{:S(2)}) collective-permute-start(bf16[9,64,640]{2,1,0:T(8,128)(2,1)S(1)} %get-tuple-element.23), channel_id=1, source_target_pairs={{0,16},{16,32},{32,48},{1,17},{17,33},{33,49},{2,18},{18,34},{34,5... | collective-permute-start | bytes 2211848 | tf_op jit(solution)/shard_map/ppermute | solution.py:34
  83.8 28.6 %collective-permute-start.10 = (bf16[9,64,640]{2,1,0:T(8,128)(2,1)S(1)}, bf16[9,64,640]{2,1,0:T(8,128)(2,1)S(1)}, u32[]{:S(2)}, u32[]{:S(2)}) collective-permute-start(bf16[9,64,640]{2,1,0:T(8,128)(2,1)S(1)} %get-tuple-element.24), channel_id=1, source_target_pairs={{1,0},{2,1},{3,2},{4,3},{5,4},{6,5},{7,6},{8,7},{9,8},{10,9},{11,1... | collective-permute-start | bytes 2211848 | tf_op jit(solution)/shard_map/ppermute | solution.py:34
  85.7 29.6 %collective-permute-start.11 = (bf16[9,64,640]{2,1,0:T(8,128)(2,1)S(1)}, bf16[9,64,640]{2,1,0:T(8,128)(2,1)S(1)}, u32[]{:S(2)}, u32[]{:S(2)}) collective-permute-start(bf16[9,64,640]{2,1,0:T(8,128)(2,1)S(1)} %get-tuple-element.25), channel_id=1, source_target_pairs={{0,1},{1,2},{2,3},{3,4},{4,5},{5,6},{6,7},{7,8},{8,9},{9,10},{10,1... | collective-permute-start | bytes 2211848 | tf_op jit(solution)/shard_map/ppermute | solution.py:34
  105.9 10.9 %collective-permute-start.12 = (bf16[9,64,640]{2,1,0:T(8,128)(2,1)S(1)}, bf16[9,64,640]{2,1,0:T(8,128)(2,1)S(1)}, u32[]{:S(2)}, u32[]{:S(2)}) collective-permute-start(bf16[9,64,640]{2,1,0:T(8,128)(2,1)S(1)} %get-tuple-element.26), channel_id=1, source_target_pairs={{1,0},{2,1},{3,2},{4,3},{5,4},{6,5},{7,6},{8,7},{9,8},{10,9},{11,1... | collective-permute-start | bytes 2211848 | tf_op jit(solution)/shard_map/ppermute | solution.py:34
  107.8 16.5 %collective-permute-start.13 = (bf16[9,64,640]{2,1,0:T(8,128)(2,1)S(1)}, bf16[9,64,640]{2,1,0:T(8,128)(2,1)S(1)}, u32[]{:S(2)}, u32[]{:S(2)}) collective-permute-start(bf16[9,64,640]{2,1,0:T(8,128)(2,1)S(1)} %get-tuple-element.27), channel_id=1, source_target_pairs={{0,1},{1,2},{2,3},{3,4},{4,5},{5,6},{6,7},{7,8},{8,9},{9,10},{10,1... | collective-permute-start | bytes 2211848 | tf_op jit(solution)/shard_map/ppermute | solution.py:34
  111.6 12.7 %copy-start.1 = (bf16[1,1,1,1024,1024]{4,3,2,1,0:T(8,128)(2,1)S(1)}, bf16[1,1,1,1024,1024]{4,3,2,1,0:T(8,128)(2,1)}, u32[]{:S(2)}) copy-start(bf16[1,1,1,1024,1024]{4,3,2,1,0:T(8,128)(2,1)} %param.3) | copy-start | bytes 6291460
  111.7 12.7 %copy-start.4 = (s32[1,1,1,26]{3,2,1,0:T(1,128)S(1)}, s32[1,1,1,26]{3,2,1,0:T(1,128)}, u32[]{:S(2)}) copy-start(s32[1,1,1,26]{3,2,1,0:T(1,128)} %param.4) | copy-start | bytes 316

commit v5 on v4

v5 whole, which is shorter than its diff:
```python
import functools

import jax
import jax.numpy as jnp
from jax import lax
from jax.experimental import pallas as pl
from jax.experimental.pallas import tpu as pltpu
from jax.sharding import PartitionSpec as P


BLOCK = 128
HALF = BLOCK // 2
STEPS = (-1, 0, 1)
SIDES = (-1, 1)
MIB = 1024 * 1024


def link(a, b, c):
    place = 9 * (a + 1) + 3 * (b + 1) + (c + 1)
    return place if place < 13 else place - 1


def cell(first, second):
    return 3 * (first + 1) + (second + 1)


def shift(value, axis, step, wrap):
    count = lax.axis_size(axis)
    pairs = [
        (source, (source + step) % count)
        for source in range(count)
        if wrap or 0 <= source + step < count
    ]
    return lax.ppermute(value, axis, pairs)


def head_kernel(
    links,
    row_here,
    layer_here,
    schur,
    vectors,
    top,
    bottom,
    low_a,
    high_a,
    matrix,
    right_side,
    sems,
):
    blocks = top.shape[0]
    copies = [pltpu.make_async_copy(vectors, right_side, sems.at[blocks])]
    for k in range(blocks):
        rows = slice(k * BLOCK, (k + 1) * BLOCK)
        copies.append(pltpu.make_async_copy(schur.at[rows, :], matrix.at[rows, :], sems.at[k]))
    for copy in copies:
        copy.start()
    copies[0].wait()
    for k in range(blocks):
        rows = slice(k * BLOCK, (k + 1) * BLOCK)
        copies[k + 1].wait()
        product = jnp.dot(
            matrix[rows, :], right_side[...], preferred_element_type=jnp.float32
        ).astype(jnp.bfloat16)
        diagonal = matrix[rows, rows]
        top[k, :, BLOCK:] = product[:HALF]
        top[k, :, :BLOCK] = diagonal[:HALF]
        bottom[k, :, BLOCK:] = product[HALF:]
        bottom[k, :, :BLOCK] = diagonal[HALF:]
    for a, out in zip(SIDES, (low_a, high_a)):
        for b in STEPS:
            for c in STEPS:
                out[cell(b, c)] = bottom[links[link(a, b, c)]]


def first_a_kernel(links, low_links, high_links, top, from_low_b, from_high_b, low_a, high_a):
    for a, out in zip(SIDES, (low_a, high_a)):
        for c in STEPS:
            out[cell(-1, c)] = from_low_b[low_links[link(a, -1, c)]]
            out[cell(0, c)] = top[links[link(a, 0, c)]]
            out[cell(1, c)] = from_high_b[high_links[link(a, 1, c)]]


def ahead_c_kernel(
    links,
    low_links,
    high_links,
    top,
    bottom,
    first_low_b,
    first_high_b,
    second_low_a,
    second_high_a,
    low_c,
    high_c,
):
    for c, out in zip(SIDES, (low_c, high_c)):
        out[0] = first_low_b[low_links[link(0, -1, c)]]
        out[1] = top[links[link(0, 0, c)]]
        out[2] = first_high_b[high_links[link(0, 1, c)]]
        out[3] = second_low_a[cell(0, c)]
        out[4] = bottom[links[link(0, 0, c)]]
        out[5] = second_high_a[cell(0, c)]


def late_c_kernel(from_low, from_high, low_c, high_c):
    for c, out in zip(SIDES, (low_c, high_c)):
        for step in STEPS:
            out[step + 1] = from_low[cell(step, c)]
            out[step + 4] = from_high[cell(step, c)]


def second_b_kernel(links, bottom, from_low_a, from_high_a, low_b, high_b):
    for b, out in zip(SIDES, (low_b, high_b)):
        for c in STEPS:
            out[cell(-1, c)] = from_low_a[cell(b, c)]
            out[cell(0, c)] = bottom[links[link(0, b, c)]]
            out[cell(1, c)] = from_high_a[cell(b, c)]


def add_into(sums, slot, piece):
    sums[slot] = sums[slot] + piece.astype(jnp.float32)


def seed_kernel(links, bottom, from_low_a, from_high_a, lower):
    lower[...] = bottom[...].astype(jnp.float32)
    for a, source in zip(SIDES, (from_low_a, from_high_a)):
        add_into(lower, links[link(-a, 0, 0)], source[cell(0, 0)])


def lower_kernel(links, seed, from_low_b, from_high_b, ahead_low_c, ahead_high_c, lower):
    lower[...] = seed[...]
    for b, source in zip(SIDES, (from_low_b, from_high_b)):
        for a in STEPS:
            add_into(lower, links[link(-a, -b, 0)], source[cell(a, 0)])
    for c, source in zip(SIDES, (ahead_low_c, ahead_high_c)):
        for a in STEPS:
            add_into(lower, links[link(-a, 0, -c)], source[a + 4])


def upper_kernel(
    links,
    low_links,
    high_links,
    top,
    from_low_b,
    from_high_b,
    from_low_a,
    from_high_a,
    ahead_low_c,
    ahead_high_c,
    from_low_c,
    from_high_c,
    upper,
):
    upper[...] = top[...].astype(jnp.float32)
    for b, source, there in zip(SIDES, (from_low_b, from_high_b), (low_links, high_links)):
        add_into(upper, links[link(0, -b, 0)], source[there[link(0, b, 0)]])
    for a, source in zip(SIDES, (from_low_a, from_high_a)):
        for b in STEPS:
            add_into(upper, links[link(-a, -b, 0)], source[cell(b, 0)])
    for c, ahead, source in zip(
        SIDES, (ahead_low_c, ahead_high_c), (from_low_c, from_high_c)
    ):
        for b in STEPS:
            add_into(upper, links[link(0, -b, -c)], ahead[b + 1])
            add_into(upper, links[link(1, -b, -c)], source[b + 1])
            add_into(upper, links[link(-1, -b, -c)], source[b + 4])


def tail_kernel(
    columns,
    layers,
    links,
    row_here,
    layer_here,
    upper,
    lower,
    from_low_c,
    from_high_c,
    schur,
    assembled,
    update,
    under,
    summed_rows,
    scaled,
    update_rows,
    counts,
    sems,
):
    blocks = upper.shape[0]
    row, layer = row_here[0], layer_here[0]
    for k in range(blocks):
        counts[k] = 1
    for a in STEPS:
        for b in STEPS:
            for c in STEPS:
                if (a, b, c) == (0, 0, 0):
                    continue
                slot = links[link(a, b, c)]
                alive = (row + b >= 0) & (row + b < columns) & (layer + c >= 0) & (layer + c < layers)
                counts[slot] = counts[slot] + jnp.where(alive, 1, 0)
    under[...] = lower[...]
    for c, source in zip(SIDES, (from_low_c, from_high_c)):
        for a in STEPS:
            add_into(under, links[link(-a, 1, -c)], source[a + 1])
            add_into(under, links[link(-a, -1, -c)], source[a + 4])
    copies = []
    for k in range(blocks):
        rows = slice(k * BLOCK, (k + 1) * BLOCK)
        whole = jnp.concatenate([upper[k], under[k]], axis=0)
        coupling = whole[:, :BLOCK]
        summed = whole[:, BLOCK:]
        summed_high = summed.astype(jnp.bfloat16)
        summed_low = (summed - summed_high.astype(jnp.float32)).astype(jnp.bfloat16)
        coupling_high = coupling.astype(jnp.bfloat16)
        coupling_low = (coupling - coupling_high.astype(jnp.float32)).astype(jnp.bfloat16)
        summed_rows[rows, :] = summed_high
        copies.append(
            pltpu.make_async_copy(summed_rows.at[rows, :], assembled.at[rows, :], sems.at[k])
        )
        copies[-1].start()
        mixed = jnp.dot(coupling_high, summed_high, preferred_element_type=jnp.float32)
        mixed += jnp.dot(coupling_high, summed_low, preferred_element_type=jnp.float32)
        mixed += jnp.dot(coupling_low, summed_high, preferred_element_type=jnp.float32)
        share = jnp.full((BLOCK, 1), counts[k], jnp.int32).astype(jnp.float32)
        scaled[rows, :] = (mixed / share).astype(jnp.bfloat16)
    for k in range(blocks):
        rows = slice(k * BLOCK, (k + 1) * BLOCK)
        update_rows[rows, :] = jnp.dot(
            schur[rows, :], scaled[...], preferred_element_type=jnp.float32
        ).astype(jnp.bfloat16)
        copies.append(
            pltpu.make_async_copy(update_rows.at[rows, :], update.at[rows, :], sems.at[blocks + k])
        )
        copies[-1].start()
    for copy in copies:
        copy.wait()


def call(kernel, outs, *operands, smem=1, scratch=(), room=4, far_in=0, far_out=False):
    near = pl.BlockSpec(memory_space=pltpu.VMEM)
    far = pl.BlockSpec(memory_space=pltpu.HBM)
    specs = [pl.BlockSpec(memory_space=pltpu.SMEM)] * smem
    specs += [near] * (len(operands) - smem - far_in) + [far] * far_in
    return pl.pallas_call(
        kernel,
        out_shape=outs,
        in_specs=specs,
        out_specs=[far if far_out else near for _ in outs],
        scratch_shapes=list(scratch),
        compiler_params=pltpu.CompilerParams(vmem_limit_bytes=room * MIB),
    )(*operands)


def local(schur, block_map, vectors):
    matrix = schur[0, 0, 0]
    right_side = vectors[0, 0, 0]
    links = block_map[0, 0, 0]
    order, width = right_side.shape
    blocks = order // BLOCK
    full = BLOCK + width
    nine = [jax.ShapeDtypeStruct((9, HALF, full), jnp.bfloat16)] * 2
    six = [jax.ShapeDtypeStruct((6, HALF, full), jnp.bfloat16)] * 2
    eight = [jax.ShapeDtypeStruct((blocks, HALF, full), jnp.bfloat16)] * 2
    half = [jax.ShapeDtypeStruct((blocks, HALF, full), jnp.float32)]
    here = [links] + [lax.axis_index(axis).astype(jnp.int32).reshape(1) for axis in ("gy", "gz")]
    maps = [links] + [shift(links, "gy", s, False) for s in SIDES]
    top, bottom, *sent = call(
        head_kernel,
        eight + nine,
        *here,
        matrix,
        right_side,
        smem=3,
        far_in=2,
        scratch=[
            pltpu.VMEM((order, order), jnp.bfloat16),
            pltpu.VMEM((order, width), jnp.bfloat16),
            pltpu.SemaphoreType.DMA((blocks + 1,)),
        ],
        room=51,
    )
    first_b = [shift(top, "gy", s, False) for s in SIDES]
    second_a = [shift(v, "gx", s, True) for s, v in zip(SIDES, sent)]
    sent = call(second_b_kernel, nine, links, bottom, *second_a)
    second_b = [shift(v, "gy", s, False) for s, v in zip(SIDES, sent)]
    (seed,) = call(seed_kernel, half, links, bottom, *second_a)
    sent = call(first_a_kernel, nine, *maps, top, *first_b, smem=3)
    first_a = [shift(v, "gx", s, True) for s, v in zip(SIDES, sent)]
    sent = call(ahead_c_kernel, six, *maps, top, bottom, *first_b, *second_a, smem=3)
    ahead_c = [shift(v, "gz", s, False) for s, v in zip(SIDES, sent)]
    sent = call(late_c_kernel, six, *first_a, smem=0)
    first_c = [shift(v, "gz", s, False) for s, v in zip(SIDES, sent)]
    sent = call(late_c_kernel, six, *second_b, smem=0)
    second_c = [shift(v, "gz", s, False) for s, v in zip(SIDES, sent)]
    (lower,) = call(lower_kernel, half, links, seed, *second_b, *ahead_c)
    (upper,) = call(upper_kernel, half, *maps, top, *first_b, *first_a, *ahead_c, *first_c, smem=3)
    assembled, update = call(
        functools.partial(tail_kernel, lax.axis_size("gy"), lax.axis_size("gz")),
        [jax.ShapeDtypeStruct((order, width), jnp.bfloat16)] * 2,
        *here,
        upper,
        lower,
        *second_c,
        matrix,
        smem=3,
        scratch=[
            pltpu.VMEM((blocks, HALF, full), jnp.float32),
            pltpu.VMEM((order, width), jnp.bfloat16),
            pltpu.VMEM((order, width), jnp.bfloat16),
            pltpu.VMEM((order, width), jnp.bfloat16),
            pltpu.SMEM((blocks,), jnp.int32),
            pltpu.SemaphoreType.DMA((2 * blocks,)),
        ],
        room=12,
        far_out=True,
    )
    return (assembled[None, None, None], update[None, None, None])


def solution(mesh):
    placed = (
        P("gx", "gy", "gz", None, None),
        P("gx", "gy", "gz", None),
        P("gx", "gy", "gz", None, None),
    )

    return jax.shard_map(
        local,
        mesh=mesh,
        in_specs=placed,
        out_specs=(P("gx", "gy", "gz", None, None), P("gx", "gy", "gz", None, None)),
        check_vma=False,
    )
```

time: 129 us -> 125 us (0.969)
  waiting for transfers between devices: 65.2 us -> 45.6 us
  starting transfers between devices: 48.1 us -> 64.4 us
  local copies, waits for them, and re-layouts: 3.48 us -> 0.65 us
  Pallas kernels: 11.1 us -> 13 us
    ppermute x14 -> x16, waiting for transfers between devices: 65.2 us -> 45.6 us  [shift(): return lax.ppermute(value, axis, pairs)]
    ppermute x14 -> x16, starting transfers between devices: 48.1 us -> 64.4 us  [shift(): return lax.ppermute(value, axis, pairs)]
    unnamed x10 -> x4, local copies, waits for them, and re-layouts: 3.48 us -> 0.65 us
    pallas_call x9 -> x10, Pallas kernels: 11.1 us -> 13 us  [call(): pl.pallas_call(kernel, out_shape=outs, in_specs=specs, out_specs=[far if...]
  transfers between devices with their start and end apart: 14 -> 16, of which waited for: 9 -> 7; matrix products, arithmetic and copies ran while one was open for 0% -> 0% of each run, Pallas kernels for 4% -> 4%
where the time goes in v5:
time: 125 us
  starting transfers between devices  64.4 us (52%)
  waiting for transfers between devices  45.6 us (36%)
  Pallas kernels  13 us (10%)
    ppermute x16, starting transfers between devices, shift(): return lax.ppermute(value, axis, pairs)  64.4 us
    ppermute x16, waiting for transfers between devices, shift(): return lax.ppermute(value, axis, pairs)  45.6 us
    pallas_call x10, Pallas kernels, call(): pl.pallas_call(kernel, out_shape=outs, in_specs=specs, out_specs=[far if...  13 us
  transfers between devices with their start and end apart: 16, of which 7 were waited for; matrix products, arithmetic and copies ran while one was open for 0% of the time, Pallas kernels for 4%

profile of v5, /device:TPU:40, one launch (start us, length us, event | category | flops | bytes accessed | tf_op | source)
XLA Modules:
  0.0 124.5 jit_solution(3508664256760552753)
XLA Ops:
  0.6 0.0 copy-start.1
  0.6 0.6 copy-done.1
  1.3 4.5 %shard_map.50 = (bf16[8,64,640]{2,1,0:T(8,128)(2,1)S(1)}, bf16[8,64,640]{2,1,0:T(8,128)(2,1)S(1)}, bf16[9,64,640]{2,1,0:T(8,128)(2,1)S(1)}, bf16[9,64,640]{2,1,0:T(8,128)(2,1)S(1)}) custom-call(s32[26]{0:T(128)S(1)} %bitcast.9, s32[1]{0:T(128)} %bitcast.1.row_here, s32[1]{0:T(128)} %bitcast.2.layer_here, bf16[1024,1024]{1,0:T(8,128)(2,1)} %bitcast.7, ...), custom_call_target="tpu_custom_call" | custom-call | tf_op jit(solution)/shard_map/pallas_call | solution.py:246
  5.8 10.9 %collective-permute-start.6 = (bf16[9,64,640]{2,1,0:T(8,128)(2,1)S(1)}, bf16[9,64,640]{2,1,0:T(8,128)(2,1)S(1)}, u32[]{:S(2)}, u32[]{:S(2)}) collective-permute-start(bf16[9,64,640]{2,1,0:T(8,128)(2,1)S(1)} %get-tuple-element.22), channel_id=1, source_target_pairs={{0,448},{64,0},{128,64},{192,128},{256,192},{320,256},{384,320},{4... | collective-permute-start | bytes 2211848 | tf_op jit(solution)/shard_map/ppermute | solution.py:34
  16.8 1.9 %collective-permute-start.7 = (bf16[9,64,640]{2,1,0:T(8,128)(2,1)S(1)}, bf16[9,64,640]{2,1,0:T(8,128)(2,1)S(1)}, u32[]{:S(2)}, u32[]{:S(2)}) collective-permute-start(bf16[9,64,640]{2,1,0:T(8,128)(2,1)S(1)} %get-tuple-element.23), channel_id=1, source_target_pairs={{0,64},{64,128},{128,192},{192,256},{256,320},{320,384},{384,448},... | collective-permute-start | bytes 2211848 | tf_op jit(solution)/shard_map/ppermute | solution.py:34
  18.7 3.1 %collective-permute-start.2 = (bf16[8,64,640]{2,1,0:T(8,128)(2,1)S(1)}, bf16[8,64,640]{2,1,0:T(8,128)(2,1)S(1)}, u32[]{:S(2)}, u32[]{:S(2)}) collective-permute-start(bf16[8,64,640]{2,1,0:T(8,128)(2,1)S(1)} %get-tuple-element.18.top), channel_id=1, source_target_pairs={{16,0},{32,16},{48,32},{17,1},{33,17},{49,33},{18,2},{34,18},{50,3... | collective-permute-start | bytes 1966088 | tf_op jit(solution)/shard_map/ppermute | solution.py:34
  21.9 3.6 %collective-permute-start.3 = (bf16[8,64,640]{2,1,0:T(8,128)(2,1)S(1)}, bf16[8,64,640]{2,1,0:T(8,128)(2,1)S(1)}, u32[]{:S(2)}, u32[]{:S(2)}) collective-permute-start(bf16[8,64,640]{2,1,0:T(8,128)(2,1)S(1)} %get-tuple-element.18.top), channel_id=1, source_target_pairs={{0,16},{16,32},{32,48},{1,17},{17,33},{33,49},{2,18},{18,34},{34,5... | collective-permute-start | bytes 1966088 | tf_op jit(solution)/shard_map/ppermute | solution.py:34
  25.5 4.3 %collective-permute-start = (s32[26]{0:T(128)S(1)}, s32[26]{0:T(128)S(1)}, u32[]{:S(2)}, u32[]{:S(2)}) collective-permute-start(s32[26]{0:T(128)S(1)} %bitcast.10), channel_id=1, source_target_pairs={{16,0},{32,16},{48,32},{17,1},{33,17},{49,33},{18,2},{34,18},{50,3... | collective-permute-start | bytes 320 | tf_op jit(solution)/shard_map/ppermute | solution.py:34
  29.8 8.1 %collective-permute-done.low_links = s32[26]{0:T(128)S(1)} collective-permute-done((s32[26]{0:T(128)S(1)}, s32[26]{0:T(128)S(1)}, u32[]{:S(2)}, u32[]{:S(2)}) %collective-permute-start) | collective-permute-done | bytes 136 | tf_op jit(solution)/shard_map/ppermute | solution.py:34
  37.9 1.9 %collective-permute-start.1 = (s32[26]{0:T(128)S(1)}, s32[26]{0:T(128)S(1)}, u32[]{:S(2)}, u32[]{:S(2)}) collective-permute-start(s32[26]{0:T(128)S(1)} %bitcast.11), channel_id=1, source_target_pairs={{0,16},{16,32},{32,48},{1,17},{17,33},{33,49},{2,18},{18,34},{34,5... | collective-permute-start | bytes 320 | tf_op jit(solution)/shard_map/ppermute | solution.py:34
  39.8 14.8 %collective-permute-done.1.high_links = s32[26]{0:T(128)S(1)} collective-permute-done((s32[26]{0:T(128)S(1)}, s32[26]{0:T(128)S(1)}, u32[]{:S(2)}, u32[]{:S(2)}) %collective-permute-start.1) | collective-permute-done | bytes 136 | tf_op jit(solution)/shard_map/ppermute | solution.py:34
  54.6 0.0 collective-permute-done.2.from_low_b.first_low_b
  54.6 0.0 collective-permute-done.3.from_high_b.first_high_b
  54.6 0.7 shard_map.51
  55.3 4.9 %collective-permute-start.4 = (bf16[9,64,640]{2,1,0:T(8,128)(2,1)S(1)}, bf16[9,64,640]{2,1,0:T(8,128)(2,1)S(1)}, u32[]{:S(2)}, u32[]{:S(2)}) collective-permute-start(bf16[9,64,640]{2,1,0:T(8,128)(2,1)S(1)} %get-tuple-element.19), channel_id=1, source_target_pairs={{0,448},{64,0},{128,64},{192,128},{256,192},{320,256},{384,320},{4... | collective-permute-start | bytes 2211848 | tf_op jit(solution)/shard_map/ppermute | solution.py:34
  60.2 1.9 %collective-permute-start.5 = (bf16[9,64,640]{2,1,0:T(8,128)(2,1)S(1)}, bf16[9,64,640]{2,1,0:T(8,128)(2,1)S(1)}, u32[]{:S(2)}, u32[]{:S(2)}) collective-permute-start(bf16[9,64,640]{2,1,0:T(8,128)(2,1)S(1)} %get-tuple-element.20), channel_id=1, source_target_pairs={{0,64},{64,128},{128,192},{192,256},{256,320},{320,384},{384,448},... | collective-permute-start | bytes 2211848 | tf_op jit(solution)/shard_map/ppermute | solution.py:34
  62.1 0.0 collective-permute-done.6.second_low_a.from_low_a
  62.1 0.0 collective-permute-done.7.second_high_a.from_high_a
  62.1 0.7 shard_map.56
  62.8 2.3 %collective-permute-start.12 = (bf16[9,64,640]{2,1,0:T(8,128)(2,1)S(1)}, bf16[9,64,640]{2,1,0:T(8,128)(2,1)S(1)}, u32[]{:S(2)}, u32[]{:S(2)}) collective-permute-start(bf16[9,64,640]{2,1,0:T(8,128)(2,1)S(1)} %get-tuple-element.28), channel_id=1, source_target_pairs={{16,0},{32,16},{48,32},{17,1},{33,17},{49,33},{18,2},{34,18},{50,3... | collective-permute-start | bytes 2211848 | tf_op jit(solution)/shard_map/ppermute | solution.py:34
  65.1 4.5 %collective-permute-start.13 = (bf16[9,64,640]{2,1,0:T(8,128)(2,1)S(1)}, bf16[9,64,640]{2,1,0:T(8,128)(2,1)S(1)}, u32[]{:S(2)}, u32[]{:S(2)}) collective-permute-start(bf16[9,64,640]{2,1,0:T(8,128)(2,1)S(1)} %get-tuple-element.29), channel_id=1, source_target_pairs={{0,16},{16,32},{32,48},{1,17},{17,33},{33,49},{2,18},{18,34},{34,5... | collective-permute-start | bytes 2211848 | tf_op jit(solution)/shard_map/ppermute | solution.py:34
  69.6 0.6 shard_map.52
  70.2 7.7 %collective-permute-start.8 = (bf16[6,64,640]{2,1,0:T(8,128)(2,1)S(1)}, bf16[6,64,640]{2,1,0:T(8,128)(2,1)S(1)}, u32[]{:S(2)}, u32[]{:S(2)}) collective-permute-start(bf16[6,64,640]{2,1,0:T(8,128)(2,1)S(1)} %get-tuple-element.24), channel_id=1, source_target_pairs={{1,0},{2,1},{3,2},{4,3},{5,4},{6,5},{7,6},{8,7},{9,8},{10,9},{11,1... | collective-permute-start | bytes 1474568 | tf_op jit(solution)/shard_map/ppermute | solution.py:34
  77.9 0.0 collective-permute-done.4.from_low.from_low_a
  77.9 1.9 %collective-permute-start.9 = (bf16[6,64,640]{2,1,0:T(8,128)(2,1)S(1)}, bf16[6,64,640]{2,1,0:T(8,128)(2,1)S(1)}, u32[]{:S(2)}, u32[]{:S(2)}) collective-permute-start(bf16[6,64,640]{2,1,0:T(8,128)(2,1)S(1)} %get-tuple-element.25), channel_id=1, source_target_pairs={{0,1},{1,2},{2,3},{3,4},{4,5},{5,6},{6,7},{7,8},{8,9},{9,10},{10,1... | collective-permute-start | bytes 1474568 | tf_op jit(solution)/shard_map/ppermute | solution.py:34
  79.9 1.4 %collective-permute-done.5.from_high.from_high_a = bf16[9,64,640]{2,1,0:T(8,128)(2,1)S(1)} collective-permute-done((bf16[9,64,640]{2,1,0:T(8,128)(2,1)S(1)}, bf16[9,64,640]{2,1,0:T(8,128)(2,1)S(1)}, u32[]{:S(2)}, u32[]{:S(2)}) %collective-permute-start.5) | collective-permute-done | bytes 737312 | tf_op jit(solution)/shard_map/ppermute | solution.py:34
  81.3 0.1 shard_map.53
  81.4 6.2 %collective-permute-start.10 = (bf16[6,64,640]{2,1,0:T(8,128)(2,1)S(1)}, bf16[6,64,640]{2,1,0:T(8,128)(2,1)S(1)}, u32[]{:S(2)}, u32[]{:S(2)}) collective-permute-start(bf16[6,64,640]{2,1,0:T(8,128)(2,1)S(1)} %get-tuple-element.26), channel_id=1, source_target_pairs={{1,0},{2,1},{3,2},{4,3},{5,4},{6,5},{7,6},{8,7},{9,8},{10,9},{11,1... | collective-permute-start | bytes 1474568 | tf_op jit(solution)/shard_map/ppermute | solution.py:34
  87.5 0.0 collective-permute-done.12.from_low_b.from_low
  87.5 1.9 %collective-permute-start.11 = (bf16[6,64,640]{2,1,0:T(8,128)(2,1)S(1)}, bf16[6,64,640]{2,1,0:T(8,128)(2,1)S(1)}, u32[]{:S(2)}, u32[]{:S(2)}) collective-permute-start(bf16[6,64,640]{2,1,0:T(8,128)(2,1)S(1)} %get-tuple-element.27), channel_id=1, source_target_pairs={{0,1},{1,2},{2,3},{3,4},{4,5},{5,6},{6,7},{7,8},{8,9},{9,10},{10,1... | collective-permute-start | bytes 1474568 | tf_op jit(solution)/shard_map/ppermute | solution.py:34
  89.5 11.7 %collective-permute-done.13.from_high_b.from_high = bf16[9,64,640]{2,1,0:T(8,128)(2,1)S(1)} collective-permute-done((bf16[9,64,640]{2,1,0:T(8,128)(2,1)S(1)}, bf16[9,64,640]{2,1,0:T(8,128)(2,1)S(1)}, u32[]{:S(2)}, u32[]{:S(2)}) %collective-permute-start.13) | collective-permute-done | bytes 737312 | tf_op jit(solution)/shard_map/ppermute | solution.py:34
  101.2 0.1 shard_map.58
  101.3 5.3 %collective-permute-start.14 = (bf16[6,64,640]{2,1,0:T(8,128)(2,1)S(1)}, bf16[6,64,640]{2,1,0:T(8,128)(2,1)S(1)}, u32[]{:S(2)}, u32[]{:S(2)}) collective-permute-start(bf16[6,64,640]{2,1,0:T(8,128)(2,1)S(1)} %get-tuple-element.30), channel_id=1, source_target_pairs={{1,0},{2,1},{3,2},{4,3},{5,4},{6,5},{7,6},{8,7},{9,8},{10,9},{11,1... | collective-permute-start | bytes 1474568 | tf_op jit(solution)/shard_map/ppermute | solution.py:34
  106.6 0.0 collective-permute-done.8.ahead_low_c
  106.6 1.9 %collective-permute-start.15 = (bf16[6,64,640]{2,1,0:T(8,128)(2,1)S(1)}, bf16[6,64,640]{2,1,0:T(8,128)(2,1)S(1)}, u32[]{:S(2)}, u32[]{:S(2)}) collective-permute-start(bf16[6,64,640]{2,1,0:T(8,128)(2,1)S(1)} %get-tuple-element.31), channel_id=1, source_target_pairs={{0,1},{1,2},{2,3},{3,4},{4,5},{5,6},{6,7},{7,8},{8,9},{9,10},{10,1... | collective-permute-start | bytes 1474568 | tf_op jit(solution)/shard_map/ppermute | solution.py:34
  108.5 0.7 shard_map.55.seed
  109.2 0.9 collective-permute-done.9.ahead_high_c
  110.1 0.8 shard_map.57.lower
  111.0 0.0 collective-permute-done.10.from_low_c
  111.0 4.4 %collective-permute-done.11.from_high_c = bf16[6,64,640]{2,1,0:T(8,128)(2,1)S(1)} collective-permute-done((bf16[6,64,640]{2,1,0:T(8,128)(2,1)S(1)}, bf16[6,64,640]{2,1,0:T(8,128)(2,1)S(1)}, u32[]{:S(2)}, u32[]{:S(2)}) %collective-permute-start.11) | collective-permute-done | bytes 491552 | tf_op jit(solution)/shard_map/ppermute | solution.py:34
  115.4 0.0 copy-start
  115.4 1.0 shard_map.54.upper
  116.4 0.0 collective-permute-done.14.from_low_c
  116.5 4.2 %collective-permute-done.15.from_high_c = bf16[6,64,640]{2,1,0:T(8,128)(2,1)S(1)} collective-permute-done((bf16[6,64,640]{2,1,0:T(8,128)(2,1)S(1)}, bf16[6,64,640]{2,1,0:T(8,128)(2,1)S(1)}, u32[]{:S(2)}, u32[]{:S(2)}) %collective-permute-start.15) | collective-permute-done | bytes 491552 | tf_op jit(solution)/shard_map/ppermute | solution.py:34
  120.7 0.0 copy-done
  120.7 3.8 %shard_map.59 = (bf16[1024,512]{1,0:T(8,128)(2,1)}, bf16[1024,512]{1,0:T(8,128)(2,1)}) custom-call(s32[26]{0:T(128)S(1)} %bitcast.18, s32[1]{0:T(128)} %bitcast.1.row_here, s32[1]{0:T(128)} %bitcast.2.layer_here, f32[8,64,640]{2,1,0:T(8,128)S(1)} %shard_map.54.upper, f32[8,64,640]{2,1,0:T(8,128)S(1)} %shard_map.57.lower, ...), custom_call_target="tpu_custom_call" | custom-call | tf_op jit(solution)/shard_map/pallas_call | solution.py:246
Async XLA Ops:
  0.6 0.7 copy-start.1
  5.8 56.3 %collective-permute-start.6 = (bf16[9,64,640]{2,1,0:T(8,128)(2,1)S(1)}, bf16[9,64,640]{2,1,0:T(8,128)(2,1)S(1)}, u32[]{:S(2)}, u32[]{:S(2)}) collective-permute-start(bf16[9,64,640]{2,1,0:T(8,128)(2,1)S(1)} %get-tuple-element.22), channel_id=1, source_target_pairs={{0,448},{64,0},{128,64},{192,128},{256,192},{320,256},{384,320},{4... | collective-permute-start | bytes 2211848 | tf_op jit(solution)/shard_map/ppermute | solution.py:34
  16.8 45.3 %collective-permute-start.7 = (bf16[9,64,640]{2,1,0:T(8,128)(2,1)S(1)}, bf16[9,64,640]{2,1,0:T(8,128)(2,1)S(1)}, u32[]{:S(2)}, u32[]{:S(2)}) collective-permute-start(bf16[9,64,640]{2,1,0:T(8,128)(2,1)S(1)} %get-tuple-element.23), channel_id=1, source_target_pairs={{0,64},{64,128},{128,192},{192,256},{256,320},{320,384},{384,448},... | collective-permute-start | bytes 2211848 | tf_op jit(solution)/shard_map/ppermute | solution.py:34
  18.7 35.9 %collective-permute-start.2 = (bf16[8,64,640]{2,1,0:T(8,128)(2,1)S(1)}, bf16[8,64,640]{2,1,0:T(8,128)(2,1)S(1)}, u32[]{:S(2)}, u32[]{:S(2)}) collective-permute-start(bf16[8,64,640]{2,1,0:T(8,128)(2,1)S(1)} %get-tuple-element.18.top), channel_id=1, source_target_pairs={{16,0},{32,16},{48,32},{17,1},{33,17},{49,33},{18,2},{34,18},{50,3... | collective-permute-start | bytes 1966088 | tf_op jit(solution)/shard_map/ppermute | solution.py:34
  21.9 32.8 %collective-permute-start.3 = (bf16[8,64,640]{2,1,0:T(8,128)(2,1)S(1)}, bf16[8,64,640]{2,1,0:T(8,128)(2,1)S(1)}, u32[]{:S(2)}, u32[]{:S(2)}) collective-permute-start(bf16[8,64,640]{2,1,0:T(8,128)(2,1)S(1)} %get-tuple-element.18.top), channel_id=1, source_target_pairs={{0,16},{16,32},{32,48},{1,17},{17,33},{33,49},{2,18},{18,34},{34,5... | collective-permute-start | bytes 1966088 | tf_op jit(solution)/shard_map/ppermute | solution.py:34
  25.5 12.4 %collective-permute-start = (s32[26]{0:T(128)S(1)}, s32[26]{0:T(128)S(1)}, u32[]{:S(2)}, u32[]{:S(2)}) collective-permute-start(s32[26]{0:T(128)S(1)} %bitcast.10), channel_id=1, source_target_pairs={{16,0},{32,16},{48,32},{17,1},{33,17},{49,33},{18,2},{34,18},{50,3... | collective-permute-start | bytes 320 | tf_op jit(solution)/shard_map/ppermute | solution.py:34
  37.9 16.7 %collective-permute-start.1 = (s32[26]{0:T(128)S(1)}, s32[26]{0:T(128)S(1)}, u32[]{:S(2)}, u32[]{:S(2)}) collective-permute-start(s32[26]{0:T(128)S(1)} %bitcast.11), channel_id=1, source_target_pairs={{0,16},{16,32},{32,48},{1,17},{17,33},{33,49},{2,18},{18,34},{34,5... | collective-permute-start | bytes 320 | tf_op jit(solution)/shard_map/ppermute | solution.py:34
  55.3 22.6 %collective-permute-start.4 = (bf16[9,64,640]{2,1,0:T(8,128)(2,1)S(1)}, bf16[9,64,640]{2,1,0:T(8,128)(2,1)S(1)}, u32[]{:S(2)}, u32[]{:S(2)}) collective-permute-start(bf16[9,64,640]{2,1,0:T(8,128)(2,1)S(1)} %get-tuple-element.19), channel_id=1, source_target_pairs={{0,448},{64,0},{128,64},{192,128},{256,192},{320,256},{384,320},{4... | collective-permute-start | bytes 2211848 | tf_op jit(solution)/shard_map/ppermute | solution.py:34
  60.2 21.1 %collective-permute-start.5 = (bf16[9,64,640]{2,1,0:T(8,128)(2,1)S(1)}, bf16[9,64,640]{2,1,0:T(8,128)(2,1)S(1)}, u32[]{:S(2)}, u32[]{:S(2)}) collective-permute-start(bf16[9,64,640]{2,1,0:T(8,128)(2,1)S(1)} %get-tuple-element.20), channel_id=1, source_target_pairs={{0,64},{64,128},{128,192},{192,256},{256,320},{320,384},{384,448},... | collective-permute-start | bytes 2211848 | tf_op jit(solution)/shard_map/ppermute | solution.py:34
  62.8 24.7 %collective-permute-start.12 = (bf16[9,64,640]{2,1,0:T(8,128)(2,1)S(1)}, bf16[9,64,640]{2,1,0:T(8,128)(2,1)S(1)}, u32[]{:S(2)}, u32[]{:S(2)}) collective-permute-start(bf16[9,64,640]{2,1,0:T(8,128)(2,1)S(1)} %get-tuple-element.28), channel_id=1, source_target_pairs={{16,0},{32,16},{48,32},{17,1},{33,17},{49,33},{18,2},{34,18},{50,3... | collective-permute-start | bytes 2211848 | tf_op jit(solution)/shard_map/ppermute | solution.py:34
  65.1 36.1 %collective-permute-start.13 = (bf16[9,64,640]{2,1,0:T(8,128)(2,1)S(1)}, bf16[9,64,640]{2,1,0:T(8,128)(2,1)S(1)}, u32[]{:S(2)}, u32[]{:S(2)}) collective-permute-start(bf16[9,64,640]{2,1,0:T(8,128)(2,1)S(1)} %get-tuple-element.29), channel_id=1, source_target_pairs={{0,16},{16,32},{32,48},{1,17},{17,33},{33,49},{2,18},{18,34},{34,5... | collective-permute-start | bytes 2211848 | tf_op jit(solution)/shard_map/ppermute | solution.py:34
  70.2 36.4 %collective-permute-start.8 = (bf16[6,64,640]{2,1,0:T(8,128)(2,1)S(1)}, bf16[6,64,640]{2,1,0:T(8,128)(2,1)S(1)}, u32[]{:S(2)}, u32[]{:S(2)}) collective-permute-start(bf16[6,64,640]{2,1,0:T(8,128)(2,1)S(1)} %get-tuple-element.24), channel_id=1, source_target_pairs={{1,0},{2,1},{3,2},{4,3},{5,4},{6,5},{7,6},{8,7},{9,8},{10,9},{11,1... | collective-permute-start | bytes 1474568 | tf_op jit(solution)/shard_map/ppermute | solution.py:34
  77.9 32.2 %collective-permute-start.9 = (bf16[6,64,640]{2,1,0:T(8,128)(2,1)S(1)}, bf16[6,64,640]{2,1,0:T(8,128)(2,1)S(1)}, u32[]{:S(2)}, u32[]{:S(2)}) collective-permute-start(bf16[6,64,640]{2,1,0:T(8,128)(2,1)S(1)} %get-tuple-element.25), channel_id=1, source_target_pairs={{0,1},{1,2},{2,3},{3,4},{4,5},{5,6},{6,7},{7,8},{8,9},{9,10},{10,1... | collective-permute-start | bytes 1474568 | tf_op jit(solution)/shard_map/ppermute | solution.py:34
  81.4 29.6 %collective-permute-start.10 = (bf16[6,64,640]{2,1,0:T(8,128)(2,1)S(1)}, bf16[6,64,640]{2,1,0:T(8,128)(2,1)S(1)}, u32[]{:S(2)}, u32[]{:S(2)}) collective-permute-start(bf16[6,64,640]{2,1,0:T(8,128)(2,1)S(1)} %get-tuple-element.26), channel_id=1, source_target_pairs={{1,0},{2,1},{3,2},{4,3},{5,4},{6,5},{7,6},{8,7},{9,8},{10,9},{11,1... | collective-permute-start | bytes 1474568 | tf_op jit(solution)/shard_map/ppermute | solution.py:34
  87.5 27.9 %collective-permute-start.11 = (bf16[6,64,640]{2,1,0:T(8,128)(2,1)S(1)}, bf16[6,64,640]{2,1,0:T(8,128)(2,1)S(1)}, u32[]{:S(2)}, u32[]{:S(2)}) collective-permute-start(bf16[6,64,640]{2,1,0:T(8,128)(2,1)S(1)} %get-tuple-element.27), channel_id=1, source_target_pairs={{0,1},{1,2},{2,3},{3,4},{4,5},{5,6},{6,7},{7,8},{8,9},{9,10},{10,1... | collective-permute-start | bytes 1474568 | tf_op jit(solution)/shard_map/ppermute | solution.py:34
  101.3 15.2 %collective-permute-start.14 = (bf16[6,64,640]{2,1,0:T(8,128)(2,1)S(1)}, bf16[6,64,640]{2,1,0:T(8,128)(2,1)S(1)}, u32[]{:S(2)}, u32[]{:S(2)}) collective-permute-start(bf16[6,64,640]{2,1,0:T(8,128)(2,1)S(1)} %get-tuple-element.30), channel_id=1, source_target_pairs={{1,0},{2,1},{3,2},{4,3},{5,4},{6,5},{7,6},{8,7},{9,8},{10,9},{11,1... | collective-permute-start | bytes 1474568 | tf_op jit(solution)/shard_map/ppermute | solution.py:34
  106.6 14.1 %collective-permute-start.15 = (bf16[6,64,640]{2,1,0:T(8,128)(2,1)S(1)}, bf16[6,64,640]{2,1,0:T(8,128)(2,1)S(1)}, u32[]{:S(2)}, u32[]{:S(2)}) collective-permute-start(bf16[6,64,640]{2,1,0:T(8,128)(2,1)S(1)} %get-tuple-element.31), channel_id=1, source_target_pairs={{0,1},{1,2},{2,3},{3,4},{4,5},{5,6},{6,7},{7,8},{8,9},{9,10},{10,1... | collective-permute-start | bytes 1474568 | tf_op jit(solution)/shard_map/ppermute | solution.py:34
  115.4 5.3 %copy-start = (bf16[1,1,1,1024,1024]{4,3,2,1,0:T(8,128)(2,1)S(1)}, bf16[1,1,1,1024,1024]{4,3,2,1,0:T(8,128)(2,1)}, u32[]{:S(2)}) copy-start(bf16[1,1,1,1024,1024]{4,3,2,1,0:T(8,128)(2,1)} %param.3) | copy-start | bytes 6291460
